TPU v7x, 32 devices: a whole 2x2x4 slice. The times are simulated.
32 devices in a mesh: fsdp: 4 (over x, core), ctx: 8 (over z, y).
Axes of the slice: x: 2, y: 2, z: 4, core: 2. Of those that a mesh axis runs over, the one named last changes fastest.
Arguments:
- inputs: bfloat16 [4096, 1536], P(('fsdp', 'ctx')), may hold values from -6 to 6
- positions: int32 [4096], P(('fsdp', 'ctx')), may hold values from 0 to 1023, as said below
- cotangent: bfloat16 [4096, 1536], P(('fsdp', 'ctx')), may hold values from -6 to 6
- attention_gain: bfloat16 [1536], replicated, may hold values from 0.5 to 1.5
- query_weight: bfloat16 [1536, 1536], P('fsdp'), may hold values from -0.15625 to 0.15625
- key_weight: bfloat16 [768, 1536], P('fsdp'), may hold values from -0.15625 to 0.15625
- value_weight: bfloat16 [768, 1536], P('fsdp'), may hold values from -0.15625 to 0.15625
- output_weight: bfloat16 [1536, 1536], P('fsdp'), may hold values from -3 to 3
- feedforward_gain: bfloat16 [1536], replicated, may hold values from 0.5 to 1.5
- gate_weight: bfloat16 [4096, 1536], P('fsdp'), may hold values from -0.15625 to 0.15625
- up_weight: bfloat16 [4096, 1536], P('fsdp'), may hold values from -0.15625 to 0.15625
- down_weight: bfloat16 [4096, 1536], P('fsdp'), may hold values from -0.09375 to 0.09375
Outputs:
- layer_output: bfloat16 [4096, 1536], P(('fsdp', 'ctx'))
- input_grad: float32 [4096, 1536], P(('fsdp', 'ctx'))
- attention_gain_grad: float32 [1536], replicated
- query_weight_grad: float32 [1536, 1536], P('fsdp')
- key_weight_grad: float32 [768, 1536], P('fsdp')
- value_weight_grad: float32 [768, 1536], P('fsdp')
- output_weight_grad: float32 [1536, 1536], P('fsdp')
- feedforward_gain_grad: float32 [1536], replicated
- gate_weight_grad: float32 [4096, 1536], P('fsdp')
- up_weight_grad: float32 [4096, 1536], P('fsdp')
- down_weight_grad: float32 [4096, 1536], P('fsdp')
Inputs may be any that keep to these rules, and one draw needn't show every extreme that they name: Within each sequence every position appears once, and each device's 2 * 64 tokens of a sequence are two whole blocks of 64 consecutive rising positions, starting at b * 64 and at (15 - b) * 64 for some b, in either order.
All inputs are finite; a program needn't handle non-finite values.
Results may differ from a plain program's by a relative error of at most 0.022.
Values may be sent and summed in bfloat16 or wider, within the bound.
A program may use at most 384 MiB of HBM per device.

v0:
```python
import math

import jax
import jax.numpy as jnp
from jax import lax
from jax.sharding import PartitionSpec as P

HEADS = 16
KV_HEADS = 8
HEAD_DIM = 96


EPSILON = 1e-05
ROPE_BASE = 100000.0


def product(left, right):
    return jnp.dot(left, right, preferred_element_type=jnp.float32)


def product_back(left, right):
    return lax.dot_general(
        left, right, (((1,), (1,)), ((), ())), preferred_element_type=jnp.float32
    )


def product_rows(left, right):
    return lax.dot_general(
        left, right, (((0,), (0,)), ((), ())), preferred_element_type=jnp.float32
    )


def rms_scale(values):
    return lax.rsqrt(jnp.mean(values * values, axis=-1, keepdims=True) + EPSILON)


def norm_back(scale_rows, unit_rows, grad_unit):
    return scale_rows * (
        grad_unit - unit_rows * jnp.mean(grad_unit * unit_rows, axis=-1, keepdims=True)
    )


def rotary_tables(places):
    half_width = HEAD_DIM // 2
    frequencies = ROPE_BASE ** (-(jnp.arange(half_width, dtype=jnp.float32) * 2.0 / HEAD_DIM))
    angles = places.astype(jnp.float32)[:, None] * frequencies[None, :]
    return (jnp.cos(angles)[:, None, :], jnp.sin(angles)[:, None, :])


def rotate(values, cosine, sine):
    half_width = values.shape[-1] // 2
    lower_half = values[..., :half_width]
    upper_half = values[..., half_width:]
    return jnp.concatenate(
        [lower_half * cosine - upper_half * sine, upper_half * cosine + lower_half * sine], axis=-1
    )


def rotate_back(grads, cosine, sine):
    half_width = grads.shape[-1] // 2
    lower_half = grads[..., :half_width]
    upper_half = grads[..., half_width:]
    return jnp.concatenate(
        [lower_half * cosine + upper_half * sine, upper_half * cosine - lower_half * sine], axis=-1
    )


def block_total_of(total_keys):
    return max(1, total_keys // 512)


def masked_scores(query_grouped, query_places, key_rows, key_places, start, width):
    key_part = lax.dynamic_slice_in_dim(key_rows, start, width, 1)
    place_part = lax.dynamic_slice_in_dim(key_places, start, width, 1)
    scores = jnp.einsum(
        "sqhgd,skhd->shgqk", query_grouped, key_part, preferred_element_type=jnp.float32
    )
    scores = scores * (1.0 / math.sqrt(HEAD_DIM))
    allowed = place_part[:, None, None, None, :] <= query_places[:, None, None, :, None]
    return jnp.where(allowed, scores, -1000000000.0)


def attend_forward(query_grouped, query_places, key_rows, value_rows, key_places):
    seq_count, row_count, head_groups, group_size = query_grouped.shape[:4]
    total_keys = key_rows.shape[1]
    block_total = block_total_of(total_keys)
    width = total_keys // block_total
    stat_shape = (seq_count, head_groups, group_size, row_count)

    def peak_step(index, carry):
        running_top, running_sum = carry
        scores = masked_scores(
            query_grouped, query_places, key_rows, key_places, index * width, width
        )
        new_top = jnp.maximum(running_top, jnp.max(scores, axis=-1))
        running_sum = running_sum * jnp.exp(running_top - new_top) + jnp.sum(
            jnp.exp(scores - new_top[..., None]), axis=-1
        )
        return (new_top, running_sum)

    running_top, running_sum = lax.fori_loop(
        0,
        block_total,
        peak_step,
        (jnp.full(stat_shape, -1e30, jnp.float32), jnp.zeros(stat_shape, jnp.float32)),
    )
    log_total = running_top + jnp.log(running_sum)

    def value_step(index, gathered):
        scores = masked_scores(
            query_grouped, query_places, key_rows, key_places, index * width, width
        )
        soft_low = jnp.exp(scores - log_total[..., None]).astype(jnp.bfloat16)
        value_part = lax.dynamic_slice_in_dim(value_rows, index * width, width, 1)
        return gathered + jnp.einsum(
            "shgqk,skhd->sqhgd", soft_low, value_part, preferred_element_type=jnp.float32
        )

    attended = lax.fori_loop(
        0, block_total, value_step, jnp.zeros(query_grouped.shape, jnp.float32)
    )
    return (attended, log_total)


def attend_backward(
    query_grouped, query_places, key_rows, value_rows, key_places, log_total, grad_attended
):
    total_keys = key_rows.shape[1]
    block_total = block_total_of(total_keys)
    width = total_keys // block_total
    score_scale = 1.0 / math.sqrt(HEAD_DIM)

    def soft_and_grad(index):
        scores = masked_scores(
            query_grouped, query_places, key_rows, key_places, index * width, width
        )
        soft_values = jnp.exp(scores - log_total[..., None])
        value_part = lax.dynamic_slice_in_dim(value_rows, index * width, width, 1)
        grad_soft = jnp.einsum(
            "sqhgd,skhd->shgqk", grad_attended, value_part, preferred_element_type=jnp.float32
        )
        return (soft_values, grad_soft)

    def delta_step(index, row_delta):
        soft_values, grad_soft = soft_and_grad(index)
        return row_delta + jnp.sum(soft_values * grad_soft, axis=-1)

    row_delta = lax.fori_loop(0, block_total, delta_step, jnp.zeros(log_total.shape, jnp.float32))

    def grad_step(index, carry):
        grad_query, grad_keys, grad_values = carry
        soft_values, grad_soft = soft_and_grad(index)
        grad_scores = (soft_values * (grad_soft - row_delta[..., None])).astype(jnp.bfloat16)
        key_part = lax.dynamic_slice_in_dim(key_rows, index * width, width, 1)
        grad_query = (
            grad_query
            + jnp.einsum(
                "shgqk,skhd->sqhgd", grad_scores, key_part, preferred_element_type=jnp.float32
            )
            * score_scale
        )
        key_term = (
            jnp.einsum(
                "shgqk,sqhgd->skhd", grad_scores, query_grouped, preferred_element_type=jnp.float32
            )
            * score_scale
        )
        value_term = jnp.einsum(
            "shgqk,sqhgd->skhd",
            soft_values.astype(jnp.bfloat16),
            grad_attended,
            preferred_element_type=jnp.float32,
        )
        grad_keys = lax.dynamic_update_slice_in_dim(grad_keys, key_term, index * width, 1)
        grad_values = lax.dynamic_update_slice_in_dim(grad_values, value_term, index * width, 1)
        return (grad_query, grad_keys, grad_values)

    initial = (
        jnp.zeros(query_grouped.shape, jnp.float32),
        jnp.zeros(key_rows.shape, jnp.float32),
        jnp.zeros(value_rows.shape, jnp.float32),
    )
    return lax.fori_loop(0, block_total, grad_step, initial)


def per_device(
    inputs,
    positions,
    cotangent,
    attention_gain,
    query_weight,
    key_weight,
    value_weight,
    output_weight,
    feedforward_gain,
    gate_weight,
    up_weight,
    down_weight,
):
    row_count = inputs.shape[0]
    groups = HEADS // KV_HEADS
    gain_one = attention_gain.astype(jnp.float32)
    gain_two = feedforward_gain.astype(jnp.float32)
    seq_count = 1

    def attention_set():
        return (
            lax.all_gather(query_weight, "fsdp", axis=0, tiled=True),
            lax.all_gather(key_weight, "fsdp", axis=0, tiled=True),
            lax.all_gather(value_weight, "fsdp", axis=0, tiled=True),
            lax.all_gather(output_weight, "fsdp", axis=0, tiled=True),
        )

    def feedforward_set():
        return (
            lax.all_gather(gate_weight, "fsdp", axis=0, tiled=True),
            lax.all_gather(up_weight, "fsdp", axis=0, tiled=True),
            lax.all_gather(down_weight, "fsdp", axis=0, tiled=True),
        )

    query_places = positions.reshape(1, row_count)
    key_places = lax.all_gather(positions, "ctx", axis=0, tiled=True).reshape(1, -1)
    flat_in = inputs.astype(jnp.float32)
    scale_one = rms_scale(flat_in)
    unit_one = flat_in * scale_one
    normed_one = (unit_one * gain_one).astype(jnp.bfloat16)
    total_rows = normed_one.shape[0]
    cosine, sine = rotary_tables(query_places.reshape(-1))
    fwd_query, fwd_key, fwd_value, fwd_output = attention_set()
    query_heads = fwd_query.shape[0] // HEAD_DIM
    kv_heads = fwd_key.shape[0] // HEAD_DIM
    kv_width = kv_heads * HEAD_DIM
    query_low = rotate(
        product_back(normed_one, fwd_query).reshape(total_rows, query_heads, HEAD_DIM), cosine, sine
    ).astype(jnp.bfloat16)
    key_low = rotate(
        product_back(normed_one, fwd_key).reshape(total_rows, kv_heads, HEAD_DIM), cosine, sine
    ).astype(jnp.bfloat16)
    value_low = product_back(normed_one, fwd_value).astype(jnp.bfloat16)
    all_keys, all_values = (
        lax.all_gather(key_low.reshape(seq_count, row_count, kv_width), "ctx", axis=1, tiled=True),
        lax.all_gather(
            value_low.reshape(seq_count, row_count, kv_width), "ctx", axis=1, tiled=True
        ),
    )
    total_keys = all_keys.shape[1]
    key_grid = all_keys.reshape(seq_count, total_keys, kv_heads, HEAD_DIM)
    value_grid = all_values.reshape(seq_count, total_keys, kv_heads, HEAD_DIM)
    query_grouped = query_low.reshape(seq_count, row_count, kv_heads, groups, HEAD_DIM)
    attended, log_total = attend_forward(
        query_grouped, query_places, key_grid, value_grid, key_places
    )
    attended_low = attended.reshape(total_rows, query_heads * HEAD_DIM).astype(jnp.bfloat16)
    hidden_state = flat_in + product(attended_low, fwd_output)
    scale_two = rms_scale(hidden_state)
    unit_two = hidden_state * scale_two
    normed_two = (unit_two * gain_two).astype(jnp.bfloat16)
    fwd_gate, fwd_up, fwd_down = feedforward_set()
    gate_values = product_back(normed_two, fwd_gate)
    upward = product_back(normed_two, fwd_up)
    sigmoid_gate = jax.nn.sigmoid(gate_values)
    activated = gate_values * sigmoid_gate
    mixed_hidden = (activated * upward).astype(jnp.bfloat16)
    layer_output = (hidden_state + product(mixed_hidden, fwd_down)).astype(jnp.bfloat16)
    grad_out = cotangent.astype(jnp.float32)
    back_gate, back_up, back_down = feedforward_set()
    grad_down = product_rows(mixed_hidden, cotangent)
    grad_mixed = product_back(cotangent, back_down)
    grad_gate_low = (
        grad_mixed * upward * sigmoid_gate * (1.0 + gate_values * (1.0 - sigmoid_gate))
    ).astype(jnp.bfloat16)
    grad_up_low = (grad_mixed * activated).astype(jnp.bfloat16)
    grad_gate = product_rows(grad_gate_low, normed_two)
    grad_up = product_rows(grad_up_low, normed_two)
    feedforward_shards = (
        lax.psum_scatter(
            grad_gate.astype(jnp.bfloat16), "fsdp", scatter_dimension=0, tiled=True
        ).astype(jnp.float32),
        lax.psum_scatter(
            grad_up.astype(jnp.bfloat16), "fsdp", scatter_dimension=0, tiled=True
        ).astype(jnp.float32),
        lax.psum_scatter(
            grad_down.astype(jnp.bfloat16), "fsdp", scatter_dimension=0, tiled=True
        ).astype(jnp.float32),
    )
    grad_normed_two = product(grad_gate_low, back_gate) + product(grad_up_low, back_up)
    gain_two_grad = jnp.sum(grad_normed_two * unit_two, axis=0)
    grad_hidden = grad_out + norm_back(scale_two, unit_two, grad_normed_two * gain_two)
    branch_rows = grad_hidden.astype(jnp.bfloat16)
    back_query, back_key, back_value, back_output = attention_set()
    grad_output = product_rows(attended_low, branch_rows)
    grad_attended = product_back(branch_rows, back_output).astype(jnp.bfloat16)
    grad_attended = grad_attended.reshape(seq_count, row_count, kv_heads, groups, HEAD_DIM)
    grad_query_rot, grad_key_all, grad_value_all = attend_backward(
        query_grouped, query_places, key_grid, value_grid, key_places, log_total, grad_attended
    )
    key_grad_own, value_grad_own = (
        lax.psum_scatter(
            grad_key_all.reshape(seq_count, total_keys, kv_width).astype(jnp.bfloat16),
            "ctx",
            scatter_dimension=1,
            tiled=True,
        ).astype(jnp.float32),
        lax.psum_scatter(
            grad_value_all.reshape(seq_count, total_keys, kv_width).astype(jnp.bfloat16),
            "ctx",
            scatter_dimension=1,
            tiled=True,
        ).astype(jnp.float32),
    )
    grad_query_low = (
        rotate_back(grad_query_rot.reshape(total_rows, query_heads, HEAD_DIM), cosine, sine)
        .reshape(total_rows, query_heads * HEAD_DIM)
        .astype(jnp.bfloat16)
    )
    grad_key_low = (
        rotate_back(key_grad_own.reshape(total_rows, kv_heads, HEAD_DIM), cosine, sine)
        .reshape(total_rows, kv_width)
        .astype(jnp.bfloat16)
    )
    grad_value_low = value_grad_own.reshape(total_rows, kv_width).astype(jnp.bfloat16)
    grad_query = product_rows(grad_query_low, normed_one)
    grad_key = product_rows(grad_key_low, normed_one)
    grad_value = product_rows(grad_value_low, normed_one)
    attention_shards = (
        lax.psum_scatter(
            grad_query.astype(jnp.bfloat16), "fsdp", scatter_dimension=0, tiled=True
        ).astype(jnp.float32),
        lax.psum_scatter(
            grad_key.astype(jnp.bfloat16), "fsdp", scatter_dimension=0, tiled=True
        ).astype(jnp.float32),
        lax.psum_scatter(
            grad_value.astype(jnp.bfloat16), "fsdp", scatter_dimension=0, tiled=True
        ).astype(jnp.float32),
        lax.psum_scatter(
            grad_output.astype(jnp.bfloat16), "fsdp", scatter_dimension=0, tiled=True
        ).astype(jnp.float32),
    )
    grad_normed_one = (
        product(grad_query_low, back_query)
        + product(grad_key_low, back_key)
        + product(grad_value_low, back_value)
    )
    gain_one_grad = jnp.sum(grad_normed_one * unit_one, axis=0)
    input_grad = grad_hidden + norm_back(scale_one, unit_one, grad_normed_one * gain_one)
    summed = (
        lax.psum(attention_shards[0].astype(jnp.bfloat16), "ctx").astype(jnp.float32),
        lax.psum(attention_shards[1].astype(jnp.bfloat16), "ctx").astype(jnp.float32),
        lax.psum(attention_shards[2].astype(jnp.bfloat16), "ctx").astype(jnp.float32),
        lax.psum(attention_shards[3].astype(jnp.bfloat16), "ctx").astype(jnp.float32),
        lax.psum(feedforward_shards[0].astype(jnp.bfloat16), "ctx").astype(jnp.float32),
        lax.psum(feedforward_shards[1].astype(jnp.bfloat16), "ctx").astype(jnp.float32),
        lax.psum(feedforward_shards[2].astype(jnp.bfloat16), "ctx").astype(jnp.float32),
    )
    gain_sums = lax.psum((gain_one_grad, gain_two_grad), ("fsdp", "ctx"))
    return (
        layer_output,
        input_grad,
        gain_sums[0],
        summed[0],
        summed[1],
        summed[2],
        summed[3],
        gain_sums[1],
        summed[4],
        summed[5],
        summed[6],
    )


def solution(mesh):
    in_specs = (
        P(("fsdp", "ctx"), None),
        P(("fsdp", "ctx")),
        P(("fsdp", "ctx"), None),
        P(),
        P("fsdp", None),
        P("fsdp", None),
        P("fsdp", None),
        P("fsdp", None),
        P(),
        P("fsdp", None),
        P("fsdp", None),
        P("fsdp", None),
    )
    out_specs = (
        P(("fsdp", "ctx"), None),
        P(("fsdp", "ctx"), None),
        P(),
        P("fsdp", None),
        P("fsdp", None),
        P("fsdp", None),
        P("fsdp", None),
        P(),
        P("fsdp", None),
        P("fsdp", None),
        P("fsdp", None),
    )
    return jax.shard_map(
        per_device, mesh=mesh, in_specs=in_specs, out_specs=out_specs, check_vma=False
    )
```

profile of v0, /device:TPU:0, one launch (start us, length us, event | category | flops | bytes accessed | tf_op | source)
XLA Modules:
  0.0 1605.4 jit_solution(15687253532271398078)
XLA Ops:
  10.6 25.8 %all-gather.12.cloned.1.call-done = bf16[768,1536]{1,0:T(8,128)(2,1)} async-done(((bf16[192,1536]{1,0:T(8,128)(2,1)}), bf16[768,1536]{1,0:T(8,128)(2,1)}) %all-gather.12.cloned.1.call-update) | async-done | bytes 2359312 | tf_op jit(solution)/shard_map/all_gather | solution.py:210
  40.6 21.4 %all-gather.14.cloned.1.call-done = bf16[768,1536]{1,0:T(8,128)(2,1)} async-done(((bf16[192,1536]{1,0:T(8,128)(2,1)}), bf16[768,1536]{1,0:T(8,128)(2,1)}) %all-gather.14.cloned.1.call-update) | async-done | bytes 2359312 | tf_op jit(solution)/shard_map/all_gather | solution.py:209
  68.2 20.5 %all-gather.1 = s32[8,1,128]{2,1,0:T(1,128)S(1)} all-gather(s32[1,1,128]{2,1,0:T(1,128)S(1)} %bitcast.402), channel_id=1, replica_groups=mesh['fsdp'=4,'ctx'=8] {'ctx'}, dimensions={0}, use_global_device_ids=true | all-gather | bytes 4608 | tf_op jit(solution)/shard_map/all_gather | solution.py:222
  88.8 20.2 %all-gather.28.cloned.1.call-done = bf16[1024,768]{1,0:T(8,128)(2,1)} async-done(((bf16[128,768]{1,0:T(8,128)(2,1)}), bf16[1024,768]{1,0:T(8,128)(2,1)}) %all-gather.28.cloned.1.call-update) | async-done | bytes 1572880 | tf_op jit(solution)/shard_map/all_gather | solution.py:242
  110.7 35.5 %all-gather.18.cloned.1.call-done = bf16[1536,1536]{1,0:T(8,128)(2,1)} async-done(((bf16[384,1536]{1,0:T(8,128)(2,1)}), bf16[1536,1536]{1,0:T(8,128)(2,1)}) %all-gather.18.cloned.1.call-update) | async-done | bytes 4718608 | tf_op jit(solution)/shard_map/all_gather | solution.py:208
  150.2 43.0 %all-gather.16.cloned.1.call-done = bf16[1,1024,768]{1,2,0:T(8,128)(2,1)} async-done(((bf16[1,128,768]{1,2,0:T(8,128)(2,1)}), bf16[1,1024,768]{1,2,0:T(8,128)(2,1)}) %all-gather.16.cloned.1.call-update) | async-done | bytes 1572880 | tf_op jit(solution)/shard_map/all_gather | solution.py:241
  193.2 14.8 while.62
  208.0 7.9 while.63
  218.3 12.0 all-gather.20.cloned.1.call-done
  233.6 80.3 %all-gather.22.cloned.1.call-done = bf16[4096,1536]{1,0:T(8,128)(2,1)} async-done(((bf16[1024,1536]{1,0:T(8,128)(2,1)}), bf16[4096,1536]{1,0:T(8,128)(2,1)}) %all-gather.22.cloned.1.call-update) | async-done | bytes 12582928 | tf_op jit(solution)/shard_map/all_gather | solution.py:216
  313.9 10.0 fusion.111
  323.9 73.7 %all-gather.24.cloned.1.call-done = bf16[4096,1536]{1,0:T(8,128)(2,1)} async-done(((bf16[1024,1536]{1,0:T(8,128)(2,1)}), bf16[4096,1536]{1,0:T(8,128)(2,1)}) %all-gather.24.cloned.1.call-update) | async-done | bytes 12582928 | tf_op jit(solution)/shard_map/all_gather | solution.py:217
  397.5 9.9 fusion.112
  407.5 73.7 %all-gather.26.cloned.1.call-done = bf16[4096,1536]{1,0:T(8,128)(2,1)} async-done(((bf16[1024,1536]{1,0:T(8,128)(2,1)}), bf16[4096,1536]{1,0:T(8,128)(2,1)}) %all-gather.26.cloned.1.call-update) | async-done | bytes 12582928 | tf_op jit(solution)/shard_map/all_gather | solution.py:218
  481.2 11.2 multiply_convert_fusion
  492.4 7.2 fusion.113
  499.6 6.7 multiply_reduce_fusion
  508.8 7.3 while.64
  518.7 25.2 %while.65 = (s32[]{:T(128)}, f32[1,128,8,2,96]{1,4,3,2,0:T(8,128)}, bf16[1,1024,8,96]{1,3,2,0:T(8,128)(2,1)}, bf16[1,1024,8,96]{1,3,2,0:T(8,128)(2,1)}, bf16[1,1...) while((s32[]{:T(128)}, f32[1,128,8,2,96]{1,4,3,2,0:T(8,128)}, ...), condition=%wide.region_13.14_spmd.clone, body=%wide.region_12.13_spmd.clone.sunk | while | flops 1018167296 | bytes 70744944 | solution.py:183
  543.9 8.3 copy.69
  564.7 56.8 %reduce-scatter.28.cloned.1.call-done = bf16[128,768]{1,0:T(8,128)(2,1)} async-done(((bf16[1024,768]{1,0:T(8,128)(2,1)}), bf16[128,768]{1,0:T(8,128)(2,1)}) %reduce-scatter.28.cloned.1.call-update) | async-done | bytes 196624
  625.5 64.6 %reduce-scatter.30.cloned.1.call-done = bf16[128,768]{1,0:T(8,128)(2,1)} async-done(((bf16[1024,768]{1,0:T(8,128)(2,1)}), bf16[128,768]{1,0:T(8,128)(2,1)}) %reduce-scatter.30.cloned.1.call-update) | async-done | bytes 196624
  703.9 6.6 convolution_convert_fusion.2
  726.0 34.6 %reduce-scatter.18.cloned.1.call-done = bf16[192,1536]{1,0:T(8,128)(2,1)} async-done(((bf16[768,1536]{1,0:T(8,128)(2,1)}), bf16[192,1536]{1,0:T(8,128)(2,1)}) %reduce-scatter.18.cloned.1.call-update) | async-done | bytes 589840 | tf_op jit(solution)/shard_map/reduce_scatter | solution.py:332
  760.6 51.0 %reduce-scatter.14.cloned.1.call-done = bf16[384,1536]{1,0:T(8,128)(2,1)} async-done(((bf16[1536,1536]{1,0:T(8,128)(2,1)}), bf16[384,1536]{1,0:T(8,128)(2,1)}) %reduce-scatter.14.cloned.1.call-update) | async-done | bytes 1179664 | tf_op jit(solution)/shard_map/reduce_scatter | solution.py:326
  811.6 51.0 %reduce-scatter.20.cloned.1.call-done = bf16[384,1536]{1,0:T(8,128)(2,1)} async-done(((bf16[1536,1536]{1,0:T(8,128)(2,1)}), bf16[384,1536]{1,0:T(8,128)(2,1)}) %reduce-scatter.20.cloned.1.call-update) | async-done | bytes 1179664 | tf_op jit(solution)/shard_map/reduce_scatter | solution.py:335
  862.5 102.3 %reduce-scatter.22.cloned.1.call-done = bf16[1024,1536]{1,0:T(8,128)(2,1)} async-done(((bf16[4096,1536]{1,0:T(8,128)(2,1)}), bf16[1024,1536]{1,0:T(8,128)(2,1)}) %reduce-scatter.22.cloned.1.call-update) | async-done | bytes 3145744 | tf_op jit(solution)/shard_map/reduce_scatter | solution.py:276
  964.8 102.1 %reduce-scatter.24.cloned.1.call-done = bf16[1024,1536]{1,0:T(8,128)(2,1)} async-done(((bf16[4096,1536]{1,0:T(8,128)(2,1)}), bf16[1024,1536]{1,0:T(8,128)(2,1)}) %reduce-scatter.24.cloned.1.call-update) | async-done | bytes 3145744 | tf_op jit(solution)/shard_map/reduce_scatter | solution.py:279
  1066.9 102.1 %reduce-scatter.26.cloned.1.call-done = bf16[1024,1536]{1,0:T(8,128)(2,1)} async-done(((bf16[4096,1536]{1,0:T(8,128)(2,1)}), bf16[1024,1536]{1,0:T(8,128)(2,1)}) %reduce-scatter.26.cloned.1.call-update) | async-done | bytes 3145744 | tf_op jit(solution)/shard_map/reduce_scatter | solution.py:282
  1172.2 7.3 fusion.86
  1182.6 44.1 %all-reduce = (f32[1536]{0:T(1024)}, f32[1536]{0:T(1024)}) all-reduce(f32[1536]{0:T(1024)S(1)} %get-tuple-element.788, f32[1536]{0:T(1024)S(1)} %get-tuple-element.786), channel_id=1, replica_groups=mesh['fsdp'=4,'ctx'=8] {'fsdp','ctx'}, use_global_device_ids=true, to_apply=%region_18.19 | all-reduce | flops 3072 | bytes 24576 | tf_op jit(solution)/shard_map/psum | solution.py:355
  1227.9 352.3 %all-reduce.4.cloned.1.call-done = (bf16[384,1536]{1,0:T(8,128)(2,1)}, bf16[192,1536]{1,0:T(8,128)(2,1)}, bf16[192,1536]{1,0:T(8,128)(2,1)}, bf16[384,1536]{1,0:...) async-done(((bf16[384,1536]{1,0:T(8,128)(2,1)}, bf16[192,1536]{1,0:T(8,128)(2,1)}, bf16[192,1536]{1,0:T(8,128)(2,1)}, ...) | async-done | bytes 12976144 | tf_op jit(solution)/shard_map/psum | solution.py:347
  (231 shorter events, 156.2 us)
Async XLA Ops:
  7.2 54.8 %copy-start.2 = (bf16[128,1536]{1,0:T(8,128)(2,1)S(1)}, bf16[128,1536]{1,0:T(8,128)(2,1)}, u32[]{:S(2)}) copy-start(bf16[128,1536]{1,0:T(8,128)(2,1)} %param.20) | copy-start | bytes 1179652
  7.2 33.2 %copy-start.33 = (s32[128]{0:T(128)S(1)}, s32[128]{0:T(128)}, u32[]{:S(2)}) copy-start(s32[128]{0:T(128)} %param.21) | copy-start | bytes 1540
  7.2 29.2 %all-gather.12.cloned.1.call-start = ((), (), s32[]{:S(2)}) async-start(), calls=%async_computation.9 | async-start | bytes 2949120 | tf_op jit(solution)/shard_map/all_gather | solution.py:210
  7.9 54.1 %all-gather.14.cloned.1.call-start = ((), (), s32[]{:S(2)}) async-start(), calls=%async_computation.10 | async-start | bytes 2949120 | tf_op jit(solution)/shard_map/all_gather | solution.py:209
  8.7 100.3 %all-gather.28.cloned.1.call-start = ((), (), s32[]{:S(2)}) async-start(), calls=%async_computation.24 | async-start | bytes 1769472 | tf_op jit(solution)/shard_map/all_gather | solution.py:242
  39.8 106.5 %all-gather.18.cloned.1.call-start = ((), (), s32[]{:S(2)}) async-start(), calls=%async_computation.12 | async-start | bytes 5898240 | tf_op jit(solution)/shard_map/all_gather | solution.py:208
  40.4 152.8 %all-gather.16.cloned.1.call-start = ((), (), s32[]{:S(2)}) async-start(), calls=%async_computation.11 | async-start | bytes 1769472 | tf_op jit(solution)/shard_map/all_gather | solution.py:241
  65.3 164.9 %all-gather.20.cloned.1.call-start = ((), (), s32[]{:S(2)}) async-start(), calls=%async_computation.13 | async-start | bytes 5898240 | tf_op jit(solution)/shard_map/all_gather | solution.py:211
  65.9 248.0 %all-gather.22.cloned.1.call-start = ((), (), s32[]{:S(2)}) async-start(), calls=%async_computation.14 | async-start | bytes 15728640 | tf_op jit(solution)/shard_map/all_gather | solution.py:216
  66.6 330.9 %all-gather.24.cloned.1.call-start = ((), (), s32[]{:S(2)}) async-start(), calls=%async_computation.15 | async-start | bytes 15728640 | tf_op jit(solution)/shard_map/all_gather | solution.py:217
  67.4 413.8 %all-gather.26.cloned.1.call-start = ((), (), s32[]{:S(2)}) async-start(), calls=%async_computation.16 | async-start | bytes 15728640 | tf_op jit(solution)/shard_map/all_gather | solution.py:218
  68.1 553.3 %reduce-scatter.28.cloned.1.call-start = ((), (), s32[]{:S(2)}) async-start(), calls=%async_computation.25 | async-start | bytes 1769472
  218.2 105.6 %copy-start.16 = (bf16[1,128,8,2,96]{1,4,3,2,0:T(8,128)(2,1)}, bf16[1,128,8,2,96]{1,4,3,2,0:T(8,128)(2,1)S(1)}, u32[]{:S(2)}) copy-start(bf16[1,128,8,2,96]{1,4,3,2,0:T(8,128)(2,1)S(1)} %convert_element_type.192) | copy-start | bytes 1179652
  233.4 272.9 %copy-start.4 = (f32[128,1536]{1,0:T(8,128)}, f32[128,1536]{1,0:T(8,128)S(1)}, u32[]{:S(2)}) copy-start(f32[128,1536]{1,0:T(8,128)S(1)} %get-tuple-element.887) | copy-start | bytes 2359300
  492.4 7.2 copy-start.12
  492.4 7.2 copy-start.10
  492.4 14.2 slice-start
  499.6 6.7 copy-start.25
  499.6 7.0 slice-start.1
  555.7 134.4 %reduce-scatter.30.cloned.1.call-start = ((), (), s32[]{:S(2)}) async-start(), calls=%async_computation.26 | async-start | bytes 1769472
  564.6 161.3 %reduce-scatter.16.cloned.1.call-start = ((), (), s32[]{:S(2)}) async-start(), calls=%async_computation.18 | async-start | bytes 2949120 | tf_op jit(solution)/shard_map/reduce_scatter | solution.py:329
  625.4 68.6 %copy-start.3 = (f32[1,128,8,2,96]{1,4,3,2,0:T(8,128)S(1)}, f32[1,128,8,2,96]{1,4,3,2,0:T(8,128)}, u32[]{:S(2)}) copy-start(f32[1,128,8,2,96]{1,4,3,2,0:T(8,128)} %get-tuple-element.634) | copy-start | bytes 2359300
  625.4 135.2 %reduce-scatter.18.cloned.1.call-start = ((), (), s32[]{:S(2)}) async-start(), calls=%async_computation.19 | async-start | bytes 2949120 | tf_op jit(solution)/shard_map/reduce_scatter | solution.py:332
  693.9 117.7 %reduce-scatter.14.cloned.1.call-start = ((), (), s32[]{:S(2)}) async-start(), calls=%async_computation.17 | async-start | bytes 5898240 | tf_op jit(solution)/shard_map/reduce_scatter | solution.py:326
  697.8 164.7 %reduce-scatter.20.cloned.1.call-start = ((), (), s32[]{:S(2)}) async-start(), calls=%async_computation.20 | async-start | bytes 5898240 | tf_op jit(solution)/shard_map/reduce_scatter | solution.py:335
  702.7 262.1 %reduce-scatter.22.cloned.1.call-start = ((), (), s32[]{:S(2)}) async-start(), calls=%async_computation.21 | async-start | bytes 15728640 | tf_op jit(solution)/shard_map/reduce_scatter | solution.py:276
  710.5 356.4 %reduce-scatter.24.cloned.1.call-start = ((), (), s32[]{:S(2)}) async-start(), calls=%async_computation.22 | async-start | bytes 15728640 | tf_op jit(solution)/shard_map/reduce_scatter | solution.py:279
  718.2 450.8 %reduce-scatter.26.cloned.1.call-start = ((), (), s32[]{:S(2)}) async-start(), calls=%async_computation.23 | async-start | bytes 15728640 | tf_op jit(solution)/shard_map/reduce_scatter | solution.py:282
  725.9 854.3 %all-reduce.4.cloned.1.call-start = ((), (), s32[]{:S(2)}) async-start(), calls=%async_computation.27 | async-start | bytes 25952256 | tf_op jit(solution)/shard_map/psum | solution.py:347
  1172.2 7.3 copy-start.9
  1580.2 5.6 copy-start.19
  1589.4 5.3 copy-start.27
  (30 other events, 73.4 us)
Sparse Core Ops, SparseCore 0:
  9.6 26.7 all-gather.11
  37.9 24.0 all-gather.13
  64.8 44.1 all-gather.27
  110.4 35.7 all-gather.17
  148.7 44.4 all-gather.15
  194.6 35.5 all-gather.19
  231.8 82.0 all-gather.21
  315.4 82.0 all-gather.23
  399.1 82.0 all-gather.25
  555.8 65.6 reduce-scatter.27
  625.5 64.5 reduce-scatter.29
  693.0 31.5 reduce-scatter.15
  727.8 32.8 reduce-scatter.17
  763.6 47.9 reduce-scatter.13
  814.5 47.9 reduce-scatter.19
  865.0 99.7 reduce-scatter.21
  967.3 99.5 reduce-scatter.23
  1069.3 99.5 reduce-scatter.25
  1174.6 405.4 all-reduce.3
where the time goes:
time: 1610 us
  waiting for transfers between devices  1310 us (81%)
  matrix products  150 us (9%)
  blocking collectives  64.6 us (4%)
  local copies, waits for them, and re-layouts  35.9 us (2%)
  other arithmetic  32 us (2%)
    psum x1, waiting for transfers between devices, per_device(): lax.psum(attention_shards[0].astype(jnp.bfloat16), 'ctx')  352 us
    unnamed x21, waiting for transfers between devices  126 us
    reduce_scatter x1, waiting for transfers between devices, per_device(): lax.psum_scatter(grad_gate.astype(jnp.bfloat16), 'fsdp', scatter_dimensio...  102 us
    reduce_scatter x1, waiting for transfers between devices, per_device(): lax.psum_scatter(grad_down.astype(jnp.bfloat16), 'fsdp', scatter_dimensio...  102 us
    reduce_scatter x1, waiting for transfers between devices, per_device(): lax.psum_scatter(grad_up.astype(jnp.bfloat16), 'fsdp', scatter_dimension=...  102 us
    all_gather x1, waiting for transfers between devices, feedforward_set(): lax.all_gather(gate_weight, 'fsdp', axis=0, tiled=True)  80.3 us
    all_gather x1, waiting for transfers between devices, feedforward_set(): lax.all_gather(down_weight, 'fsdp', axis=0, tiled=True)  73.7 us
    all_gather x1, waiting for transfers between devices, feedforward_set(): lax.all_gather(up_weight, 'fsdp', axis=0, tiled=True)  73.7 us
  transfers between devices with their start and end apart: 19, of which 18 were waited for; matrix products, arithmetic and copies ran while one was open for 7% of the time, Pallas kernels for 0%

commit v1 on v0

v1 whole, which is shorter than its diff:
```python
import math

import jax
import jax.numpy as jnp
from jax import lax
from jax.sharding import PartitionSpec as P

HEADS = 16
KV_HEADS = 8
HEAD_DIM = 96


EPSILON = 1e-05
ROPE_BASE = 100000.0


def product(left, right):
    return jnp.dot(left, right, preferred_element_type=jnp.float32)


def product_back(left, right):
    return lax.dot_general(
        left, right, (((1,), (1,)), ((), ())), preferred_element_type=jnp.float32
    )


def product_rows(left, right):
    return lax.dot_general(
        left, right, (((0,), (0,)), ((), ())), preferred_element_type=jnp.float32
    )


def rms_scale(values):
    return lax.rsqrt(jnp.mean(values * values, axis=-1, keepdims=True) + EPSILON)


def norm_back(scale_rows, unit_rows, grad_unit):
    return scale_rows * (
        grad_unit - unit_rows * jnp.mean(grad_unit * unit_rows, axis=-1, keepdims=True)
    )


def rotary_tables(places):
    half_width = HEAD_DIM // 2
    frequencies = ROPE_BASE ** (-(jnp.arange(half_width, dtype=jnp.float32) * 2.0 / HEAD_DIM))
    angles = places.astype(jnp.float32)[:, None] * frequencies[None, :]
    return (jnp.cos(angles)[:, None, :], jnp.sin(angles)[:, None, :])


def rotate(values, cosine, sine):
    half_width = values.shape[-1] // 2
    lower_half = values[..., :half_width]
    upper_half = values[..., half_width:]
    return jnp.concatenate(
        [lower_half * cosine - upper_half * sine, upper_half * cosine + lower_half * sine], axis=-1
    )


def rotate_back(grads, cosine, sine):
    half_width = grads.shape[-1] // 2
    lower_half = grads[..., :half_width]
    upper_half = grads[..., half_width:]
    return jnp.concatenate(
        [lower_half * cosine + upper_half * sine, upper_half * cosine - lower_half * sine], axis=-1
    )


def block_total_of(total_keys):
    return max(1, total_keys // 512)


def masked_scores(query_grouped, query_places, key_rows, key_places, start, width):
    key_part = lax.dynamic_slice_in_dim(key_rows, start, width, 2)
    place_part = lax.dynamic_slice_in_dim(key_places, start, width, 1)
    scores = jnp.einsum(
        "sqhgd,shkd->shgqk", query_grouped, key_part, preferred_element_type=jnp.float32
    )
    scores = scores * (1.0 / math.sqrt(HEAD_DIM))
    allowed = place_part[:, None, None, None, :] <= query_places[:, None, None, :, None]
    return jnp.where(allowed, scores, -1000000000.0)


def attend_forward(query_grouped, query_places, key_rows, value_rows, key_places):
    seq_count, row_count, head_groups, group_size = query_grouped.shape[:4]
    total_keys = key_rows.shape[2]
    block_total = block_total_of(total_keys)
    width = total_keys // block_total
    stat_shape = (seq_count, head_groups, group_size, row_count)

    def peak_step(index, carry):
        running_top, running_sum = carry
        scores = masked_scores(
            query_grouped, query_places, key_rows, key_places, index * width, width
        )
        new_top = jnp.maximum(running_top, jnp.max(scores, axis=-1))
        running_sum = running_sum * jnp.exp(running_top - new_top) + jnp.sum(
            jnp.exp(scores - new_top[..., None]), axis=-1
        )
        return (new_top, running_sum)

    running_top, running_sum = lax.fori_loop(
        0,
        block_total,
        peak_step,
        (jnp.full(stat_shape, -1e30, jnp.float32), jnp.zeros(stat_shape, jnp.float32)),
    )
    log_total = running_top + jnp.log(running_sum)

    def value_step(index, gathered):
        scores = masked_scores(
            query_grouped, query_places, key_rows, key_places, index * width, width
        )
        soft_low = jnp.exp(scores - log_total[..., None]).astype(jnp.bfloat16)
        value_part = lax.dynamic_slice_in_dim(value_rows, index * width, width, 2)
        return gathered + jnp.einsum(
            "shgqk,shkd->sqhgd", soft_low, value_part, preferred_element_type=jnp.float32
        )

    attended = lax.fori_loop(
        0, block_total, value_step, jnp.zeros(query_grouped.shape, jnp.float32)
    )
    return (attended, log_total)


def attend_backward(
    query_grouped, query_places, key_rows, value_rows, key_places, log_total, grad_attended
):
    total_keys = key_rows.shape[2]
    block_total = block_total_of(total_keys)
    width = total_keys // block_total
    score_scale = 1.0 / math.sqrt(HEAD_DIM)

    def soft_and_grad(index):
        scores = masked_scores(
            query_grouped, query_places, key_rows, key_places, index * width, width
        )
        soft_values = jnp.exp(scores - log_total[..., None])
        value_part = lax.dynamic_slice_in_dim(value_rows, index * width, width, 2)
        grad_soft = jnp.einsum(
            "sqhgd,shkd->shgqk", grad_attended, value_part, preferred_element_type=jnp.float32
        )
        return (soft_values, grad_soft)

    def delta_step(index, row_delta):
        soft_values, grad_soft = soft_and_grad(index)
        return row_delta + jnp.sum(soft_values * grad_soft, axis=-1)

    row_delta = lax.fori_loop(0, block_total, delta_step, jnp.zeros(log_total.shape, jnp.float32))

    def grad_step(index, carry):
        grad_query, grad_keys, grad_values = carry
        soft_values, grad_soft = soft_and_grad(index)
        grad_scores = (soft_values * (grad_soft - row_delta[..., None])).astype(jnp.bfloat16)
        key_part = lax.dynamic_slice_in_dim(key_rows, index * width, width, 2)
        grad_query = (
            grad_query
            + jnp.einsum(
                "shgqk,shkd->sqhgd", grad_scores, key_part, preferred_element_type=jnp.float32
            )
            * score_scale
        )
        key_term = (
            jnp.einsum(
                "shgqk,sqhgd->shkd", grad_scores, query_grouped, preferred_element_type=jnp.float32
            )
            * score_scale
        )
        value_term = jnp.einsum(
            "shgqk,sqhgd->shkd",
            soft_values.astype(jnp.bfloat16),
            grad_attended,
            preferred_element_type=jnp.float32,
        )
        grad_keys = lax.dynamic_update_slice_in_dim(grad_keys, key_term, index * width, 2)
        grad_values = lax.dynamic_update_slice_in_dim(grad_values, value_term, index * width, 2)
        return (grad_query, grad_keys, grad_values)

    initial = (
        jnp.zeros(query_grouped.shape, jnp.float32),
        jnp.zeros(key_rows.shape, jnp.float32),
        jnp.zeros(value_rows.shape, jnp.float32),
    )
    return lax.fori_loop(0, block_total, grad_step, initial)


def gather_rows(values):
    return lax.all_gather(values, "fsdp", axis=0, tiled=True)


def scatter_rows(values):
    return lax.psum_scatter(
        values.astype(jnp.bfloat16), "fsdp", scatter_dimension=0, tiled=True
    ).astype(jnp.float32)


def per_device(
    inputs,
    positions,
    cotangent,
    attention_gain,
    query_weight,
    key_weight,
    value_weight,
    output_weight,
    feedforward_gain,
    gate_weight,
    up_weight,
    down_weight,
):
    row_count = inputs.shape[0]
    groups = HEADS // KV_HEADS
    gain_one = attention_gain.astype(jnp.float32)
    gain_two = feedforward_gain.astype(jnp.float32)
    seq_count = lax.axis_size("fsdp")
    first_row = lax.axis_index("fsdp") * row_count

    def own(values):
        return lax.dynamic_slice_in_dim(values, first_row, row_count, 0)

    query_places = gather_rows(positions).reshape(seq_count, row_count)
    key_places = lax.all_gather(query_places, "ctx", axis=1, tiled=True)
    all_cotangent = gather_rows(cotangent)
    flat_in = gather_rows(inputs).astype(jnp.float32)
    scale_one = rms_scale(flat_in)
    unit_one = flat_in * scale_one
    normed_one = (unit_one * gain_one).astype(jnp.bfloat16)
    total_rows = normed_one.shape[0]
    cosine, sine = rotary_tables(query_places.reshape(-1))
    query_heads = query_weight.shape[0] // HEAD_DIM
    kv_heads = key_weight.shape[0] // HEAD_DIM
    kv_width = kv_heads * HEAD_DIM
    query_low = rotate(
        product_back(normed_one, query_weight).reshape(total_rows, query_heads, HEAD_DIM), cosine, sine
    ).astype(jnp.bfloat16)
    key_low = rotate(
        product_back(normed_one, key_weight).reshape(total_rows, kv_heads, HEAD_DIM), cosine, sine
    ).astype(jnp.bfloat16)
    value_low = product_back(normed_one, value_weight).astype(jnp.bfloat16)
    ctx_size = lax.axis_size("ctx")

    def spread(values):
        rows = lax.all_gather(values, "ctx", axis=0, tiled=True)
        rows = rows.reshape(ctx_size, seq_count, row_count, kv_width).swapaxes(0, 1)
        return rows.reshape(seq_count, ctx_size * row_count, kv_width)

    def collect(values):
        rows = values.astype(jnp.bfloat16).swapaxes(1, 2)
        rows = rows.reshape(seq_count, ctx_size, row_count, kv_width).swapaxes(0, 1)
        return lax.psum_scatter(
            rows.reshape(-1, kv_width), "ctx", scatter_dimension=0, tiled=True
        )

    all_keys = spread(key_low.reshape(total_rows, kv_width))
    all_values = spread(value_low)
    total_keys = all_keys.shape[1]
    key_grid = all_keys.reshape(seq_count, total_keys, kv_heads, HEAD_DIM).swapaxes(1, 2)
    value_grid = all_values.reshape(seq_count, total_keys, kv_heads, HEAD_DIM).swapaxes(1, 2)
    query_grouped = query_low.reshape(seq_count, row_count, kv_heads, groups, HEAD_DIM)
    attended, log_total = attend_forward(
        query_grouped, query_places, key_grid, value_grid, key_places
    )
    attended_low = attended.reshape(total_rows, query_heads * HEAD_DIM).astype(jnp.bfloat16)
    hidden_state = inputs.astype(jnp.float32) + scatter_rows(product(attended_low, output_weight))
    scale_two = rms_scale(hidden_state)
    unit_two = hidden_state * scale_two
    normed_two = gather_rows((unit_two * gain_two).astype(jnp.bfloat16))
    gate_values = product_back(normed_two, gate_weight)
    upward = product_back(normed_two, up_weight)
    sigmoid_gate = jax.nn.sigmoid(gate_values)
    activated = gate_values * sigmoid_gate
    mixed_hidden = (activated * upward).astype(jnp.bfloat16)
    grad_out = cotangent.astype(jnp.float32)
    grad_down = product_rows(mixed_hidden, all_cotangent)
    grad_mixed = product_back(all_cotangent, down_weight)
    grad_gate_low = (
        grad_mixed * upward * sigmoid_gate * (1.0 + gate_values * (1.0 - sigmoid_gate))
    ).astype(jnp.bfloat16)
    grad_up_low = (grad_mixed * activated).astype(jnp.bfloat16)
    grad_normed_two = scatter_rows(
        product(grad_gate_low, gate_weight) + product(grad_up_low, up_weight)
    )
    gain_two_grad = jnp.sum(grad_normed_two * unit_two, axis=0)
    grad_hidden = grad_out + norm_back(scale_two, unit_two, grad_normed_two * gain_two)
    branch_rows = gather_rows(grad_hidden.astype(jnp.bfloat16))
    layer_output = (hidden_state + scatter_rows(product(mixed_hidden, down_weight))).astype(
        jnp.bfloat16
    )
    grad_gate = product_rows(grad_gate_low, normed_two)
    grad_up = product_rows(grad_up_low, normed_two)
    grad_output = product_rows(attended_low, branch_rows)
    grad_attended = product_back(branch_rows, output_weight).astype(jnp.bfloat16)
    grad_attended = grad_attended.reshape(seq_count, row_count, kv_heads, groups, HEAD_DIM)
    grad_query_rot, grad_key_all, grad_value_all = attend_backward(
        query_grouped, query_places, key_grid, value_grid, key_places, log_total, grad_attended
    )
    grad_key_own = collect(grad_key_all).astype(jnp.float32)
    grad_value_low = collect(grad_value_all)
    grad_query_low = (
        rotate_back(grad_query_rot.reshape(total_rows, query_heads, HEAD_DIM), cosine, sine)
        .reshape(total_rows, query_heads * HEAD_DIM)
        .astype(jnp.bfloat16)
    )
    grad_key_low = (
        rotate_back(
            grad_key_own.reshape(total_rows, kv_heads, HEAD_DIM), cosine, sine
        )
        .reshape(total_rows, kv_width)
        .astype(jnp.bfloat16)
    )
    grad_query = product_rows(grad_query_low, normed_one)
    grad_key = product_rows(grad_key_low, normed_one)
    grad_value = product_rows(grad_value_low, normed_one)
    grad_normed_one = scatter_rows(
        product(grad_query_low, query_weight)
        + product(grad_key_low, key_weight)
        + product(grad_value_low, value_weight)
    )
    own_unit = own(unit_one)
    gain_one_grad = jnp.sum(grad_normed_one * own_unit, axis=0)
    input_grad = grad_hidden + norm_back(own(scale_one), own_unit, grad_normed_one * gain_one)

    def ctx_sum(grad):
        return lax.psum(grad.astype(jnp.bfloat16), "ctx").astype(jnp.float32)

    gain_sums = lax.psum(jnp.stack([gain_one_grad, gain_two_grad]), ("fsdp", "ctx"))
    return (
        layer_output,
        input_grad,
        gain_sums[0],
        ctx_sum(grad_query),
        ctx_sum(grad_key),
        ctx_sum(grad_value),
        ctx_sum(grad_output),
        gain_sums[1],
        ctx_sum(grad_gate),
        ctx_sum(grad_up),
        ctx_sum(grad_down),
    )


def solution(mesh):
    in_specs = (
        P(("fsdp", "ctx"), None),
        P(("fsdp", "ctx")),
        P(("fsdp", "ctx"), None),
        P(),
        P("fsdp", None),
        P("fsdp", None),
        P("fsdp", None),
        P("fsdp", None),
        P(),
        P("fsdp", None),
        P("fsdp", None),
        P("fsdp", None),
    )
    out_specs = (
        P(("fsdp", "ctx"), None),
        P(("fsdp", "ctx"), None),
        P(),
        P("fsdp", None),
        P("fsdp", None),
        P("fsdp", None),
        P("fsdp", None),
        P(),
        P("fsdp", None),
        P("fsdp", None),
        P("fsdp", None),
    )
    return jax.shard_map(
        per_device, mesh=mesh, in_specs=in_specs, out_specs=out_specs, check_vma=False
    )
```

time: 1610 us -> 996 us (0.62)
  waiting for transfers between devices: 1310 us -> 648 us
  other arithmetic: 32 us -> 66.2 us
  matrix products: 150 us -> 120 us
  local copies, waits for them, and re-layouts: 35.9 us -> 62.2 us
    all_gather x9 -> x6, waiting for transfers between devices: 385 us -> 91.6 us  [the longest x4 67 us: gather_rows(): return lax.all_gather(values, 'fsdp', axis=0, tiled=True)]
    reduce_scatter x7 -> x6, waiting for transfers between devices: 443 us -> 163 us  [the longest x2 110 us: collect(): lax.psum_scatter(rows.reshape(-1, kv_width), 'ctx', scatter_dimension=0,...]
    unnamed x21 -> x13, waiting for transfers between devices: 126 us -> 1.38 us
    psum x1, waiting for transfers between devices: 352 us -> 392 us  [ctx_sum(): return lax.psum(grad.astype(jnp.bfloat16), 'ctx').astype(jnp.float32)]
    reshape x0 -> x8, local copies, waits for them, and re-layouts: none -> 26.1 us  [the longest x2 7.68 us: collect(): rows.reshape(-1, kv_width)]
    unnamed x70 -> x84, local copies, waits for them, and re-layouts: 31.2 us -> 10.3 us
    dot_general x7, matrix products: 42.6 us -> 26.5 us  [product_back(): lax.dot_general(left, right, (((1,), (1,)), ((), ())), preferred_element_...]
    all_gather x1 -> x2, blocking collectives: 20.5 us -> 32.5 us  [the longest x1 26.4 us: per_device(): key_places = lax.all_gather(query_places, 'ctx', axis=1, tiled=True)]
  transfers between devices with their start and end apart: 19 -> 13, of which waited for: 18 -> 11; matrix products, arithmetic and copies ran while one was open for 7% -> 11% of each run, Pallas kernels for 0% -> 0%
where the time goes in v1:
time: 996 us; the launch traced here: 986 us
  waiting for transfers between devices  648 us (65%)
  matrix products  120 us (12%)
  blocking collectives  72.2 us (7%)
  other arithmetic  66.2 us (7%)
  local copies, waits for them, and re-layouts  62.2 us (6%)
  between operations  14.7 us (1%)
    psum x1, waiting for transfers between devices, ctx_sum(): return lax.psum(grad.astype(jnp.bfloat16), 'ctx').astype(jnp.float32)  392 us
    reduce_scatter x2, waiting for transfers between devices, collect(): lax.psum_scatter(rows.reshape(-1, kv_width), 'ctx', scatter_dimension=0,...  110 us
    all_gather x4, waiting for transfers between devices, gather_rows(): return lax.all_gather(values, 'fsdp', axis=0, tiled=True)  67 us
    reduce_scatter x4, waiting for transfers between devices, scatter_rows(): lax.psum_scatter(values.astype(jnp.bfloat16), 'fsdp', scatter_dimension=0...  53.2 us
    psum x1, blocking collectives, per_device(): lax.psum(jnp.stack([gain_one_grad, gain_two_grad]), ('fsdp', 'ctx'))  39.7 us
    dot_general x7, matrix products, product_back(): lax.dot_general(left, right, (((1,), (1,)), ((), ())), preferred_element_...  26.5 us
    all_gather x1, blocking collectives, per_device(): key_places = lax.all_gather(query_places, 'ctx', axis=1, tiled=True)  26.4 us
    all_gather x2, waiting for transfers between devices, spread(): rows = lax.all_gather(values, 'ctx', axis=0, tiled=True)  24.5 us
  transfers between devices with their start and end apart: 13, of which 11 were waited for; matrix products, arithmetic and copies ran while one was open for 11% of the time, Pallas kernels for 0%

profile of v1, /device:TPU:0, one launch (start us, length us, event | category | flops | bytes accessed | tf_op | source)
XLA Modules:
  0.0 985.7 jit_solution(4520594425977909812)
XLA Ops:
  8.8 6.2 all-gather
  15.5 16.5 %all-gather.8.cloned.1.call-done = bf16[512,1536]{1,0:T(8,128)(2,1)} async-done(((bf16[128,1536]{1,0:T(8,128)(2,1)}), bf16[512,1536]{1,0:T(8,128)(2,1)}) %all-gather.8.cloned.1.call-update) | async-done | bytes 1572880 | tf_op jit(solution)/shard_map/all_gather | solution.py:187
  36.9 26.4 %all_gather.27 = s32[4,1024]{1,0:T(4,128)S(1)} all-gather(s32[4,128]{1,0:T(4,128)S(1)} %bitcast.305), channel_id=1, replica_groups=mesh['fsdp'=4,'ctx'=8] {'ctx'}, dimensions={1}, use_global_device_ids=true | all-gather | bytes 18432 | tf_op jit(solution)/shard_map/all_gather | solution.py:221
  71.2 10.2 %all-gather.12.cloned.1.call-done = bf16[4096,192]{0,1:T(8,128)(2,1)} async-done(((bf16[512,192]{0,1:T(8,128)(2,1)}), bf16[4096,192]{0,1:T(8,128)(2,1)}) %all-gather.12.cloned.1.call-update) | async-done | bytes 1572880 | tf_op jit(solution)/shard_map/all_gather | solution.py:242
  81.4 3.8 reshape.215
  91.7 20.6 %while.62 = (s32[]{:T(128)}, f32[4,2,2,128]{3,2,1,0:T(2,128)}, f32[4,2,2,128]{3,2,1,0:T(2,128)}, s32[4,1024]{1,0:T(4,128)S(1)}, s32[512]{0:T(512)}, /*index=5*/b...) while((s32[]{:T(128)}, f32[4,2,2,128]{3,2,1,0:T(2,128)}, ...), condition=%wide.region_4.5_spmd.clone, body=%wide.region_1.4_spmd.clone.sunk | while | flops 208939008 | bytes 11634982 | solution.py:101
  92.8 4.7 fusion.162
  103.0 4.7 fusion.162
  112.3 14.3 %all-gather.10.cloned.1.call-done = bf16[4096,192]{0,1:T(8,128)(2,1)} async-done(((bf16[512,192]{0,1:T(8,128)(2,1)}), bf16[4096,192]{0,1:T(8,128)(2,1)}) %all-gather.10.cloned.1.call-update) | async-done | bytes 1572880 | tf_op jit(solution)/shard_map/all_gather | solution.py:242
  126.6 3.8 reshape.212
  138.2 11.5 %while.63 = (s32[]{:T(128)}, f32[4,128,2,2,96]{1,4,3,2,0:T(8,128)}, bf16[4,2,1024,96]{2,3,1,0:T(8,128)(2,1)}, s32[4,1024]{1,0:T(4,128)S(1)}, s32[512]{0:T(512)},...) while((s32[]{:T(128)}, f32[4,128,2,2,96]{1,4,3,2,0:T(8,128)}, ...), condition=%wide.region_6.7_spmd.clone, body=%wide.region_5.6_spmd.clone.sunk | while | flops 407502848 | bytes 4099768 | solution.py:119
  139.9 3.9 fusion.168
  145.5 4.1 fusion.168
  156.7 25.1 %reduce-scatter.7.cloned.1.call-done = bf16[128,1536]{1,0:T(8,128)(2,1)} async-done(((bf16[512,1536]{1,0:T(8,128)(2,1)}), bf16[128,1536]{1,0:T(8,128)(2,1)}) %reduce-scatter.7.cloned.1.call-update) | async-done | bytes 393232 | tf_op jit(solution)/shard_map/reduce_scatter | solution.py:191
  186.8 18.7 %all-gather.14.cloned.1.call-done = bf16[512,1536]{1,0:T(8,128)(2,1)} async-done(((bf16[128,1536]{1,0:T(8,128)(2,1)}), bf16[512,1536]{1,0:T(8,128)(2,1)}) %all-gather.14.cloned.1.call-update) | async-done | bytes 1572880 | tf_op jit(solution)/shard_map/all_gather | solution.py:187
  205.5 5.6 fusion.85
  214.3 12.3 %all-gather.16.cloned.1.call-done = bf16[512,1536]{1,0:T(8,128)(2,1)} async-done(((bf16[128,1536]{1,0:T(8,128)(2,1)}), bf16[512,1536]{1,0:T(8,128)(2,1)}) %all-gather.16.cloned.1.call-update) | async-done | bytes 1572880 | tf_op jit(solution)/shard_map/all_gather | solution.py:187
  226.6 6.3 multiply_convert_fusion.1
  238.6 28.1 %reduce-scatter.11.cloned.1.call-done = bf16[128,1536]{1,0:T(8,128)(2,1)} async-done(((bf16[512,1536]{1,0:T(8,128)(2,1)}), bf16[128,1536]{1,0:T(8,128)(2,1)}) %reduce-scatter.11.cloned.1.call-update) | async-done | bytes 393232 | tf_op jit(solution)/shard_map/reduce_scatter | solution.py:191
  272.1 19.5 %all-gather.18.cloned.1.call-done = bf16[512,1536]{1,0:T(8,128)(2,1)} async-done(((bf16[128,1536]{1,0:T(8,128)(2,1)}), bf16[512,1536]{1,0:T(8,128)(2,1)}) %all-gather.18.cloned.1.call-update) | async-done | bytes 1572880 | tf_op jit(solution)/shard_map/all_gather | solution.py:187
  299.2 11.5 %while.64 = (s32[]{:T(128)}, f32[4,2,2,128]{3,2,1,0:T(2,128)}, s32[4,1024]{1,0:T(4,128)S(1)}, s32[512]{0:T(512)}, bf16[4,2,1024,96]{2,3,1,0:T(8,128)(2,1)}, /*in...) while((s32[]{:T(128)}, f32[4,2,2,128]{3,2,1,0:T(2,128)}, ...), condition=%wide.region_14.0_spmd.clone, body=%wide.region_12.0_spmd.clone.sunk | while | flops 408160256 | bytes 19245368 | solution.py:148
  313.5 29.0 %while.65 = (s32[]{:T(128)}, f32[4,128,2,2,96]{1,4,3,2,0:T(8,128)}, bf16[4,2,1024,96]{2,3,1,0:T(8,128)(2,1)}, bf16[4,2,1024,96]{2,3,1,0:T(8,128)(2,1)}, bf16[4,2...) while((s32[]{:T(128)}, f32[4,128,2,2,96]{1,4,3,2,0:T(8,128)}, ...), condition=%wide.region_16.17_spmd.clone, body=%wide.region_15.16_spmd.clone.sunk | while | flops 1018363904 | bytes 86141536 | solution.py:183
  347.5 3.8 reshape.220
  356.7 3.8 reshape.224
  369.7 47.9 %reduce-scatter.13.cloned.1.call-done = bf16[512,192]{0,1:T(8,128)(2,1)} async-done(((bf16[4096,192]{0,1:T(8,128)(2,1)}), bf16[512,192]{0,1:T(8,128)(2,1)}) %reduce-scatter.13.cloned.1.call-update) | async-done | bytes 196624 | tf_op jit(solution)/shard_map/reduce_scatter | solution.py:249
  420.3 4.2 convolution_add_fusion.1
  424.5 62.0 %reduce-scatter.15.cloned.1.call-done = bf16[512,192]{0,1:T(8,128)(2,1)} async-done(((bf16[4096,192]{0,1:T(8,128)(2,1)}), bf16[512,192]{0,1:T(8,128)(2,1)}) %reduce-scatter.15.cloned.1.call-update) | async-done | bytes 196624 | tf_op jit(solution)/shard_map/reduce_scatter | solution.py:249
  486.5 3.9 fusion.63
  490.5 4.2 convolution_convert_fusion.3
  495.0 5.6 convolution_convert_fusion.2
  522.3 39.7 %psum.56 = f32[2,1536]{1,0:T(2,128)} all-reduce(f32[2,1536]{1,0:T(2,128)} %pad_maximum_fusion.4), channel_id=1, replica_groups=mesh['fsdp'=4,'ctx'=8] {'fsdp','ctx'}, use_global_device_ids=true, to_apply=%region_23.24 | all-reduce | flops 3072 | bytes 24576 | tf_op jit(solution)/shard_map/psum | solution.py:325
  567.7 392.1 %all-reduce.3.cloned.1.call-done = (bf16[384,1536]{1,0:T(8,128)(2,1)}, bf16[192,1536]{1,0:T(8,128)(2,1)}, bf16[192,1536]{1,0:T(8,128)(2,1)}, bf16[384,1536]{1,0:...) async-done(((bf16[384,1536]{1,0:T(8,128)(2,1)}, bf16[192,1536]{1,0:T(8,128)(2,1)}, bf16[192,1536]{1,0:T(8,128)(2,1)}, ...) | async-done | bytes 12976144 | tf_op jit(solution)/shard_map/psum | solution.py:323
  (310 shorter events, 189.0 us)
Async XLA Ops:
  7.2 219.4 %copy-start = (bf16[1024,1536]{1,0:T(8,128)(2,1)S(1)}, bf16[1024,1536]{1,0:T(8,128)(2,1)}, u32[]{:S(2)}) copy-start(bf16[1024,1536]{1,0:T(8,128)(2,1)} %param.31) | copy-start | bytes 9437188
  7.2 24.8 %all-gather.8.cloned.1.call-start = ((), (), s32[]{:S(2)}) async-start(), calls=%async_computation.6 | async-start | bytes 1966080 | tf_op jit(solution)/shard_map/all_gather | solution.py:187
  7.9 73.5 %all-gather.12.cloned.1.call-start = ((), (), s32[]{:S(2)}) async-start(), calls=%async_computation.8 | async-start | bytes 1769472 | tf_op jit(solution)/shard_map/all_gather | solution.py:242
  8.8 54.5 %copy-start.40 = (f32[1536]{0:T(1024)}, f32[1536]{0:T(1024)S(1)}, u32[]{:S(2)}) copy-start(f32[1536]{0:T(1024)S(1)} %convert_element_type.162) | copy-start | bytes 18436
  15.0 21.9 %copy-start.23 = (s32[4,1,128]{2,1,0:T(1,128)}, s32[4,1,128]{2,1,0:T(1,128)S(1)}, u32[]{:S(2)}) copy-start(s32[4,1,128]{2,1,0:T(1,128)S(1)} %all-gather) | copy-start | bytes 6148
  15.5 50.5 %copy-start.13 = (f32[512,48]{0,1:T(8,128)}, f32[512,48]{0,1:T(8,128)S(1)}, u32[]{:S(2)}) copy-start(f32[512,48]{0,1:T(8,128)S(1)} %get-tuple-element.994) | copy-start | bytes 294916
  15.5 50.5 %copy-start.15 = (f32[512,48]{0,1:T(8,128)}, f32[512,48]{0,1:T(8,128)S(1)}, u32[]{:S(2)}) copy-start(f32[512,48]{0,1:T(8,128)S(1)} %get-tuple-element.995) | copy-start | bytes 294916
  33.7 29.5 %copy-start.44 = (f32[512]{0:T(512)}, f32[512]{0:T(512)S(1)}, u32[]{:S(2)}) copy-start(f32[512]{0:T(512)S(1)} %add_rsqrt_fusion) | copy-start | bytes 6148
  36.8 89.8 %all-gather.10.cloned.1.call-start = ((), (), s32[]{:S(2)}) async-start(), calls=%async_computation.7 | async-start | bytes 1769472 | tf_op jit(solution)/shard_map/all_gather | solution.py:242
  71.2 110.6 %reduce-scatter.7.cloned.1.call-start = ((), (), s32[]{:S(2)}) async-start(), calls=%async_computation.9 | async-start | bytes 1966080 | tf_op jit(solution)/shard_map/reduce_scatter | solution.py:191
  92.8 4.7 copy-start.3
  103.0 4.7 copy-start.3
  155.4 50.1 %all-gather.14.cloned.1.call-start = ((), (), s32[]{:S(2)}) async-start(), calls=%async_computation.10 | async-start | bytes 1966080 | tf_op jit(solution)/shard_map/all_gather | solution.py:187
  185.7 40.9 %all-gather.16.cloned.1.call-start = ((), (), s32[]{:S(2)}) async-start(), calls=%async_computation.12 | async-start | bytes 1966080 | tf_op jit(solution)/shard_map/all_gather | solution.py:187
  186.3 80.4 %reduce-scatter.11.cloned.1.call-start = ((), (), s32[]{:S(2)}) async-start(), calls=%async_computation.13 | async-start | bytes 1966080 | tf_op jit(solution)/shard_map/reduce_scatter | solution.py:191
  205.5 5.7 copy-start.51
  205.5 5.7 copy-start.53
  226.6 6.3 copy-start.50
  238.6 53.1 %all-gather.18.cloned.1.call-start = ((), (), s32[]{:S(2)}) async-start(), calls=%async_computation.14 | async-start | bytes 1966080 | tf_op jit(solution)/shard_map/all_gather | solution.py:187
  271.9 145.7 %reduce-scatter.13.cloned.1.call-start = ((), (), s32[]{:S(2)}) async-start(), calls=%async_computation.15 | async-start | bytes 1769472 | tf_op jit(solution)/shard_map/reduce_scatter | solution.py:249
  318.8 6.8 copy-start.2
  333.2 6.9 copy-start.2
  351.4 135.1 %reduce-scatter.15.cloned.1.call-start = ((), (), s32[]{:S(2)}) async-start(), calls=%async_computation.16 | async-start | bytes 1769472 | tf_op jit(solution)/shard_map/reduce_scatter | solution.py:249
  360.5 5.0 copy-start.14
  360.5 5.0 copy-start.16
  360.5 158.4 %reduce-scatter.17.cloned.1.call-start = ((), (), s32[]{:S(2)}) async-start(), calls=%async_computation.17 | async-start | bytes 1966080 | tf_op jit(solution)/shard_map/reduce_scatter | solution.py:191
  490.4 74.1 %reduce-scatter.9.cloned.1.call-start = ((), (), s32[]{:S(2)}) async-start(), calls=%async_computation.11 | async-start | bytes 1966080 | tf_op jit(solution)/shard_map/reduce_scatter | solution.py:191
  494.6 465.2 %all-reduce.3.cloned.1.call-start = ((), (), s32[]{:S(2)}) async-start(), calls=%async_computation.18 | async-start | bytes 25952256 | tf_op jit(solution)/shard_map/psum | solution.py:323
  494.9 5.6 copy-start.54
  495.0 5.6 copy-start.58
  514.9 49.6 %copy-start.4 = (bf16[128,1536]{1,0:T(8,128)(2,1)S(1)}, bf16[128,1536]{1,0:T(8,128)(2,1)}, u32[]{:S(2)}) copy-start(bf16[128,1536]{1,0:T(8,128)(2,1)} %param.20) | copy-start | bytes 1179652
  514.9 49.6 %copy-start.37 = (f32[1536]{0:T(1024)S(1)}, f32[1536]{0:T(1024)}, u32[]{:S(2)}) copy-start(f32[1536]{0:T(1024)} %convert_element_type.171) | copy-start | bytes 18436
  (63 other events, 157.4 us)
Sparse Core Ops, SparseCore 0:
  9.6 22.3 all-gather.7
  37.0 44.4 all-gather.11
  84.1 42.5 all-gather.9
  155.5 26.2 reduce-scatter.6
  185.8 19.6 all-gather.13
  206.9 19.6 all-gather.15
  238.7 27.9 reduce-scatter.10
  272.0 19.6 all-gather.17
  351.5 66.0 reduce-scatter.12
  421.4 65.0 reduce-scatter.14
  490.5 26.8 reduce-scatter.16
  520.3 27.9 reduce-scatter.8
  555.2 404.5 all-reduce.2

commit v2 on v1

--- a/solution.py
+++ b/solution.py
@@ -1,8 +1,11 @@
+import functools
 import math
 
 import jax
 import jax.numpy as jnp
 from jax import lax
+from jax.experimental import pallas as pl
+from jax.experimental.pallas import tpu as pltpu
 from jax.sharding import PartitionSpec as P
 
 HEADS = 16
@@ -181,6 +184,156 @@
         jnp.zeros(value_rows.shape, jnp.float32),
     )
     return lax.fori_loop(0, block_total, grad_step, initial)
+
+
+def softmax_parts(query_rows, key_rows, first_row):
+    scores = product_back(query_rows, key_rows) * (1.0 / math.sqrt(HEAD_DIM))
+    rows = lax.broadcasted_iota(jnp.int32, scores.shape, 0) + first_row
+    columns = lax.broadcasted_iota(jnp.int32, scores.shape, 1)
+    scores = jnp.where(columns <= rows, scores, -1e30)
+    spread = jnp.exp(scores - jnp.max(scores, axis=-1, keepdims=True))
+    return spread * (1.0 / jnp.sum(spread, axis=-1, keepdims=True))
+
+
+def sort_blocks(place_ref, source_ref, targets, block):
+    block_total = source_ref.shape[0] // block
+    for slot in range(block_total):
+        place = place_ref[slot * block]
+        rows = source_ref[pl.ds(slot * block, block), :]
+        start = 0
+        for target in targets:
+            width = target.shape[-1]
+            target[pl.ds(pl.multiple_of(place, block), block), :] = rows[:, start : start + width]
+            start += width
+
+
+def attention_forward_kernel(block, place_ref, packed_ref, out_ref, q0, q1, k, v, result):
+    sort_blocks(place_ref, packed_ref, (q0, q1, k, v), block)
+    length = packed_ref.shape[0]
+    tile = min(256, length)
+    for first in range(0, length, tile):
+        parts = []
+        for q in (q0, q1):
+            soft = softmax_parts(q[first : first + tile, :], k[: first + tile, :], first)
+            parts.append(product(soft.astype(jnp.bfloat16), v[: first + tile, :]))
+        result[first : first + tile, :] = jnp.concatenate(parts, axis=-1)
+    for slot in range(length // block):
+        place = pl.multiple_of(place_ref[slot * block], block)
+        out_ref[pl.ds(slot * block, block), :] = result[pl.ds(place, block), :].astype(
+            jnp.bfloat16
+        )
+
+
+def attention_backward_kernel(
+    block, place_ref, packed_ref, grad_ref, out_ref, q0, q1, k, v, g0, g1, result, dk, dv
+):
+    sort_blocks(place_ref, packed_ref, (q0, q1, k, v), block)
+    sort_blocks(place_ref, grad_ref, (g0, g1), block)
+    length = packed_ref.shape[0]
+    tile = min(256, length)
+    scale = 1.0 / math.sqrt(HEAD_DIM)
+    dk[...] = jnp.zeros_like(dk)
+    dv[...] = jnp.zeros_like(dv)
+    for first in range(0, length, tile):
+        top = first + tile
+        parts = []
+        for q, g in ((q0, g0), (q1, g1)):
+            query_rows = q[first:top, :]
+            grad_rows = g[first:top, :]
+            soft = softmax_parts(query_rows, k[:top, :], first)
+            grad_soft = product_back(grad_rows, v[:top, :])
+            delta = jnp.sum(soft * grad_soft, axis=-1, keepdims=True)
+            grad_scores = (soft * (grad_soft - delta)).astype(jnp.bfloat16)
+            parts.append(product(grad_scores, k[:top, :]) * scale)
+            dk[:top, :] += product_rows(grad_scores, query_rows) * scale
+            dv[:top, :] += product_rows(soft.astype(jnp.bfloat16), grad_rows)
+        result[first:top, :] = jnp.concatenate(parts, axis=-1)
+    for slot in range(length // block):
+        place = pl.multiple_of(place_ref[slot * block], block)
+        span = pl.ds(place, block)
+        out_ref[pl.ds(slot * block, block), :] = jnp.concatenate(
+            [result[span, :], dk[span, :], dv[span, :]], axis=-1
+        ).astype(jnp.bfloat16)
+
+
+def vmem():
+    return pl.BlockSpec(memory_space=pltpu.VMEM)
+
+
+def attention_calls(length, block):
+    wide = 4 * HEAD_DIM
+    pair = 2 * HEAD_DIM
+    half = [pltpu.VMEM((length, HEAD_DIM), jnp.bfloat16)]
+    full = [pltpu.VMEM((length, HEAD_DIM), jnp.float32)]
+    params = pltpu.CompilerParams(vmem_limit_bytes=48 * 2**20)
+    places = pl.BlockSpec(memory_space=pltpu.SMEM)
+    forward = pl.pallas_call(
+        functools.partial(attention_forward_kernel, block),
+        out_shape=jax.ShapeDtypeStruct((length, pair), jnp.bfloat16),
+        in_specs=[places, vmem()],
+        out_specs=vmem(),
+        scratch_shapes=half * 4 + [pltpu.VMEM((length, pair), jnp.float32)],
+        compiler_params=params,
+        name="attention_forward",
+    )
+    backward = pl.pallas_call(
+        functools.partial(attention_backward_kernel, block),
+        out_shape=jax.ShapeDtypeStruct((length, wide), jnp.bfloat16),
+        in_specs=[places, vmem(), vmem()],
+        out_specs=vmem(),
+        scratch_shapes=half * 6 + [pltpu.VMEM((length, pair), jnp.float32)] + full * 2,
+        compiler_params=params,
+        name="attention_backward",
+    )
+    return forward, backward
+
+
+def peer(ctx_index):
+    return dict(device_id={"ctx": ctx_index}, device_id_type=pl.DeviceIdType.MESH)
+
+
+def exchange_kernel(count, in_ref, out_ref, send_sem, recv_sem, own_sem):
+    me = lax.axis_index("ctx")
+    barrier = pltpu.get_barrier_semaphore()
+    for step in range(1, count):
+        pl.semaphore_signal(barrier, inc=1, **peer(lax.rem(me + step, count)))
+    own = pltpu.make_async_copy(in_ref.at[me], out_ref.at[me], own_sem)
+    own.start()
+    pl.semaphore_wait(barrier, count - 1)
+    copies = []
+    for step in range(1, count):
+        other = lax.rem(me + step, count)
+        copies.append(
+            pltpu.make_async_remote_copy(
+                src_ref=in_ref.at[other],
+                dst_ref=out_ref.at[me],
+                send_sem=send_sem.at[step],
+                recv_sem=recv_sem.at[step],
+                **peer(other),
+            )
+        )
+    for copy in copies:
+        copy.start()
+    own.wait()
+    for copy in copies:
+        copy.wait()
+
+
+def exchange(values, key):
+    count = values.shape[0]
+    return pl.pallas_call(
+        functools.partial(exchange_kernel, count),
+        out_shape=jax.ShapeDtypeStruct(values.shape, values.dtype),
+        in_specs=[pl.BlockSpec(memory_space=pl.ANY)],
+        out_specs=pl.BlockSpec(memory_space=pl.ANY),
+        scratch_shapes=[
+            pltpu.SemaphoreType.DMA((count,)),
+            pltpu.SemaphoreType.DMA((count,)),
+            pltpu.SemaphoreType.DMA,
+        ],
+        compiler_params=pltpu.CompilerParams(collective_id=key, has_side_effects=True),
+        name=f"exchange_{key}",
+    )(values)
 
 
 def gather_rows(values):
@@ -237,29 +390,60 @@
     ).astype(jnp.bfloat16)
     value_low = product_back(normed_one, value_weight).astype(jnp.bfloat16)
     ctx_size = lax.axis_size("ctx")
-
-    def spread(values):
-        rows = lax.all_gather(values, "ctx", axis=0, tiled=True)
-        rows = rows.reshape(ctx_size, seq_count, row_count, kv_width).swapaxes(0, 1)
-        return rows.reshape(seq_count, ctx_size * row_count, kv_width)
-
-    def collect(values):
-        rows = values.astype(jnp.bfloat16).swapaxes(1, 2)
-        rows = rows.reshape(seq_count, ctx_size, row_count, kv_width).swapaxes(0, 1)
-        return lax.psum_scatter(
-            rows.reshape(-1, kv_width), "ctx", scatter_dimension=0, tiled=True
-        )
-
-    all_keys = spread(key_low.reshape(total_rows, kv_width))
-    all_values = spread(value_low)
-    total_keys = all_keys.shape[1]
-    key_grid = all_keys.reshape(seq_count, total_keys, kv_heads, HEAD_DIM).swapaxes(1, 2)
-    value_grid = all_values.reshape(seq_count, total_keys, kv_heads, HEAD_DIM).swapaxes(1, 2)
-    query_grouped = query_low.reshape(seq_count, row_count, kv_heads, groups, HEAD_DIM)
-    attended, log_total = attend_forward(
-        query_grouped, query_places, key_grid, value_grid, key_places
-    )
-    attended_low = attended.reshape(total_rows, query_heads * HEAD_DIM).astype(jnp.bfloat16)
+    by_head = ctx_size == seq_count * kv_heads
+
+    def to_heads(parts):
+        grouped = [
+            part.reshape(seq_count, row_count, kv_heads, -1).swapaxes(1, 2) for part in parts
+        ]
+        return jnp.concatenate(grouped, axis=-1).reshape(ctx_size, row_count, -1)
+
+    def from_heads(values, widths):
+        grouped = values.reshape(seq_count, kv_heads, row_count, -1).swapaxes(1, 2)
+        parts, start = [], 0
+        for width in widths:
+            parts.append(grouped[..., start : start + width].reshape(total_rows, kv_heads * width))
+            start += width
+        return parts
+
+    pair = groups * HEAD_DIM
+    flat_query = query_low.reshape(total_rows, query_heads * HEAD_DIM)
+    if by_head:
+        own_sequence = lax.axis_index("ctx") // kv_heads
+        head_places = lax.dynamic_index_in_dim(key_places, own_sequence, 0, keepdims=False)
+        length = head_places.shape[0]
+        block = row_count // 2
+        forward_call, backward_call = attention_calls(length, block)
+        packed = exchange(
+            to_heads([flat_query, key_low.reshape(total_rows, kv_width), value_low]), 1
+        ).reshape(length, -1)
+        attended_low = from_heads(
+            exchange(forward_call(head_places, packed).reshape(ctx_size, row_count, pair), 2),
+            (pair,),
+        )[0]
+    else:
+        def spread(values):
+            rows = lax.all_gather(values, "ctx", axis=0, tiled=True)
+            rows = rows.reshape(ctx_size, seq_count, row_count, kv_width).swapaxes(0, 1)
+            return rows.reshape(seq_count, ctx_size * row_count, kv_width)
+
+        def collect(values):
+            rows = values.astype(jnp.bfloat16).swapaxes(1, 2)
+            rows = rows.reshape(seq_count, ctx_size, row_count, kv_width).swapaxes(0, 1)
+            return lax.psum_scatter(
+                rows.reshape(-1, kv_width), "ctx", scatter_dimension=0, tiled=True
+            )
+
+        all_keys = spread(key_low.reshape(total_rows, kv_width))
+        all_values = spread(value_low)
+        total_keys = all_keys.shape[1]
+        key_grid = all_keys.reshape(seq_count, total_keys, kv_heads, HEAD_DIM).swapaxes(1, 2)
+        value_grid = all_values.reshape(seq_count, total_keys, kv_heads, HEAD_DIM).swapaxes(1, 2)
+        query_grouped = query_low.reshape(seq_count, row_count, kv_heads, groups, HEAD_DIM)
+        attended, log_total = attend_forward(
+            query_grouped, query_places, key_grid, value_grid, key_places
+        )
+        attended_low = attended.reshape(total_rows, query_heads * HEAD_DIM).astype(jnp.bfloat16)
     hidden_state = inputs.astype(jnp.float32) + scatter_rows(product(attended_low, output_weight))
     scale_two = rms_scale(hidden_state)
     unit_two = hidden_state * scale_two
@@ -289,12 +473,23 @@
     grad_up = product_rows(grad_up_low, normed_two)
     grad_output = product_rows(attended_low, branch_rows)
     grad_attended = product_back(branch_rows, output_weight).astype(jnp.bfloat16)
-    grad_attended = grad_attended.reshape(seq_count, row_count, kv_heads, groups, HEAD_DIM)
-    grad_query_rot, grad_key_all, grad_value_all = attend_backward(
-        query_grouped, query_places, key_grid, value_grid, key_places, log_total, grad_attended
-    )
-    grad_key_own = collect(grad_key_all).astype(jnp.float32)
-    grad_value_low = collect(grad_value_all)
+    if by_head:
+        grad_heads = exchange(to_heads([grad_attended]), 3).reshape(length, pair)
+        packed_grads = exchange(
+            backward_call(head_places, packed, grad_heads).reshape(ctx_size, row_count, -1), 4
+        )
+        grad_query_rot, grad_key_own, grad_value_low = from_heads(
+            packed_grads, (pair, HEAD_DIM, HEAD_DIM)
+        )
+        grad_query_rot = grad_query_rot.astype(jnp.float32)
+        grad_key_own = grad_key_own.astype(jnp.float32)
+    else:
+        grad_attended = grad_attended.reshape(seq_count, row_count, kv_heads, groups, HEAD_DIM)
+        grad_query_rot, grad_key_all, grad_value_all = attend_backward(
+            query_grouped, query_places, key_grid, value_grid, key_places, log_total, grad_attended
+        )
+        grad_key_own = collect(grad_key_all).astype(jnp.float32)
+        grad_value_low = collect(grad_value_all)
     grad_query_low = (
         rotate_back(grad_query_rot.reshape(total_rows, query_heads, HEAD_DIM), cosine, sine)
         .reshape(total_rows, query_heads * HEAD_DIM)

time: 996 us -> 825 us (0.83)
  waiting for transfers between devices: 648 us -> 515 us
  Pallas kernels: 0 us -> 75.6 us
  matrix products: 120 us -> 64.5 us
  local copies, waits for them, and re-layouts: 62.2 us -> 27.7 us
  other arithmetic: 66.2 us -> 44.9 us
    reduce_scatter x2 -> x0, waiting for transfers between devices: 110 us -> none  [collect(): lax.psum_scatter(rows.reshape(-1, kv_width), 'ctx', scatter_dimension=0,...]
    pallas_call x0 -> x6, Pallas kernels: none -> 75.6 us  [the longest x4 61.8 us: exchange(): pl.pallas_call(functools.partial(exchange_kernel, count), out_shape=jax.S...]
    dot_general x18 -> x0, matrix products: 51.2 us -> none  [the longest x6 17.5 us: masked_scores(): jnp.einsum('sqhgd,shkd->shgqk', query_grouped, key_part, preferred_elemen...]
    all_gather x2 -> x0, waiting for transfers between devices: 24.5 us -> none  [spread(): rows = lax.all_gather(values, 'ctx', axis=0, tiled=True)]
    reshape x8 -> x4, local copies, waits for them, and re-layouts: 26.1 us -> 6.78 us  [the longest x2 4.21 us: from_heads(): grouped = values.reshape(seq_count, kv_heads, row_count, -1).swapaxes(1, 2)]
    all_gather x4, waiting for transfers between devices: 67 us -> 50.9 us  [gather_rows(): return lax.all_gather(values, 'fsdp', axis=0, tiled=True)]
    reduce_scatter x4, waiting for transfers between devices: 53.2 us -> 65 us  [scatter_rows(): lax.psum_scatter(values.astype(jnp.bfloat16), 'fsdp', scatter_dimension=0...]
    another operation x5 -> x1, local copies, waits for them, and re-layouts: 10.7 us -> 0.08 us  [the longest x1 3.74 us: per_device(): all_keys.reshape(seq_count, total_keys, kv_heads, HEAD_DIM).swapaxes(1, 2)]
  transfers between devices with their start and end apart: 13 -> 9, of which waited for: 11 -> 7; matrix products, arithmetic and copies ran while one was open for 11% -> 5% of each run, Pallas kernels for 0% -> 0%
where the time goes in v2:
time: 825 us; the launch traced here: 817 us
  waiting for transfers between devices  515 us (62%)
  Pallas kernels  75.6 us (9%)
  blocking collectives  72.9 us (9%)
  matrix products  64.5 us (8%)
  other arithmetic  44.9 us (5%)
  local copies, waits for them, and re-layouts  27.7 us (3%)
  between operations  14.8 us (2%)
    psum x1, waiting for transfers between devices, ctx_sum(): return lax.psum(grad.astype(jnp.bfloat16), 'ctx').astype(jnp.float32)  398 us
    reduce_scatter x4, waiting for transfers between devices, scatter_rows(): lax.psum_scatter(values.astype(jnp.bfloat16), 'fsdp', scatter_dimension=0...  65 us
    pallas_call x4, Pallas kernels, exchange(): pl.pallas_call(functools.partial(exchange_kernel, count), out_shape=jax.S...  61.8 us
    all_gather x4, waiting for transfers between devices, gather_rows(): return lax.all_gather(values, 'fsdp', axis=0, tiled=True)  50.9 us
    psum x1, blocking collectives, per_device(): lax.psum(jnp.stack([gain_one_grad, gain_two_grad]), ('fsdp', 'ctx'))  39.8 us
    all_gather x1, blocking collectives, per_device(): key_places = lax.all_gather(query_places, 'ctx', axis=1, tiled=True)  26.9 us
    dot_general x7, matrix products, product_back(): lax.dot_general(left, right, (((1,), (1,)), ((), ())), preferred_element_...  25.8 us
    dot_general x7, matrix products, product(): return jnp.dot(left, right, preferred_element_type=jnp.float32)  19.7 us
  transfers between devices with their start and end apart: 9, of which 7 were waited for; matrix products, arithmetic and copies ran while one was open for 5% of the time, Pallas kernels for 0%

profile of v2, /device:TPU:0, one launch (start us, length us, event | category | flops | bytes accessed | tf_op | source)
XLA Modules:
  0.0 816.6 jit_solution(10844911141454761481)
XLA Ops:
  8.8 6.2 all-gather
  15.0 26.9 %all_gather.19 = s32[4,1024]{1,0:T(4,128)S(1)} all-gather(s32[4,128]{1,0:T(4,128)S(1)} %bitcast.113), channel_id=1, replica_groups=mesh['fsdp'=4,'ctx'=8] {'ctx'}, dimensions={1}, use_global_device_ids=true | all-gather | bytes 18432 | tf_op jit(solution)/shard_map/all_gather | solution.py:374
  60.5 12.4 %exchange_1.1 = bf16[8,128,384]{2,1,0:T(8,128)(2,1)} custom-call(bf16[8,128,384]{2,1,0:T(8,128)(2,1)} %bitcast.94), custom_call_target="tpu_custom_call" | custom-call | tf_op jit(solution)/shard_map/exchange_1/pallas_call | solution.py:324
  74.0 5.6 attention_forward.1
  80.4 16.4 %exchange_2.1 = bf16[8,128,192]{2,1,0:T(8,128)(2,1)} custom-call(bf16[8,128,192]{2,1,0:T(8,128)(2,1)} %bitcast.90), custom_call_target="tpu_custom_call" | custom-call | tf_op jit(solution)/shard_map/exchange_2/pallas_call | solution.py:324
  98.9 3.6 convolution_convert_fusion.4
  102.5 30.3 %reduce-scatter.5.cloned.1.call-done = bf16[128,1536]{1,0:T(8,128)(2,1)} async-done(((bf16[512,1536]{1,0:T(8,128)(2,1)}), bf16[128,1536]{1,0:T(8,128)(2,1)}) %reduce-scatter.5.cloned.1.call-update) | async-done | bytes 393232 | tf_op jit(solution)/shard_map/reduce_scatter | solution.py:344
  136.8 19.0 %all-gather.8.cloned.1.call-done = bf16[512,1536]{1,0:T(8,128)(2,1)} async-done(((bf16[128,1536]{1,0:T(8,128)(2,1)}), bf16[512,1536]{1,0:T(8,128)(2,1)}) %all-gather.8.cloned.1.call-update) | async-done | bytes 1572880 | tf_op jit(solution)/shard_map/all_gather | solution.py:340
  155.8 5.7 fusion.29
  161.5 3.1 fusion.30
  164.6 12.3 %all-gather.10.cloned.1.call-done = bf16[512,1536]{1,0:T(8,128)(2,1)} async-done(((bf16[128,1536]{1,0:T(8,128)(2,1)}), bf16[512,1536]{1,0:T(8,128)(2,1)}) %all-gather.10.cloned.1.call-update) | async-done | bytes 1572880 | tf_op jit(solution)/shard_map/all_gather | solution.py:340
  176.9 6.3 multiply_convert_fusion.1
  185.9 3.0 fusion.1
  188.9 28.1 %reduce-scatter.9.cloned.1.call-done = bf16[128,1536]{1,0:T(8,128)(2,1)} async-done(((bf16[512,1536]{1,0:T(8,128)(2,1)}), bf16[128,1536]{1,0:T(8,128)(2,1)}) %reduce-scatter.9.cloned.1.call-update) | async-done | bytes 393232 | tf_op jit(solution)/shard_map/reduce_scatter | solution.py:344
  222.2 19.5 %all-gather.12.cloned.1.call-done = bf16[512,1536]{1,0:T(8,128)(2,1)} async-done(((bf16[128,1536]{1,0:T(8,128)(2,1)}), bf16[512,1536]{1,0:T(8,128)(2,1)}) %all-gather.12.cloned.1.call-update) | async-done | bytes 1572880 | tf_op jit(solution)/shard_map/all_gather | solution.py:340
  241.8 3.5 convolution_convert_fusion.9
  251.0 13.5 %exchange_3.1 = bf16[8,128,192]{2,1,0:T(8,128)(2,1)} custom-call(bf16[8,128,192]{2,1,0:T(8,128)(2,1)} %bitcast.101), custom_call_target="tpu_custom_call" | custom-call | tf_op jit(solution)/shard_map/exchange_3/pallas_call | solution.py:324
  266.7 8.2 %attention_backward.1 = bf16[1024,384]{1,0:T(8,128)(2,1)S(1)} custom-call(s32[1024]{0:T(1024)S(1)} %bitcast.93, bf16[1024,384]{1,0:T(8,128)(2,1)S(1)} %bitcast.88, bf16[1024,192]{1,0:T(8,128)(2,1)S(1)} %bitcast.91), custom_call_target="tpu_custom_call" | custom-call | tf_op jit(solution)/shard_map/attention_backward/pallas_call | solution.py:479
  275.8 19.5 %exchange_4.1 = bf16[8,128,384]{2,1,0:T(8,128)(2,1)} custom-call(bf16[8,128,384]{2,1,0:T(8,128)(2,1)} %bitcast.89), custom_call_target="tpu_custom_call" | custom-call | tf_op jit(solution)/shard_map/exchange_4/pallas_call | solution.py:324
  311.0 2.8 convolution_add_fusion.1
  316.0 4.2 convolution_convert_fusion.3
  320.2 5.4 convolution_convert_fusion.2
  325.6 3.5 convolution_convert_fusion.1
  329.1 3.5 convolution_convert_fusion
  341.4 6.6 reduce-scatter.11.cloned.1.call-done
  349.5 39.8 %psum.56 = f32[2,1536]{1,0:T(2,128)S(1)} all-reduce(f32[2,1536]{1,0:T(2,128)S(1)} %pad_maximum_fusion.4), channel_id=1, replica_groups=mesh['fsdp'=4,'ctx'=8] {'fsdp','ctx'}, use_global_device_ids=true, to_apply=%region_10.11 | all-reduce | flops 3072 | bytes 24576 | tf_op jit(solution)/shard_map/psum | solution.py:520
  389.9 2.8 fusion.10
  392.7 398.0 %all-reduce.3.cloned.1.call-done = (bf16[384,1536]{1,0:T(8,128)(2,1)}, bf16[192,1536]{1,0:T(8,128)(2,1)}, bf16[192,1536]{1,0:T(8,128)(2,1)}, bf16[384,1536]{1,0:...) async-done(((bf16[384,1536]{1,0:T(8,128)(2,1)}, bf16[192,1536]{1,0:T(8,128)(2,1)}, bf16[192,1536]{1,0:T(8,128)(2,1)}, ...) | async-done | bytes 12976144 | tf_op jit(solution)/shard_map/psum | solution.py:518
  790.7 3.1 convert_element_type.171
  798.8 3.6 convert_element_type.179
  802.4 3.6 convert_element_type.181
  806.0 3.6 convert_element_type.183
  (174 shorter events, 78.5 us)
Async XLA Ops:
  7.2 169.8 %copy-start = (bf16[1024,1536]{1,0:T(8,128)(2,1)S(1)}, bf16[1024,1536]{1,0:T(8,128)(2,1)}, u32[]{:S(2)}) copy-start(bf16[1024,1536]{1,0:T(8,128)(2,1)} %param.23) | copy-start | bytes 9437188
  7.2 35.2 %all-gather.6.cloned.1.call-start = ((), (), s32[]{:S(2)}) async-start(), calls=%async_computation.4 | async-start | bytes 1966080 | tf_op jit(solution)/shard_map/all_gather | solution.py:340
  7.9 125.0 %reduce-scatter.5.cloned.1.call-start = ((), (), s32[]{:S(2)}) async-start(), calls=%async_computation.5 | async-start | bytes 1966080 | tf_op jit(solution)/shard_map/reduce_scatter | solution.py:344
  8.8 42.2 %copy-start.29 = (f32[1536]{0:T(1024)}, f32[1536]{0:T(1024)S(1)}, u32[]{:S(2)}) copy-start(f32[1536]{0:T(1024)S(1)} %convert_element_type.142) | copy-start | bytes 18436
  42.4 11.3 %copy-start.17 = (f32[512,48]{0,1:T(8,128)}, f32[512,48]{0,1:T(8,128)S(1)}, u32[]{:S(2)}) copy-start(f32[512,48]{0,1:T(8,128)S(1)} %get-tuple-element.39) | copy-start | bytes 294916
  42.4 11.3 %copy-start.18 = (f32[512,48]{0,1:T(8,128)}, f32[512,48]{0,1:T(8,128)S(1)}, u32[]{:S(2)}) copy-start(f32[512,48]{0,1:T(8,128)S(1)} %get-tuple-element.40) | copy-start | bytes 294916
  44.3 6.7 copy-start.32
  98.9 3.7 copy-start.34
  98.9 34.0 %copy-start.7 = (bf16[128,1536]{1,0:T(8,128)(2,1)S(1)}, bf16[128,1536]{1,0:T(8,128)(2,1)}, u32[]{:S(2)}) copy-start(bf16[128,1536]{1,0:T(8,128)(2,1)} %param.12) | copy-start | bytes 1179652
  102.5 53.4 %all-gather.8.cloned.1.call-start = ((), (), s32[]{:S(2)}) async-start(), calls=%async_computation.6 | async-start | bytes 1966080 | tf_op jit(solution)/shard_map/all_gather | solution.py:340
  136.0 40.9 %all-gather.10.cloned.1.call-start = ((), (), s32[]{:S(2)}) async-start(), calls=%async_computation.8 | async-start | bytes 1966080 | tf_op jit(solution)/shard_map/all_gather | solution.py:340
  136.6 80.4 %reduce-scatter.9.cloned.1.call-start = ((), (), s32[]{:S(2)}) async-start(), calls=%async_computation.9 | async-start | bytes 1966080 | tf_op jit(solution)/shard_map/reduce_scatter | solution.py:344
  155.8 5.7 copy-start.38
  155.8 5.7 copy-start.40
  176.9 6.3 copy-start.37
  188.9 52.9 %all-gather.12.cloned.1.call-start = ((), (), s32[]{:S(2)}) async-start(), calls=%async_computation.10 | async-start | bytes 1966080 | tf_op jit(solution)/shard_map/all_gather | solution.py:340
  222.0 126.0 %reduce-scatter.11.cloned.1.call-start = ((), (), s32[]{:S(2)}) async-start(), calls=%async_computation.11 | async-start | bytes 1966080 | tf_op jit(solution)/shard_map/reduce_scatter | solution.py:344
  315.6 74.3 %reduce-scatter.7.cloned.1.call-start = ((), (), s32[]{:S(2)}) async-start(), calls=%async_computation.7 | async-start | bytes 1966080 | tf_op jit(solution)/shard_map/reduce_scatter | solution.py:344
  320.1 5.5 copy-start.41
  320.1 5.4 copy-start.45
  320.2 470.6 %all-reduce.3.cloned.1.call-start = ((), (), s32[]{:S(2)}) async-start(), calls=%async_computation.12 | async-start | bytes 25952256 | tf_op jit(solution)/shard_map/psum | solution.py:518
  325.6 3.5 copy-start.42
  329.1 3.5 copy-start.9
  329.1 3.5 copy-start.23
  339.5 50.4 %copy-start.8 = (bf16[128,1536]{1,0:T(8,128)(2,1)S(1)}, bf16[128,1536]{1,0:T(8,128)(2,1)}, u32[]{:S(2)}) copy-start(bf16[128,1536]{1,0:T(8,128)(2,1)} %reduce-scatter.5.cloned.1.call-done) | copy-start | bytes 1179652
  339.5 50.4 %copy-start.10 = (bf16[128,1536]{1,0:T(8,128)(2,1)S(1)}, bf16[128,1536]{1,0:T(8,128)(2,1)}, u32[]{:S(2)}) copy-start(bf16[128,1536]{1,0:T(8,128)(2,1)} %param.14) | copy-start | bytes 1179652
  339.5 50.4 %copy-start.11 = (bf16[128,1536]{1,0:T(8,128)(2,1)S(1)}, bf16[128,1536]{1,0:T(8,128)(2,1)}, u32[]{:S(2)}) copy-start(bf16[128,1536]{1,0:T(8,128)(2,1)} %reduce-scatter.9.cloned.1.call-done) | copy-start | bytes 1179652
  339.5 50.5 %copy-start.36 = (f32[128]{0:T(128)S(1)}, f32[128]{0:T(128)}, u32[]{:S(2)}) copy-start(f32[128]{0:T(128)} %copy-done.35) | copy-start | bytes 1540
  790.7 4.2 copy-start.26
  798.8 3.6 copy-start.13
  802.4 3.6 copy-start.12
  806.0 3.6 copy-start.1
  (25 other events, 51.6 us)
Sparse Core Ops, SparseCore 0:
  9.6 22.3 all-gather.5
  102.6 30.2 reduce-scatter.4
  136.2 19.6 all-gather.7
  157.2 19.6 all-gather.9
  189.0 27.9 reduce-scatter.8
  222.1 19.6 all-gather.11
  315.8 32.1 reduce-scatter.10
  351.1 28.1 reduce-scatter.6
  386.1 404.5 all-reduce.2

commit v3 on v2

--- a/solution.py
+++ b/solution.py
@@ -336,6 +336,336 @@
     )(values)
 
 
+SPINE_ROWS = 48
+LINE_ROWS = 64
+ROUND_ROWS = 2 * SPINE_ROWS + LINE_ROWS
+LEAD = 2
+
+
+def reduce_kernel(
+    rounds,
+    grads_ref,
+    gain_ref,
+    out_ref,
+    gain_out_ref,
+    own,
+    spine_in,
+    line_in,
+    gain_near,
+    gain_far,
+    load_sem,
+    spine_up,
+    spine_got,
+    leaf_up,
+    line_up,
+    line_got,
+    spine_down,
+    spine_back,
+    leaf_back,
+    line_down,
+    line_back,
+    near_send,
+    near_recv,
+    far_send,
+    far_recv,
+):
+    me = lax.axis_index("ctx")
+    row = lax.axis_index("fsdp")
+    depth = lax.div(me, 2)
+    side = lax.rem(me, 2)
+    other_side = me + 1 - 2 * side
+    above, below = depth < 3, depth > 0
+    barrier = pltpu.get_barrier_semaphore()
+
+    for step in range(1, 4):
+        pl.semaphore_signal(
+            barrier,
+            inc=1,
+            device_id={"fsdp": lax.rem(row + step, 4)},
+            device_id_type=pl.DeviceIdType.MESH,
+        )
+    for step in range(1, 8):
+        pl.semaphore_signal(barrier, inc=1, **peer(lax.rem(me + step, 8)))
+
+    def load(index):
+        span = pl.ds(pl.multiple_of(index * ROUND_ROWS, 16), ROUND_ROWS)
+        return pltpu.make_async_copy(grads_ref.at[span], own.at[span], load_sem.at[index])
+
+    @pl.loop(0, rounds)
+    def _(index):
+        load(index).start()
+
+    pl.semaphore_wait(barrier, 10)
+    gain_near[row] = gain_ref[...]
+    near = [
+        pltpu.make_async_remote_copy(
+            src_ref=gain_ref,
+            dst_ref=gain_near.at[row],
+            send_sem=near_send.at[step],
+            recv_sem=near_recv.at[step],
+            device_id={"fsdp": lax.rem(row + step, 4)},
+            device_id_type=pl.DeviceIdType.MESH,
+        )
+        for step in range(1, 4)
+    ]
+    for copy in near:
+        copy.start()
+    far = [
+        pltpu.make_async_remote_copy(
+            src_ref=gain_far.at[me],
+            dst_ref=gain_far.at[me],
+            send_sem=far_send.at[step],
+            recv_sem=far_recv.at[step],
+            **peer(lax.rem(me + step, 8)),
+        )
+        for step in range(1, 8)
+    ]
+
+    def rows_at(start, count):
+        return pl.ds(pl.multiple_of(start, 16), count)
+
+    class Tree:
+        def __init__(self, index, line):
+            self.line = line
+            if line:
+                center = lax.rem(index, 4)
+                count = LINE_ROWS
+                start = index * ROUND_ROWS + 2 * SPINE_ROWS
+                self.box, self.up, self.got = line_in, line_up, line_got
+                self.down, self.back = line_down, line_back
+                root_side = lax.rem(index, 2)
+                on_cross = depth == center
+                self.root = jnp.logical_and(on_cross, side == root_side)
+                has_side = self.root
+                to_side = jnp.logical_and(on_cross, side != root_side)
+                reach = jnp.maximum(center, 3 - center)
+                away = jnp.abs(depth - center)
+                crossed = jnp.where(side == root_side, 0, 1)
+                self.rise_age = reach - away + jnp.where(self.root, 1, 0)
+                self.fall_age = reach + 1 + away + crossed
+            else:
+                center = 1 + side
+                count = SPINE_ROWS
+                start = index * ROUND_ROWS + side * SPINE_ROWS
+                self.box, self.up, self.got = spine_in, spine_up, spine_got
+                self.down, self.back = spine_down, spine_back
+                self.root = depth == center
+                has_side = None
+                to_side = None
+            self.rows = rows_at(start, count)
+            self.slot_rows = rows_at(index * count, count)
+            self.index = index
+            self.children = (
+                (jnp.logical_and(below, depth <= center), me - 2, 0),
+                (jnp.logical_and(above, depth >= center), me + 2, 1),
+                (has_side, other_side, 2),
+            )
+            parent = jnp.where(depth < center, me + 2, me - 2)
+            slot = jnp.where(depth < center, 0, 1)
+            if line:
+                parent = jnp.where(to_side, other_side, parent)
+                slot = jnp.where(to_side, 2, slot)
+            self.parent = jnp.where(self.root, other_side, parent)
+            self.parent_slot = jnp.where(self.root, 2, slot)
+
+        def up_copy(self):
+            return pltpu.make_async_remote_copy(
+                src_ref=own.at[self.rows],
+                dst_ref=self.box.at[self.parent_slot, self.slot_rows],
+                send_sem=self.up.at[self.index],
+                recv_sem=self.got.at[self.parent_slot, self.index],
+                **peer(self.parent),
+            )
+
+        def got_copy(self, child, slot):
+            return pltpu.make_async_remote_copy(
+                src_ref=own.at[self.rows],
+                dst_ref=self.box.at[slot, self.slot_rows],
+                send_sem=self.up.at[self.index],
+                recv_sem=self.got.at[slot, self.index],
+                **peer(child),
+            )
+
+        def down_copy(self, child, slot, source):
+            return pltpu.make_async_remote_copy(
+                src_ref=source.at[self.rows],
+                dst_ref=out_ref.at[self.rows],
+                send_sem=self.down.at[slot, self.index],
+                recv_sem=(self.back if slot < 2 or self.line else leaf_back).at[self.index],
+                **peer(child),
+            )
+
+        def each_child(self, action):
+            for present, child, slot in self.children:
+                if present is None:
+                    action(child, slot)
+                else:
+                    pl.when(present)(functools.partial(action, child, slot))
+
+        def rise(self):
+            self.each_child(lambda child, slot: self.got_copy(child, slot).wait_recv())
+            first, count = self.rows.start, self.rows.size
+            base = self.slot_rows.start
+            for piece in range(0, count, 16):
+                span = rows_at(first + piece, 16)
+                total = own[span, :].astype(jnp.float32)
+                for present, _, slot in self.children:
+                    part = self.box[slot, rows_at(base + piece, 16), :].astype(jnp.float32)
+                    total += part if present is None else jnp.where(present, part, 0.0)
+                own[span, :] = total.astype(jnp.bfloat16)
+
+            @pl.when(jnp.logical_not(self.root))
+            def _():
+                self.up_copy().start()
+
+            @pl.when(self.root)
+            def _():
+                self.keep().start()
+                self.each_child(lambda child, slot: self.down_copy(child, slot, own).start())
+
+        def keep(self):
+            return pltpu.make_async_copy(
+                own.at[self.rows], out_ref.at[self.rows], self.up.at[self.index]
+            )
+
+        def fall(self):
+            @pl.when(jnp.logical_not(self.root))
+            def _():
+                self.down_copy(self.parent, 0, out_ref).wait_recv()
+                self.each_child(lambda child, slot: self.down_copy(child, slot, out_ref).start())
+
+        def finish(self):
+            @pl.when(jnp.logical_not(self.root))
+            def _():
+                self.up_copy().wait_send()
+
+            @pl.when(self.root)
+            def _():
+                self.keep().wait()
+
+            self.each_child(lambda child, slot: self.down_copy(child, slot, out_ref).wait_send())
+
+    def leaf_rows(index):
+        return rows_at(index * ROUND_ROWS + (1 - side) * SPINE_ROWS, SPINE_ROWS)
+
+    def leaf_copy(index):
+        return pltpu.make_async_remote_copy(
+            src_ref=grads_ref.at[leaf_rows(index)],
+            dst_ref=spine_in.at[2, rows_at(index * SPINE_ROWS, SPINE_ROWS)],
+            send_sem=leaf_up.at[index],
+            recv_sem=spine_got.at[2, index],
+            **peer(other_side),
+        )
+
+    def leaf_result(index):
+        return pltpu.make_async_remote_copy(
+            src_ref=own.at[leaf_rows(index)],
+            dst_ref=out_ref.at[leaf_rows(index)],
+            send_sem=leaf_up.at[index],
+            recv_sem=leaf_back.at[index],
+            **peer(other_side),
+        )
+
+    for index in range(min(LEAD, rounds)):
+        leaf_copy(index).start()
+
+    def valid(index):
+        return jnp.logical_and(index >= 0, index < rounds)
+
+    @pl.loop(0, rounds + 9)
+    def _(now):
+        @pl.when(now < rounds)
+        def _():
+            load(now).wait()
+
+        @pl.when(now + LEAD < rounds)
+        def _():
+            leaf_copy(now + LEAD).start()
+
+        @pl.when(now == 1)
+        def _():
+            for copy in near:
+                copy.wait()
+            gain_far[me] = gain_near[0] + gain_near[1] + gain_near[2] + gain_near[3]
+            for copy in far:
+                copy.start()
+
+        far_side = jnp.abs(depth - 2 + side)
+        off_center = jnp.abs(depth - 1 - side)
+        spine_rise = Tree(now - 3 + off_center, False)
+        pl.when(valid(spine_rise.index))(spine_rise.rise)
+
+        @pl.loop(0, 5)
+        def _(age):
+            tree = Tree(now - age, True)
+            pl.when(jnp.logical_and(valid(tree.index), tree.rise_age == age))(tree.rise)
+
+        spine_fall = Tree(now - 3 - off_center, False)
+        pl.when(valid(spine_fall.index))(spine_fall.fall)
+
+        @pl.loop(4, 9)
+        def _(age):
+            tree = Tree(now - age, True)
+            pl.when(jnp.logical_and(valid(tree.index), tree.fall_age == age))(tree.fall)
+
+        leaf_fall = now - 4 - far_side
+        pl.when(valid(leaf_fall))(lambda: leaf_result(leaf_fall).wait_recv())
+
+    for copy in far:
+        copy.wait()
+    gain_total = gain_far[0]
+    for step in range(1, 8):
+        gain_total += gain_far[step]
+    gain_out_ref[...] = gain_total
+
+    @pl.loop(0, rounds)
+    def _(index):
+        Tree(index, False).finish()
+        Tree(index, True).finish()
+        leaf_copy(index).wait_send()
+
+
+def reduce_gradients(grads, gains, key):
+    rounds = grads.shape[0] // ROUND_ROWS
+    width = grads.shape[1]
+    dma = pltpu.SemaphoreType.DMA
+    return pl.pallas_call(
+        functools.partial(reduce_kernel, rounds),
+        out_shape=(
+            jax.ShapeDtypeStruct(grads.shape, grads.dtype),
+            jax.ShapeDtypeStruct(gains.shape, gains.dtype),
+        ),
+        in_specs=[pl.BlockSpec(memory_space=pl.ANY), vmem()],
+        out_specs=(pl.BlockSpec(memory_space=pl.ANY), vmem()),
+        scratch_shapes=[
+            pltpu.VMEM(grads.shape, grads.dtype),
+            pltpu.VMEM((3, rounds * SPINE_ROWS, width), grads.dtype),
+            pltpu.VMEM((3, rounds * LINE_ROWS, width), grads.dtype),
+            pltpu.VMEM((4,) + gains.shape, gains.dtype),
+            pltpu.VMEM((8,) + gains.shape, gains.dtype),
+            dma((rounds,)),
+            dma((rounds,)),
+            dma((3, rounds)),
+            dma((rounds,)),
+            dma((rounds,)),
+            dma((3, rounds)),
+            dma((3, rounds)),
+            dma((rounds,)),
+            dma((rounds,)),
+            dma((3, rounds)),
+            dma((rounds,)),
+            dma((4,)),
+            dma((4,)),
+            dma((8,)),
+            dma((8,)),
+        ],
+        compiler_params=pltpu.CompilerParams(
+            collective_id=key, has_side_effects=True, vmem_limit_bytes=60 * 2**20
+        ),
+        name="reduce_gradients",
+    )(grads, gains)
+
+
 def gather_rows(values):
     return lax.all_gather(values, "fsdp", axis=0, tiled=True)
 
@@ -514,22 +844,38 @@
     gain_one_grad = jnp.sum(grad_normed_one * own_unit, axis=0)
     input_grad = grad_hidden + norm_back(own(scale_one), own_unit, grad_normed_one * gain_one)
 
-    def ctx_sum(grad):
-        return lax.psum(grad.astype(jnp.bfloat16), "ctx").astype(jnp.float32)
-
-    gain_sums = lax.psum(jnp.stack([gain_one_grad, gain_two_grad]), ("fsdp", "ctx"))
+    grads = (grad_query, grad_key, grad_value, grad_output, grad_gate, grad_up, grad_down)
+    if by_head:
+        rows = sum(grad.shape[0] for grad in grads)
+        spare = jnp.zeros((-rows % ROUND_ROWS, grads[0].shape[1]), jnp.bfloat16)
+        gain_parts = jnp.stack([gain_one_grad, gain_two_grad]).reshape(24, 128)
+        summed, gain_sums = reduce_gradients(
+            jnp.concatenate([grad.astype(jnp.bfloat16) for grad in grads] + [spare]),
+            gain_parts,
+            5,
+        )
+        gain_sums = gain_sums.reshape(2, -1)
+        parts, start = [], 0
+        for grad in grads:
+            parts.append(summed[start : start + grad.shape[0]].astype(jnp.float32))
+            start += grad.shape[0]
+    else:
+        parts = [
+            lax.psum(grad.astype(jnp.bfloat16), "ctx").astype(jnp.float32) for grad in grads
+        ]
+        gain_sums = lax.psum(jnp.stack([gain_one_grad, gain_two_grad]), ("fsdp", "ctx"))
     return (
         layer_output,
         input_grad,
         gain_sums[0],
-        ctx_sum(grad_query),
-        ctx_sum(grad_key),
-        ctx_sum(grad_value),
-        ctx_sum(grad_output),
+        parts[0],
+        parts[1],
+        parts[2],
+        parts[3],
         gain_sums[1],
-        ctx_sum(grad_gate),
-        ctx_sum(grad_up),
-        ctx_sum(grad_down),
+        parts[4],
+        parts[5],
+        parts[6],
     )
 
 

time: 825 us -> 637 us (0.77)
  waiting for transfers between devices: 515 us -> 115 us
  Pallas kernels: 75.6 us -> 325 us
  blocking collectives: 72.9 us -> 33.2 us
    psum x1 -> x0, waiting for transfers between devices: 398 us -> none  [ctx_sum(): return lax.psum(grad.astype(jnp.bfloat16), 'ctx').astype(jnp.float32)]
    pallas_call x0 -> x1, Pallas kernels: none -> 249 us  [reduce_gradients(): pl.pallas_call(functools.partial(reduce_kernel, rounds), out_shape=(jax.S...]
    psum x1 -> x0, blocking collectives: 39.8 us -> none  [per_device(): lax.psum(jnp.stack([gain_one_grad, gain_two_grad]), ('fsdp', 'ctx'))]
    convert_element_type x7 -> x3, other arithmetic: 17.8 us -> 17.1 us  [per_device(): parts.append(summed[start:start + grad.shape[0]].astype(jnp.float32))]
  transfers between devices with their start and end apart: 9 -> 8, of which waited for: 7 -> 6; matrix products, arithmetic and copies ran while one was open for 5% -> 9% of each run, Pallas kernels for 0% -> 40%
where the time goes in v3:
time: 637 us; the launch traced here: 629 us
  Pallas kernels  325 us (51%)
  waiting for transfers between devices  115 us (18%)
  matrix products  60.7 us (10%)
  other arithmetic  48.2 us (8%)
  blocking collectives  33.2 us (5%)
  local copies, waits for them, and re-layouts  30.5 us (5%)
  between operations  15.1 us (2%)
    pallas_call x1, Pallas kernels, reduce_gradients(): pl.pallas_call(functools.partial(reduce_kernel, rounds), out_shape=(jax.S...  249 us
    reduce_scatter x4, waiting for transfers between devices, scatter_rows(): lax.psum_scatter(values.astype(jnp.bfloat16), 'fsdp', scatter_dimension=0...  62.9 us
    pallas_call x4, Pallas kernels, exchange(): pl.pallas_call(functools.partial(exchange_kernel, count), out_shape=jax.S...  61.8 us
    all_gather x4, waiting for transfers between devices, gather_rows(): return lax.all_gather(values, 'fsdp', axis=0, tiled=True)  50.9 us
    all_gather x1, blocking collectives, per_device(): key_places = lax.all_gather(query_places, 'ctx', axis=1, tiled=True)  26.9 us
    dot_general x7, matrix products, product_back(): lax.dot_general(left, right, (((1,), (1,)), ((), ())), preferred_element_...  25.7 us
    dot_general x7, matrix products, product_rows(): lax.dot_general(left, right, (((0,), (0,)), ((), ())), preferred_element_...  18.9 us
    convert_element_type x3, other arithmetic, per_device(): parts.append(summed[start:start + grad.shape[0]].astype(jnp.float32))  17.1 us
  transfers between devices with their start and end apart: 8, of which 6 were waited for; matrix products, arithmetic and copies ran while one was open for 9% of the time, Pallas kernels for 40%

profile of v3, /device:TPU:0, one launch (start us, length us, event | category | flops | bytes accessed | tf_op | source)
XLA Modules:
  0.0 628.5 jit_solution(16233315717346233013)
XLA Ops:
  8.0 6.3 %all-gather = s32[4,1,128]{2,1,0:T(1,128)S(1)} all-gather(s32[1,1,128]{2,1,0:T(1,128)} %bitcast.119), channel_id=1, replica_groups=mesh['fsdp'=4,'ctx'=8] {'fsdp'}, dimensions={0}, use_global_device_ids=true | all-gather | bytes 2560 | tf_op jit(solution)/shard_map/all_gather | solution.py:670
  15.0 26.9 %all_gather.19 = s32[4,1024]{1,0:T(4,128)S(1)} all-gather(s32[4,128]{1,0:T(4,128)S(1)} %bitcast.117), channel_id=1, replica_groups=mesh['fsdp'=4,'ctx'=8] {'ctx'}, dimensions={1}, use_global_device_ids=true | all-gather | bytes 18432 | tf_op jit(solution)/shard_map/all_gather | solution.py:704
  51.0 2.6 fusion.34
  60.5 12.4 %exchange_1.1 = bf16[8,128,384]{2,1,0:T(8,128)(2,1)} custom-call(bf16[8,128,384]{2,1,0:T(8,128)(2,1)} %bitcast.98), custom_call_target="tpu_custom_call" | custom-call | tf_op jit(solution)/shard_map/exchange_1/pallas_call | solution.py:324
  74.0 5.6 attention_forward.1
  80.4 16.4 %exchange_2.1 = bf16[8,128,192]{2,1,0:T(8,128)(2,1)} custom-call(bf16[8,128,192]{2,1,0:T(8,128)(2,1)} %bitcast.94), custom_call_target="tpu_custom_call" | custom-call | tf_op jit(solution)/shard_map/exchange_2/pallas_call | solution.py:324
  98.9 3.5 convolution_convert_fusion.4
  102.5 30.3 %reduce-scatter.5.cloned.1.call-done = bf16[128,1536]{1,0:T(8,128)(2,1)} async-done(((bf16[512,1536]{1,0:T(8,128)(2,1)}), bf16[128,1536]{1,0:T(8,128)(2,1)}) %reduce-scatter.5.cloned.1.call-update) | async-done | bytes 393232 | tf_op jit(solution)/shard_map/reduce_scatter | solution.py:674
  136.8 19.0 %all-gather.8.cloned.1.call-done = bf16[512,1536]{1,0:T(8,128)(2,1)} async-done(((bf16[128,1536]{1,0:T(8,128)(2,1)}), bf16[512,1536]{1,0:T(8,128)(2,1)}) %all-gather.8.cloned.1.call-update) | async-done | bytes 1572880 | tf_op jit(solution)/shard_map/all_gather | solution.py:670
  155.8 5.6 fusion.37
  161.4 3.1 fusion.36
  164.6 12.3 %all-gather.10.cloned.1.call-done = bf16[512,1536]{1,0:T(8,128)(2,1)} async-done(((bf16[128,1536]{1,0:T(8,128)(2,1)}), bf16[512,1536]{1,0:T(8,128)(2,1)}) %all-gather.10.cloned.1.call-update) | async-done | bytes 1572880 | tf_op jit(solution)/shard_map/all_gather | solution.py:670
  176.9 6.3 %multiply_convert_fusion.1 = (bf16[512,1024]{1,0:T(8,128)(2,1)S(1)}, bf16[512,1024]{1,0:T(8,128)(2,1)S(1)}, bf16[512,1024]{1,0:T(8,128)(2,1)}) fusion(f32[512,1024]{1,0:T(8,128)} %fusion.36, f32[512,1024]{1,0:T(8,128)} %fusion.37, bf16[512,1536]{1,0:T(8,128)(2,1)} %all-gather.10.cloned.1.call-done, bf16[1024,1536]{1,0:T(8,128)(2,1)S(1)} %copy-done), kind=kOutput, calls=%fused_computation.28 | convolution fusion | flops 1618477056 | bytes 12058624 | tf_op jit(solution)/shard_map/dot_general | solution.py:25
  185.8 3.0 fusion.4
  188.9 28.2 %reduce-scatter.9.cloned.1.call-done = bf16[128,1536]{1,0:T(8,128)(2,1)} async-done(((bf16[512,1536]{1,0:T(8,128)(2,1)}), bf16[128,1536]{1,0:T(8,128)(2,1)}) %reduce-scatter.9.cloned.1.call-update) | async-done | bytes 393232 | tf_op jit(solution)/shard_map/reduce_scatter | solution.py:674
  222.2 19.5 %all-gather.12.cloned.1.call-done = bf16[512,1536]{1,0:T(8,128)(2,1)} async-done(((bf16[128,1536]{1,0:T(8,128)(2,1)}), bf16[512,1536]{1,0:T(8,128)(2,1)}) %all-gather.12.cloned.1.call-update) | async-done | bytes 1572880 | tf_op jit(solution)/shard_map/all_gather | solution.py:670
  241.8 3.5 convolution_convert_fusion.9
  251.0 13.5 %exchange_3.1 = bf16[8,128,192]{2,1,0:T(8,128)(2,1)} custom-call(bf16[8,128,192]{2,1,0:T(8,128)(2,1)} %bitcast.105), custom_call_target="tpu_custom_call" | custom-call | tf_op jit(solution)/shard_map/exchange_3/pallas_call | solution.py:324
  266.8 8.2 %attention_backward.1 = bf16[1024,384]{1,0:T(8,128)(2,1)S(1)} custom-call(s32[1024]{0:T(1024)S(1)} %bitcast.97, bf16[1024,384]{1,0:T(8,128)(2,1)S(1)} %bitcast.92, bf16[1024,192]{1,0:T(8,128)(2,1)S(1)} %bitcast.95), custom_call_target="tpu_custom_call" | custom-call | tf_op jit(solution)/shard_map/attention_backward/pallas_call | solution.py:809
  275.9 19.5 %exchange_4.1 = bf16[8,128,384]{2,1,0:T(8,128)(2,1)} custom-call(bf16[8,128,384]{2,1,0:T(8,128)(2,1)} %bitcast.93), custom_call_target="tpu_custom_call" | custom-call | tf_op jit(solution)/shard_map/exchange_4/pallas_call | solution.py:324
  316.3 3.4 convert_multiply_fusion
  319.7 3.0 convolution_convert_fusion.3
  323.5 3.5 fusion.6
  331.9 3.5 fusion.2
  335.4 3.5 fusion.1
  339.0 3.6 fusion
  343.2 4.4 reduce-scatter.11.cloned.1.call-done
  349.8 249.2 %reduce_gradients.1 = (bf16[4320,1536]{1,0:T(8,128)(2,1)}, f32[24,128]{1,0:T(8,128)}) custom-call(bf16[4320,1536]{1,0:T(8,128)(2,1)} %broadcast_dynamic-update-slice_fusion.grads_ref, f32[24,128]{1,0:T(8,128)} %reshape.202.gain_ref), custom_call_target="tpu_custom_call" | custom-call | tf_op jit(solution)/shard_map/reduce_gradients/pallas_call | solution.py:632
  600.9 2.9 slice_convert_fusion.5
  603.8 4.5 slice_convert_fusion.3
  608.3 9.7 %slice_convert_fusion = (f32[1024,1536]{1,0:T(8,128)}, f32[1024,1536]{1,0:T(8,128)}, f32[1024,1536]{1,0:T(8,128)}) fusion(bf16[4320,1536]{1,0:T(8,128)(2,1)} %get-tuple-element.14), kind=kLoop, calls=%fused_computation.12 | loop fusion | flops 4718592 | bytes 28311552 | tf_op jit(solution)/shard_map/convert_element_type | solution.py:860
  618.0 3.2 fusion.17
  (151 shorter events, 73.2 us)
Async XLA Ops:
  7.2 169.7 %copy-start = (bf16[1024,1536]{1,0:T(8,128)(2,1)S(1)}, bf16[1024,1536]{1,0:T(8,128)(2,1)}, u32[]{:S(2)}) copy-start(bf16[1024,1536]{1,0:T(8,128)(2,1)} %param.23) | copy-start | bytes 9437188
  7.2 35.2 %all-gather.6.cloned.1.call-start = ((), (), s32[]{:S(2)}) async-start(), calls=%async_computation.4 | async-start | bytes 1966080 | tf_op jit(solution)/shard_map/all_gather | solution.py:670
  7.9 124.9 %reduce-scatter.5.cloned.1.call-start = ((), (), s32[]{:S(2)}) async-start(), calls=%async_computation.5 | async-start | bytes 1966080 | tf_op jit(solution)/shard_map/reduce_scatter | solution.py:674
  15.0 36.0 %copy-start.19 = (f32[1536]{0:T(1024)}, f32[1536]{0:T(1024)S(1)}, u32[]{:S(2)}) copy-start(f32[1536]{0:T(1024)S(1)} %convert_element_type.142) | copy-start | bytes 18436
  42.4 11.3 %copy-start.10 = (f32[512,48]{0,1:T(8,128)}, f32[512,48]{0,1:T(8,128)S(1)}, u32[]{:S(2)}) copy-start(f32[512,48]{0,1:T(8,128)S(1)} %get-tuple-element.43) | copy-start | bytes 294916
  42.4 11.3 %copy-start.11 = (f32[512,48]{0,1:T(8,128)}, f32[512,48]{0,1:T(8,128)S(1)}, u32[]{:S(2)}) copy-start(f32[512,48]{0,1:T(8,128)S(1)} %get-tuple-element.44) | copy-start | bytes 294916
  44.3 6.7 %copy-start.21 = (f32[512]{0:T(512)}, f32[512]{0:T(512)S(1)}, u32[]{:S(2)}) copy-start(f32[512]{0:T(512)S(1)} %add_rsqrt_fusion) | copy-start | bytes 6148
  80.4 22.1 %copy-start.23 = (bf16[1536]{0:T(1024)(128)(2,1)S(1)}, bf16[1536]{0:T(1024)(128)(2,1)}, u32[]{:S(2)}) copy-start(bf16[1536]{0:T(1024)(128)(2,1)} %param.20) | copy-start | bytes 9220
  80.4 52.4 %copy-start.7 = (bf16[128,1536]{1,0:T(8,128)(2,1)S(1)}, bf16[128,1536]{1,0:T(8,128)(2,1)}, u32[]{:S(2)}) copy-start(bf16[128,1536]{1,0:T(8,128)(2,1)} %param.12) | copy-start | bytes 1179652
  102.4 53.3 %all-gather.8.cloned.1.call-start = ((), (), s32[]{:S(2)}) async-start(), calls=%async_computation.6 | async-start | bytes 1966080 | tf_op jit(solution)/shard_map/all_gather | solution.py:670
  136.0 40.9 %all-gather.10.cloned.1.call-start = ((), (), s32[]{:S(2)}) async-start(), calls=%async_computation.8 | async-start | bytes 1966080 | tf_op jit(solution)/shard_map/all_gather | solution.py:670
  136.6 80.5 %reduce-scatter.9.cloned.1.call-start = ((), (), s32[]{:S(2)}) async-start(), calls=%async_computation.9 | async-start | bytes 1966080 | tf_op jit(solution)/shard_map/reduce_scatter | solution.py:674
  155.8 5.7 copy-start.26
  155.8 5.7 copy-start.29
  176.9 6.3 %copy-start.27 = (bf16[1024,1536]{1,0:T(8,128)(2,1)S(1)}, bf16[1024,1536]{1,0:T(8,128)(2,1)}, u32[]{:S(2)}) copy-start(bf16[1024,1536]{1,0:T(8,128)(2,1)} %param.21) | copy-start | bytes 9437188
  183.2 2.6 copy-start.28
  188.8 53.0 %all-gather.12.cloned.1.call-start = ((), (), s32[]{:S(2)}) async-start(), calls=%async_computation.10 | async-start | bytes 1966080 | tf_op jit(solution)/shard_map/all_gather | solution.py:670
  222.0 125.7 %reduce-scatter.11.cloned.1.call-start = ((), (), s32[]{:S(2)}) async-start(), calls=%async_computation.11 | async-start | bytes 1966080 | tf_op jit(solution)/shard_map/reduce_scatter | solution.py:674
  309.9 2.5 copy-start.9
  309.9 2.5 copy-start.17
  315.4 302.7 %reduce-scatter.7.cloned.1.call-start = ((), (), s32[]{:S(2)}) async-start(), calls=%async_computation.7 | async-start | bytes 1966080 | tf_op jit(solution)/shard_map/reduce_scatter | solution.py:674
  315.7 4.0 copy-start.37
  322.7 4.4 copy-start.8
  322.7 4.4 copy-start.14
  322.7 4.4 copy-start.20
  327.1 3.0 copy-start.12
  327.1 3.0 copy-start.32
  331.9 3.5 copy-start.34
  335.4 3.5 copy-start.31
  335.4 3.5 copy-start.38
  608.3 9.8 %copy-start.25 = (f32[128]{0:T(128)S(1)}, f32[128]{0:T(128)}, u32[]{:S(2)}) copy-start(f32[128]{0:T(128)} %copy-done.24) | copy-start | bytes 1540
  608.3 12.9 %copy-start.1 = (bf16[1024,1536]{1,0:T(8,128)(2,1)S(1)}, bf16[1024,1536]{1,0:T(8,128)(2,1)}, u32[]{:S(2)}) copy-start(bf16[1024,1536]{1,0:T(8,128)(2,1)} %param.23) | copy-start | bytes 9437188
  (15 other events, 19.3 us)
Sparse Core Ops, SparseCore 0:
  9.6 22.3 all-gather.5
  102.6 30.2 reduce-scatter.4
  136.1 19.6 all-gather.7
  157.2 19.6 all-gather.9
  188.9 28.0 reduce-scatter.8
  222.1 19.6 all-gather.11
  315.5 32.1 reduce-scatter.10
  350.2 27.9 reduce-scatter.6

commit v4 on v2

--- a/solution.py
+++ b/solution.py
@@ -186,16 +186,7 @@
     return lax.fori_loop(0, block_total, grad_step, initial)
 
 
-def softmax_parts(query_rows, key_rows, first_row):
-    scores = product_back(query_rows, key_rows) * (1.0 / math.sqrt(HEAD_DIM))
-    rows = lax.broadcasted_iota(jnp.int32, scores.shape, 0) + first_row
-    columns = lax.broadcasted_iota(jnp.int32, scores.shape, 1)
-    scores = jnp.where(columns <= rows, scores, -1e30)
-    spread = jnp.exp(scores - jnp.max(scores, axis=-1, keepdims=True))
-    return spread * (1.0 / jnp.sum(spread, axis=-1, keepdims=True))
-
-
-def sort_blocks(place_ref, source_ref, targets, block):
+def sort_places(place_ref, source_ref, targets, block):
     block_total = source_ref.shape[0] // block
     for slot in range(block_total):
         place = place_ref[slot * block]
@@ -208,7 +199,7 @@
 
 
 def attention_forward_kernel(block, place_ref, packed_ref, out_ref, q0, q1, k, v, result):
-    sort_blocks(place_ref, packed_ref, (q0, q1, k, v), block)
+    sort_places(place_ref, packed_ref, (q0, q1, k, v), block)
     length = packed_ref.shape[0]
     tile = min(256, length)
     for first in range(0, length, tile):
@@ -224,47 +215,13 @@
         )
 
 
-def attention_backward_kernel(
-    block, place_ref, packed_ref, grad_ref, out_ref, q0, q1, k, v, g0, g1, result, dk, dv
-):
-    sort_blocks(place_ref, packed_ref, (q0, q1, k, v), block)
-    sort_blocks(place_ref, grad_ref, (g0, g1), block)
-    length = packed_ref.shape[0]
-    tile = min(256, length)
-    scale = 1.0 / math.sqrt(HEAD_DIM)
-    dk[...] = jnp.zeros_like(dk)
-    dv[...] = jnp.zeros_like(dv)
-    for first in range(0, length, tile):
-        top = first + tile
-        parts = []
-        for q, g in ((q0, g0), (q1, g1)):
-            query_rows = q[first:top, :]
-            grad_rows = g[first:top, :]
-            soft = softmax_parts(query_rows, k[:top, :], first)
-            grad_soft = product_back(grad_rows, v[:top, :])
-            delta = jnp.sum(soft * grad_soft, axis=-1, keepdims=True)
-            grad_scores = (soft * (grad_soft - delta)).astype(jnp.bfloat16)
-            parts.append(product(grad_scores, k[:top, :]) * scale)
-            dk[:top, :] += product_rows(grad_scores, query_rows) * scale
-            dv[:top, :] += product_rows(soft.astype(jnp.bfloat16), grad_rows)
-        result[first:top, :] = jnp.concatenate(parts, axis=-1)
-    for slot in range(length // block):
-        place = pl.multiple_of(place_ref[slot * block], block)
-        span = pl.ds(place, block)
-        out_ref[pl.ds(slot * block, block), :] = jnp.concatenate(
-            [result[span, :], dk[span, :], dv[span, :]], axis=-1
-        ).astype(jnp.bfloat16)
-
-
 def vmem():
     return pl.BlockSpec(memory_space=pltpu.VMEM)
 
 
-def attention_calls(length, block):
-    wide = 4 * HEAD_DIM
+def attention_call(length, block):
     pair = 2 * HEAD_DIM
     half = [pltpu.VMEM((length, HEAD_DIM), jnp.bfloat16)]
-    full = [pltpu.VMEM((length, HEAD_DIM), jnp.float32)]
     params = pltpu.CompilerParams(vmem_limit_bytes=48 * 2**20)
     places = pl.BlockSpec(memory_space=pltpu.SMEM)
     forward = pl.pallas_call(
@@ -276,16 +233,7 @@
         compiler_params=params,
         name="attention_forward",
     )
-    backward = pl.pallas_call(
-        functools.partial(attention_backward_kernel, block),
-        out_shape=jax.ShapeDtypeStruct((length, wide), jnp.bfloat16),
-        in_specs=[places, vmem(), vmem()],
-        out_specs=vmem(),
-        scratch_shapes=half * 6 + [pltpu.VMEM((length, pair), jnp.float32)] + full * 2,
-        compiler_params=params,
-        name="attention_backward",
-    )
-    return forward, backward
+    return forward
 
 
 def peer(ctx_index):
@@ -334,6 +282,771 @@
         compiler_params=pltpu.CompilerParams(collective_id=key, has_side_effects=True),
         name=f"exchange_{key}",
     )(values)
+
+
+SPINE_ROWS = 48
+LINE_ROWS = 64
+ROUND_ROWS = 2 * SPINE_ROWS + LINE_ROWS
+LEAD = 2
+RING = 12
+TILE = 128
+PAIR = (HEADS // KV_HEADS) * HEAD_DIM
+WIDE = PAIR + 2 * HEAD_DIM
+
+
+def near_fsdp(index):
+    return dict(device_id={"fsdp": index}, device_id_type=pl.DeviceIdType.MESH)
+
+
+def rows_at(start, count):
+    return pl.ds(pl.multiple_of(start, 16), count)
+
+
+class Place:
+    def __init__(self):
+        self.ctx = lax.axis_index("ctx")
+        self.row = lax.axis_index("fsdp")
+        self.chip, self.core = lax.div(self.row, 2), lax.rem(self.row, 2)
+        self.partner = 2 * self.chip + 1 - self.core
+        self.across = 2 * (1 - self.chip) + self.core
+        self.corner = 2 * (1 - self.chip) + 1 - self.core
+
+    def greet(self):
+        barrier = pltpu.get_barrier_semaphore()
+        for step in range(1, 4):
+            pl.semaphore_signal(barrier, inc=1, **near_fsdp(lax.rem(self.row + step, 4)))
+        for step in range(1, 8):
+            pl.semaphore_signal(barrier, inc=1, **peer(lax.rem(self.ctx + step, 8)))
+        pl.semaphore_wait(barrier, 10)
+
+
+class Fold:
+    def __init__(self, place, part, near, send, far, send_sem, recv_sem):
+        self.place, self.part, self.near, self.send, self.far = place, part, near, send, far
+        self.send_sem, self.recv_sem = send_sem, recv_sem
+
+    def partner_copy(self, chip):
+        block = 2 * chip + 1 - self.place.core
+        return pltpu.make_async_remote_copy(
+            src_ref=self.part.at[rows_at(block * TILE, TILE)],
+            dst_ref=self.near.at[chip],
+            send_sem=self.send_sem.at[chip],
+            recv_sem=self.recv_sem.at[chip],
+            **near_fsdp(self.place.partner),
+        )
+
+    def across_copy(self):
+        return pltpu.make_async_remote_copy(
+            src_ref=self.send,
+            dst_ref=self.far,
+            send_sem=self.send_sem.at[2],
+            recv_sem=self.recv_sem.at[2],
+            **near_fsdp(self.place.across),
+        )
+
+    def start(self):
+        self.partner_copy(1 - self.place.chip).start()
+        self.partner_copy(self.place.chip).start()
+
+    def relay(self):
+        there = 1 - self.place.chip
+        self.partner_copy(there).wait_recv()
+        base = self.place.across * TILE
+
+        @pl.loop(0, TILE // 32)
+        def _(piece):
+            mine = self.part[rows_at(base + piece * 32, 32), :].astype(jnp.float32)
+            span = rows_at(piece * 32, 32)
+            self.send[span, :] = (
+                mine + self.near[there, span, :].astype(jnp.float32)
+            ).astype(jnp.bfloat16)
+
+        self.across_copy().start()
+
+    def arrive(self):
+        self.partner_copy(self.place.chip).wait_recv()
+        copy = self.across_copy()
+        copy.wait_recv()
+        copy.wait_send()
+        self.partner_copy(0).wait_send()
+        self.partner_copy(1).wait_send()
+
+    def rows(self, start, count):
+        mine = self.part[rows_at(self.place.row * TILE + start, count), :].astype(jnp.float32)
+        span = rows_at(start, count)
+        near = self.near[self.place.chip, span, :].astype(jnp.float32)
+        return mine + near + self.far[span, :].astype(jnp.float32)
+
+
+class Gather:
+    def __init__(self, place, full, send_sem, recv_sem):
+        self.place, self.full, self.send_sem, self.recv_sem = place, full, send_sem, recv_sem
+
+    def copy(self, block, target, key):
+        span = rows_at(block * TILE, TILE)
+        return pltpu.make_async_remote_copy(
+            src_ref=self.full.at[span],
+            dst_ref=self.full.at[span],
+            send_sem=self.send_sem.at[key],
+            recv_sem=self.recv_sem.at[key],
+            **near_fsdp(target),
+        )
+
+    def start(self):
+        self.copy(self.place.row, self.place.across, 1).start()
+        self.copy(self.place.row, self.place.partner, 0).start()
+
+    def relay(self):
+        self.copy(self.place.across, self.place.across, 1).wait_recv()
+        self.copy(self.place.across, self.place.partner, 2).start()
+
+    def arrive(self):
+        self.copy(self.place.partner, self.place.partner, 0).wait_recv()
+        self.copy(self.place.corner, self.place.partner, 2).wait_recv()
+        self.copy(self.place.row, self.place.across, 1).wait_send()
+        self.copy(self.place.row, self.place.partner, 0).wait_send()
+        self.copy(self.place.across, self.place.partner, 2).wait_send()
+
+
+class Swap:
+    def __init__(self, place, source, target, send_sem, recv_sem):
+        self.place, self.source, self.target = place, source, target
+        self.send_sem, self.recv_sem = send_sem, recv_sem
+
+    def copy(self, step):
+        other = lax.rem(self.place.ctx + step, 8)
+        return pltpu.make_async_remote_copy(
+            src_ref=self.source.at[self.span(other)],
+            dst_ref=self.target.at[self.span(self.place.ctx)],
+            send_sem=self.send_sem.at[step],
+            recv_sem=self.recv_sem.at[step],
+            **peer(other),
+        )
+
+    def span(self, index):
+        blocks = self.source.shape[0] // 8
+        return pl.ds(index * blocks, blocks)
+
+    def start(self):
+        for step in range(1, 8):
+            self.copy(step).start()
+        own = self.span(self.place.ctx)
+        self.target[own] = self.source[own]
+
+    def arrive(self):
+        for step in range(1, 8):
+            self.copy(step).wait()
+
+
+class Spread:
+    def __init__(self, slots, index, count, device, send_sem, recv_sem):
+        self.slots, self.index, self.count, self.device = slots, index, count, device
+        self.send_sem, self.recv_sem = send_sem, recv_sem
+
+    def copy(self, step):
+        return pltpu.make_async_remote_copy(
+            src_ref=self.slots.at[self.index],
+            dst_ref=self.slots.at[self.index],
+            send_sem=self.send_sem.at[step],
+            recv_sem=self.recv_sem.at[step],
+            **self.device(lax.rem(self.index + step, self.count)),
+        )
+
+    def start(self):
+        for step in range(1, self.count):
+            self.copy(step).start()
+
+    def total(self):
+        for step in range(1, self.count):
+            self.copy(step).wait()
+        result = self.slots[0]
+        for step in range(1, self.count):
+            result += self.slots[step]
+        return result
+
+
+class Tree:
+    def __init__(self, place, own, out_ref, index, line, box, sems, leaf_back):
+        me = place.ctx
+        depth, side = lax.div(me, 2), lax.rem(me, 2)
+        other_side = me + 1 - 2 * side
+        self.own, self.out, self.box, self.index, self.line = own, out_ref, box, index, line
+        self.up, self.got, self.down, self.back = sems
+        self.leaf_back = leaf_back
+        if line:
+            center = lax.rem(index, 4)
+            count = LINE_ROWS
+            start = index * ROUND_ROWS + 2 * SPINE_ROWS
+            root_side = lax.rem(index, 2)
+            on_cross = depth == center
+            self.root = jnp.logical_and(on_cross, side == root_side)
+            has_side = self.root
+            to_side = jnp.logical_and(on_cross, side != root_side)
+            reach = jnp.maximum(center, 3 - center)
+            away = jnp.abs(depth - center)
+            crossed = jnp.where(side == root_side, 0, 1)
+            self.rise_age = reach - away + jnp.where(self.root, 1, 0)
+            self.fall_age = reach + 1 + away + crossed
+        else:
+            center = 1 + side
+            count = SPINE_ROWS
+            start = index * ROUND_ROWS + side * SPINE_ROWS
+            self.root = depth == center
+            has_side = None
+        self.count = count
+        self.start = start
+        self.slot = lax.rem(index, RING)
+        self.rows = rows_at(start, count)
+        self.children = (
+            (jnp.logical_and(depth > 0, depth <= center), me - 2, 0),
+            (jnp.logical_and(depth < 3, depth >= center), me + 2, 1),
+            (has_side, other_side, 2),
+        )
+        parent = jnp.where(depth < center, me + 2, me - 2)
+        slot = jnp.where(depth < center, 0, 1)
+        if line:
+            parent = jnp.where(to_side, other_side, parent)
+            slot = jnp.where(to_side, 2, slot)
+        self.parent = jnp.where(self.root, other_side, parent)
+        self.parent_slot = jnp.where(self.root, 2, slot)
+
+    def boxed(self, slot):
+        return self.box.at[slot, rows_at(self.slot * self.count, self.count)]
+
+    def up_copy(self, target, slot):
+        return pltpu.make_async_remote_copy(
+            src_ref=self.own.at[self.rows],
+            dst_ref=self.boxed(slot),
+            send_sem=self.up.at[self.slot],
+            recv_sem=self.got.at[slot, self.slot],
+            **peer(target),
+        )
+
+    def down_copy(self, child, slot, source):
+        back = self.back if slot < 2 or self.line else self.leaf_back
+        return pltpu.make_async_remote_copy(
+            src_ref=source.at[self.rows],
+            dst_ref=self.out.at[self.rows],
+            send_sem=self.down.at[slot, self.slot],
+            recv_sem=back.at[self.slot],
+            **peer(child),
+        )
+
+    def each_child(self, action):
+        for present, child, slot in self.children:
+            if present is None:
+                action(child, slot)
+            else:
+                pl.when(present)(functools.partial(action, child, slot))
+
+    def keep(self):
+        return pltpu.make_async_copy(
+            self.own.at[self.rows], self.out.at[self.rows], self.up.at[self.slot]
+        )
+
+    def rise(self):
+        self.each_child(lambda child, slot: self.up_copy(child, slot).wait_recv())
+        base = self.slot * self.count
+        for piece in range(0, self.count, 16):
+            span = rows_at(self.start + piece, 16)
+            total = self.own[span, :].astype(jnp.float32)
+            for present, _, slot in self.children:
+                part = self.box[slot, rows_at(base + piece, 16), :].astype(jnp.float32)
+                total += part if present is None else jnp.where(present, part, 0.0)
+            self.own[span, :] = total.astype(jnp.bfloat16)
+
+        @pl.when(jnp.logical_not(self.root))
+        def _():
+            self.up_copy(self.parent, self.parent_slot).start()
+
+        @pl.when(self.root)
+        def _():
+            self.keep().start()
+            self.each_child(lambda child, slot: self.down_copy(child, slot, self.own).start())
+
+    def fall(self):
+        @pl.when(jnp.logical_not(self.root))
+        def _():
+            self.down_copy(self.parent, 0, self.out).wait_recv()
+            self.each_child(lambda child, slot: self.down_copy(child, slot, self.out).start())
+
+    def finish(self):
+        @pl.when(jnp.logical_not(self.root))
+        def _():
+            self.up_copy(self.parent, self.parent_slot).wait_send()
+
+        @pl.when(self.root)
+        def _():
+            self.keep().wait()
+
+        self.each_child(lambda child, slot: self.down_copy(child, slot, self.out).wait_send())
+
+
+def softmax_parts(query_rows, key_rows, first_row):
+    scores = product_back(query_rows, key_rows) * (1.0 / math.sqrt(HEAD_DIM))
+    rows = lax.broadcasted_iota(jnp.int32, scores.shape, 0) + first_row
+    columns = lax.broadcasted_iota(jnp.int32, scores.shape, 1)
+    scores = jnp.where(columns <= rows, scores, -1e30)
+    spread = jnp.exp(scores - jnp.max(scores, axis=-1, keepdims=True))
+    return spread * (1.0 / jnp.sum(spread, axis=-1, keepdims=True))
+
+
+def sort_blocks(slot_ref, source, targets):
+    block_total, block, _ = source.shape
+    for index in range(block_total):
+        rows = source[slot_ref[index]]
+        start = 0
+        for target in targets:
+            width = target.shape[-1]
+            target[index * block : (index + 1) * block, :] = rows[:, start : start + width]
+            start += width
+
+
+def norm_back_rows(values, grad_unit):
+    scale = rms_scale(values)
+    unit = values * scale
+    return unit, lambda grad: norm_back(scale, unit, grad)
+
+
+def backward_kernel(
+    rounds,
+    block,
+    order_ref,
+    gate_ref,
+    up_ref,
+    down_ref,
+    part_ref,
+    hidden_ref,
+    cotangent_ref,
+    input_ref,
+    gain_ref,
+    output_weight_ref,
+    attended_ref,
+    packed_ref,
+    normed_ref,
+    cosine_ref,
+    sine_ref,
+    half_swap_ref,
+    weight_ref,
+    out_ref,
+    gain_out_ref,
+    input_grad_ref,
+    own,
+    spine_in,
+    line_in,
+    part,
+    hidden,
+    cotangent,
+    inputs,
+    output_weight,
+    attended,
+    packed,
+    normed,
+    cosine,
+    sine,
+    half_swap,
+    weight,
+    near,
+    send,
+    far,
+    branch,
+    grad_hidden,
+    gain_part,
+    heads_out,
+    heads_in,
+    q0,
+    q1,
+    k,
+    v,
+    g0,
+    g1,
+    result,
+    dk,
+    dv,
+    packed_out,
+    packed_in,
+    turned,
+    gain_near,
+    gain_far,
+    fetch_sem,
+    spine_up,
+    spine_got,
+    spine_down,
+    spine_back,
+    leaf_up,
+    leaf_back,
+    line_up,
+    line_got,
+    line_down,
+    line_back,
+    fold_send,
+    fold_recv,
+    gather_send,
+    gather_recv,
+    swap_send,
+    swap_recv,
+    near_send,
+    near_recv,
+    far_send,
+    far_recv,
+):
+    place = Place()
+    me = place.ctx
+    depth, side = lax.div(me, 2), lax.rem(me, 2)
+    other_side = me + 1 - 2 * side
+    hidden_units = gate_ref.shape[0]
+    base = 3 * hidden_units
+    spare = rounds * ROUND_ROWS - base - 3 * WIDE
+    length = q0.shape[0]
+    halves = TILE // block
+    tile = min(256, length)
+    tiles = length // tile
+    scale = 1.0 / math.sqrt(HEAD_DIM)
+
+    fetches = {}
+    for key, (source, target) in enumerate(
+        (
+            (part_ref, part),
+            (gate_ref, own.at[pl.ds(0, hidden_units)]),
+            (up_ref, own.at[pl.ds(hidden_units, hidden_units)]),
+            (hidden_ref, hidden),
+            (cotangent_ref, cotangent),
+            (output_weight_ref, output_weight),
+            (packed_ref, packed),
+            (attended_ref, attended),
+            (down_ref, own.at[pl.ds(2 * hidden_units, hidden_units)]),
+            (normed_ref, normed),
+            (cosine_ref, cosine),
+            (sine_ref, sine),
+            (half_swap_ref, half_swap),
+            (weight_ref, weight),
+            (input_ref, inputs),
+        )
+    ):
+        fetches[id(source)] = pltpu.make_async_copy(source, target, fetch_sem.at[key])
+
+    def fetch(*sources):
+        for source in sources:
+            fetches[id(source)].wait()
+
+    for copy in fetches.values():
+        copy.start()
+    if spare:
+        own[base + 3 * WIDE :, :] = jnp.zeros((spare, own.shape[1]), own.dtype)
+    place.greet()
+    fetch(part_ref)
+    fold_two = Fold(place, part, near.at[0], send.at[0], far.at[0], fold_send.at[0], fold_recv.at[0])
+    fold_one = Fold(place, part, near.at[1], send.at[1], far.at[1], fold_send.at[1], fold_recv.at[1])
+    gather = Gather(place, branch, gather_send, gather_recv)
+    swap_heads = Swap(place, heads_out, heads_in, swap_send.at[0], swap_recv.at[0])
+    swap_packed = Swap(place, packed_out, packed_in, swap_send.at[1], swap_recv.at[1])
+    spread_near = Spread(gain_near, place.row, 4, near_fsdp, near_send, near_recv)
+    spread_far = Spread(gain_far, me, 8, peer, far_send, far_recv)
+    fold_two.start()
+    fetch(gate_ref, up_ref, down_ref)
+
+    spine_sems = (spine_up, spine_got, spine_down, spine_back)
+    line_sems = (line_up, line_got, line_down, line_back)
+
+    def spine(index):
+        return Tree(place, own, out_ref, index, False, spine_in, spine_sems, leaf_back)
+
+    def line(index):
+        return Tree(place, own, out_ref, index, True, line_in, line_sems, None)
+
+    def leaf_rows(index):
+        return rows_at(index * ROUND_ROWS + (1 - side) * SPINE_ROWS, SPINE_ROWS)
+
+    def leaf_copy(index):
+        slot = lax.rem(index, RING)
+        return pltpu.make_async_remote_copy(
+            src_ref=own.at[leaf_rows(index)],
+            dst_ref=spine_in.at[2, rows_at(slot * SPINE_ROWS, SPINE_ROWS)],
+            send_sem=leaf_up.at[slot],
+            recv_sem=spine_got.at[2, slot],
+            **peer(other_side),
+        )
+
+    def leaf_result(index):
+        slot = lax.rem(index, RING)
+        return pltpu.make_async_remote_copy(
+            src_ref=own.at[leaf_rows(index)],
+            dst_ref=out_ref.at[leaf_rows(index)],
+            send_sem=leaf_up.at[slot],
+            recv_sem=leaf_back.at[slot],
+            **peer(other_side),
+        )
+
+    def stage_norm_two():
+        fetch(hidden_ref, cotangent_ref)
+        fold_two.arrive()
+        gain_part[...] = jnp.zeros_like(gain_part)
+
+        @pl.loop(0, TILE // 16)
+        def _(piece):
+            span = rows_at(piece * 16, 16)
+            grad = fold_two.rows(piece * 16, 16)
+            unit, back = norm_back_rows(hidden[span, :], None)
+            gain_part[1] += (grad * unit).reshape(2, 8, -1).sum(axis=0)
+            total = cotangent[span, :].astype(jnp.float32) + back(grad * gain_ref[1:2, :])
+            grad_hidden[span, :] = total
+            branch[rows_at(place.row * TILE + piece * 16, 16), :] = total.astype(jnp.bfloat16)
+
+        gather.start()
+
+    def stage_heads():
+        fetch(output_weight_ref)
+        gather.arrive()
+
+        @pl.loop(0, 4)
+        def _(sequence):
+            rows = branch[rows_at(sequence * TILE, TILE), :]
+            grads = product_back(rows, output_weight[...]).astype(jnp.bfloat16)
+            for head in range(2):
+                heads_out[pl.ds((2 * sequence + head) * halves, halves)] = grads[
+                    :, head * PAIR : (head + 1) * PAIR
+                ].reshape(halves, block, PAIR)
+
+        swap_heads.start()
+
+    def stage_sort():
+        fetch(packed_ref)
+        sort_blocks(order_ref, packed, (q0, q1, k, v))
+
+    def stage_output_grad():
+        fetch(attended_ref)
+        for first in range(0, own.shape[1], 512):
+            columns = slice(first, first + 512)
+            own[base + 2 * WIDE :base + 3 * WIDE, columns] = product_rows(
+                attended[...], branch[:, columns]
+            ).astype(jnp.bfloat16)
+
+    def stage_sort_grads():
+        swap_heads.arrive()
+        sort_blocks(order_ref, heads_in, (g0, g1))
+        dk[...] = jnp.zeros_like(dk)
+        dv[...] = jnp.zeros_like(dv)
+
+    def stage_attention(index):
+        first, top = index * tile, (index + 1) * tile
+        parts = []
+        for q, g in ((q0, g0), (q1, g1)):
+            query_rows = q[first:top, :]
+            grad_rows = g[first:top, :]
+            soft = softmax_parts(query_rows, k[:top, :], first)
+            grad_soft = product_back(grad_rows, v[:top, :])
+            delta = jnp.sum(soft * grad_soft, axis=-1, keepdims=True)
+            grad_scores = (soft * (grad_soft - delta)).astype(jnp.bfloat16)
+            parts.append(product(grad_scores, k[:top, :]) * scale)
+            key_term = product_rows(grad_scores, query_rows) * scale
+            value_term = product_rows(soft.astype(jnp.bfloat16), grad_rows)
+            dk[: top // block] += key_term.reshape(-1, block, HEAD_DIM)
+            dv[: top // block] += value_term.reshape(-1, block, HEAD_DIM)
+        result[first // block : top // block] = jnp.concatenate(parts, axis=-1).reshape(
+            -1, block, PAIR
+        )
+
+    def stage_unsort():
+        for slot in range(length // block):
+            spot = order_ref[length // block + slot]
+            packed_out[slot] = jnp.concatenate(
+                [result[spot], dk[spot], dv[spot]], axis=-1
+            ).astype(jnp.bfloat16)
+        swap_packed.start()
+
+    def stage_turn():
+        fetch(cosine_ref, sine_ref, half_swap_ref, weight_ref)
+        swap_packed.arrive()
+
+        @pl.loop(0, 4)
+        def _(sequence):
+            span = rows_at(sequence * TILE, TILE)
+            total = None
+            for head in range(2):
+                grads = packed_in[pl.ds((2 * sequence + head) * halves, halves)]
+                grads = grads.reshape(TILE, WIDE)
+                swapped = product(grads, half_swap[...])
+                low = (
+                    grads.astype(jnp.float32) * cosine[span, :] + swapped * sine[span, :]
+                ).astype(jnp.bfloat16)
+                turned[head, span, :] = low
+                term = product(low, weight[head])
+                total = term if total is None else total + term
+            part[span, :] = total.astype(jnp.bfloat16)
+
+        fold_one.start()
+
+    def stage_projection_grads(head):
+        if head == 0:
+            fetch(normed_ref)
+        query_base = base + head * PAIR
+        key_base = base + WIDE + head * HEAD_DIM
+        value_base = key_base + 2 * HEAD_DIM
+        for first in range(0, own.shape[1], 512):
+            columns = slice(first, first + 512)
+            grads = product_rows(turned[head], normed[:, columns]).astype(jnp.bfloat16)
+            own[query_base : query_base + PAIR, columns] = grads[:PAIR]
+            own[key_base : key_base + HEAD_DIM, columns] = grads[PAIR : PAIR + HEAD_DIM]
+            own[value_base : value_base + HEAD_DIM, columns] = grads[PAIR + HEAD_DIM :]
+
+    def stage_norm_one():
+        fetch(input_ref)
+        fold_one.arrive()
+
+        @pl.loop(0, TILE // 16)
+        def _(piece):
+            span = rows_at(piece * 16, 16)
+            grad = fold_one.rows(piece * 16, 16)
+            unit, back = norm_back_rows(inputs[span, :].astype(jnp.float32), None)
+            gain_part[0] += (grad * unit).reshape(2, 8, -1).sum(axis=0)
+            input_grad_ref[span, :] = grad_hidden[span, :] + back(grad * gain_ref[0:1, :])
+
+        gain_near[place.row] = jnp.sum(gain_part[...], axis=1)
+        spread_near.start()
+
+    def stage_gain():
+        gain_far[me] = spread_near.total()
+        spread_far.start()
+
+    stages = [
+        (0, fold_two.relay),
+        (0, stage_sort),
+        (2, stage_norm_two),
+        (3, gather.relay),
+        (4, stage_heads),
+        (5, stage_output_grad),
+        (6, stage_sort_grads),
+    ]
+    stages += [(6 + index, functools.partial(stage_attention, index)) for index in range(tiles)]
+    now = 6 + tiles - 1
+    stages += [
+        (now, stage_unsort),
+        (now + 2, stage_turn),
+        (now + 3, fold_one.relay),
+        (now + 3, functools.partial(stage_projection_grads, 0)),
+        (now + 4, functools.partial(stage_projection_grads, 1)),
+        (now + 5, stage_norm_one),
+        (now + 6, stage_gain),
+    ]
+    needed = base // ROUND_ROWS - LEAD
+    assert now + 4 < needed
+
+    for index in range(LEAD):
+        leaf_copy(index).start()
+
+    def valid(index):
+        return jnp.logical_and(index >= 0, index < rounds)
+
+    @pl.loop(0, rounds + RING)
+    def _(now):
+        far_side = jnp.abs(depth - 2 + side)
+        off_center = jnp.abs(depth - 1 - side)
+        done = now - RING + 1
+        for tree in (spine(done), line(done)):
+            pl.when(valid(done))(tree.finish)
+
+        @pl.when(now + LEAD < rounds)
+        def _():
+            leaf_copy(now + LEAD).start()
+
+        rising = spine(now - 3 + off_center)
+        pl.when(valid(rising.index))(rising.rise)
+
+        @pl.loop(0, 5)
+        def _(age):
+            tree = line(now - age)
+            pl.when(jnp.logical_and(valid(tree.index), tree.rise_age == age))(tree.rise)
+
+        falling = spine(now - 3 - off_center)
+        pl.when(valid(falling.index))(falling.fall)
+
+        @pl.loop(4, 9)
+        def _(age):
+            tree = line(now - age)
+            pl.when(jnp.logical_and(valid(tree.index), tree.fall_age == age))(tree.fall)
+
+        leaf_fall = now - 4 - far_side
+
+        @pl.when(valid(leaf_fall))
+        def _():
+            leaf_result(leaf_fall).wait_recv()
+            leaf_copy(leaf_fall).wait_send()
+
+        for when, stage in stages:
+            pl.when(now == when)(stage)
+
+    gain_out_ref[...] = spread_far.total()
+
+
+def backward(order, grads, part, hidden, cotangent, inputs, gains, output_weight, attended,
+             packed, normed, cosine, sine, half_swap, weight, block, key):
+    width = hidden.shape[1]
+    rows = 3 * grads[0].shape[0] + 3 * WIDE
+    rounds = -(-rows // ROUND_ROWS)
+    length = packed.shape[0]
+    packed = packed.reshape(-1, block, WIDE)
+    dma = pltpu.SemaphoreType.DMA
+    low, full = jnp.bfloat16, jnp.float32
+    any_spec = pl.BlockSpec(memory_space=pl.ANY)
+    operands = (
+        order, *grads, part, hidden, cotangent, inputs, gains, output_weight, attended,
+        packed, normed, cosine, sine, half_swap, weight,
+    )
+
+    def like(array):
+        return pltpu.VMEM(array.shape, array.dtype)
+
+    return pl.pallas_call(
+        functools.partial(backward_kernel, rounds, block),
+        out_shape=(
+            jax.ShapeDtypeStruct((rounds * ROUND_ROWS, width), low),
+            jax.ShapeDtypeStruct((2, width), full),
+            jax.ShapeDtypeStruct((TILE, width), full),
+        ),
+        in_specs=[pl.BlockSpec(memory_space=pltpu.SMEM)]
+        + [any_spec] * 7
+        + [vmem()]
+        + [any_spec] * 8,
+        out_specs=(any_spec, vmem(), vmem()),
+        scratch_shapes=[
+            pltpu.VMEM((rounds * ROUND_ROWS, width), low),
+            pltpu.VMEM((3, RING * SPINE_ROWS, width), low),
+            pltpu.VMEM((3, RING * LINE_ROWS, width), low),
+            like(part), like(hidden), like(cotangent), like(inputs), like(output_weight),
+            like(attended), like(packed), like(normed), like(cosine), like(sine),
+            like(half_swap), like(weight),
+            pltpu.VMEM((2, 2, TILE, width), low),
+            pltpu.VMEM((2, TILE, width), low),
+            pltpu.VMEM((2, TILE, width), low),
+            pltpu.VMEM((4 * TILE, width), low),
+            pltpu.VMEM((TILE, width), full),
+            pltpu.VMEM((2, 8, width), full),
+            pltpu.VMEM((length // block, block, PAIR), low),
+            pltpu.VMEM((length // block, block, PAIR), low),
+        ]
+        + [pltpu.VMEM((length, HEAD_DIM), low)] * 6
+        + [pltpu.VMEM((length // block, block, PAIR), full)]
+        + [pltpu.VMEM((length // block, block, HEAD_DIM), full)] * 2
+        + [
+            pltpu.VMEM((length // block, block, WIDE), low),
+            pltpu.VMEM((length // block, block, WIDE), low),
+            pltpu.VMEM((2, 4 * TILE, WIDE), low),
+            pltpu.VMEM((4, 2, width), full),
+            pltpu.VMEM((8, 2, width), full),
+            dma((15,)),
+            dma((RING,)), dma((3, RING)), dma((3, RING)), dma((RING,)),
+            dma((RING,)), dma((RING,)),
+            dma((RING,)), dma((3, RING)), dma((3, RING)), dma((RING,)),
+            dma((2, 3)), dma((2, 3)),
+            dma((3,)), dma((3,)),
+            dma((2, 8)), dma((2, 8)),
+            dma((4,)), dma((4,)), dma((8,)), dma((8,)),
+        ],
+        compiler_params=pltpu.CompilerParams(
+            collective_id=key, has_side_effects=True, vmem_limit_bytes=63 * 2**20
+        ),
+        name="backward",
+    )(*operands)
 
 
 def gather_rows(values):
@@ -413,7 +1126,7 @@
         head_places = lax.dynamic_index_in_dim(key_places, own_sequence, 0, keepdims=False)
         length = head_places.shape[0]
         block = row_count // 2
-        forward_call, backward_call = attention_calls(length, block)
+        forward_call = attention_call(length, block)
         packed = exchange(
             to_heads([flat_query, key_low.reshape(total_rows, kv_width), value_low]), 1
         ).reshape(length, -1)
@@ -460,9 +1173,57 @@
         grad_mixed * upward * sigmoid_gate * (1.0 + gate_values * (1.0 - sigmoid_gate))
     ).astype(jnp.bfloat16)
     grad_up_low = (grad_mixed * activated).astype(jnp.bfloat16)
-    grad_normed_two = scatter_rows(
+    grad_unit_part = (
         product(grad_gate_low, gate_weight) + product(grad_up_low, up_weight)
-    )
+    ).astype(jnp.bfloat16)
+    if by_head:
+        starts = head_places.reshape(-1, block)[:, 0] // block
+        slots = jnp.arange(length // block, dtype=jnp.int32)
+        found = jnp.where(starts[None, :] == slots[:, None], slots[None, :], 0)
+        order = jnp.concatenate([jnp.sum(found, axis=1), starts]).astype(jnp.int32)
+        half = HEAD_DIM // 2
+        flat_cosine, flat_sine = cosine[:, 0, :], sine[:, 0, :]
+        ones = jnp.ones((total_rows, HEAD_DIM), jnp.float32)
+        wide_cosine = jnp.concatenate([flat_cosine] * (2 * groups + 2) + [ones], axis=1)
+        wide_sine = jnp.concatenate(
+            [flat_sine, -flat_sine] * (groups + 1) + [jnp.zeros_like(ones)], axis=1
+        )
+        lanes = jnp.arange(WIDE, dtype=jnp.int32)
+        partner_lane = lanes + jnp.where(lanes % HEAD_DIM < half, half, -half)
+        half_swap = jnp.logical_and(
+            lanes[:, None] == partner_lane[None, :], lanes[None, :] < PAIR + HEAD_DIM
+        ).astype(jnp.bfloat16)
+        width = inputs.shape[1]
+        weight = jnp.concatenate(
+            [
+                query_weight.reshape(kv_heads, pair, width),
+                key_weight.reshape(kv_heads, HEAD_DIM, width),
+                value_weight.reshape(kv_heads, HEAD_DIM, width),
+            ],
+            axis=1,
+        )
+        layer_output = (hidden_state + scatter_rows(product(mixed_hidden, down_weight))).astype(
+            jnp.bfloat16
+        )
+        ff_grads = (
+            product_rows(grad_gate_low, normed_two).astype(jnp.bfloat16),
+            product_rows(grad_up_low, normed_two).astype(jnp.bfloat16),
+            grad_down.astype(jnp.bfloat16),
+        )
+        summed, gain_sums, input_grad = backward(
+            order, ff_grads, grad_unit_part, hidden_state, cotangent, inputs,
+            jnp.stack([gain_one, gain_two]), output_weight, attended_low, packed, normed_one,
+            wide_cosine, wide_sine, half_swap, weight, block, 5,
+        )
+        parts, start = [], 0
+        for grad in (gate_weight, up_weight, down_weight, query_weight, key_weight, value_weight,
+                     output_weight):
+            parts.append(summed[start : start + grad.shape[0]].astype(jnp.float32))
+            start += grad.shape[0]
+        return (
+            layer_output, input_grad, gain_sums[0], *parts[3:], gain_sums[1], *parts[:3],
+        )
+    grad_normed_two = scatter_rows(grad_unit_part)
     gain_two_grad = jnp.sum(grad_normed_two * unit_two, axis=0)
     grad_hidden = grad_out + norm_back(scale_two, unit_two, grad_normed_two * gain_two)
     branch_rows = gather_rows(grad_hidden.astype(jnp.bfloat16))
@@ -473,23 +1234,12 @@
     grad_up = product_rows(grad_up_low, normed_two)
     grad_output = product_rows(attended_low, branch_rows)
     grad_attended = product_back(branch_rows, output_weight).astype(jnp.bfloat16)
-    if by_head:
-        grad_heads = exchange(to_heads([grad_attended]), 3).reshape(length, pair)
-        packed_grads = exchange(
-            backward_call(head_places, packed, grad_heads).reshape(ctx_size, row_count, -1), 4
-        )
-        grad_query_rot, grad_key_own, grad_value_low = from_heads(
-            packed_grads, (pair, HEAD_DIM, HEAD_DIM)
-        )
-        grad_query_rot = grad_query_rot.astype(jnp.float32)
-        grad_key_own = grad_key_own.astype(jnp.float32)
-    else:
-        grad_attended = grad_attended.reshape(seq_count, row_count, kv_heads, groups, HEAD_DIM)
-        grad_query_rot, grad_key_all, grad_value_all = attend_backward(
-            query_grouped, query_places, key_grid, value_grid, key_places, log_total, grad_attended
-        )
-        grad_key_own = collect(grad_key_all).astype(jnp.float32)
-        grad_value_low = collect(grad_value_all)
+    grad_attended = grad_attended.reshape(seq_count, row_count, kv_heads, groups, HEAD_DIM)
+    grad_query_rot, grad_key_all, grad_value_all = attend_backward(
+        query_grouped, query_places, key_grid, value_grid, key_places, log_total, grad_attended
+    )
+    grad_key_own = collect(grad_key_all).astype(jnp.float32)
+    grad_value_low = collect(grad_value_all)
     grad_query_low = (
         rotate_back(grad_query_rot.reshape(total_rows, query_heads, HEAD_DIM), cosine, sine)
         .reshape(total_rows, query_heads * HEAD_DIM)
@@ -514,22 +1264,21 @@
     gain_one_grad = jnp.sum(grad_normed_one * own_unit, axis=0)
     input_grad = grad_hidden + norm_back(own(scale_one), own_unit, grad_normed_one * gain_one)
 
-    def ctx_sum(grad):
-        return lax.psum(grad.astype(jnp.bfloat16), "ctx").astype(jnp.float32)
-
+    grads = (grad_query, grad_key, grad_value, grad_output, grad_gate, grad_up, grad_down)
+    parts = [lax.psum(grad.astype(jnp.bfloat16), "ctx").astype(jnp.float32) for grad in grads]
     gain_sums = lax.psum(jnp.stack([gain_one_grad, gain_two_grad]), ("fsdp", "ctx"))
     return (
         layer_output,
         input_grad,
         gain_sums[0],
-        ctx_sum(grad_query),
-        ctx_sum(grad_key),
-        ctx_sum(grad_value),
-        ctx_sum(grad_output),
+        parts[0],
+        parts[1],
+        parts[2],
+        parts[3],
         gain_sums[1],
-        ctx_sum(grad_gate),
-        ctx_sum(grad_up),
-        ctx_sum(grad_down),
+        parts[4],
+        parts[5],
+        parts[6],
     )
 
 

time: 825 us -> 522 us (0.63)
  waiting for transfers between devices: 515 us -> 52.6 us
  Pallas kernels: 75.6 us -> 315 us
  blocking collectives: 72.9 us -> 33.1 us
  matrix products: 64.5 us -> 51.5 us
  other arithmetic: 44.9 us -> 33.2 us
  local copies, waits for them, and re-layouts: 27.7 us -> 16.4 us
    psum x1 -> x0, waiting for transfers between devices: 398 us -> none  [ctx_sum(): return lax.psum(grad.astype(jnp.bfloat16), 'ctx').astype(jnp.float32)]
    pallas_call x1, Pallas kernels: 8.21 us -> 280 us  [backward(): pl.pallas_call(functools.partial(backward_kernel, rounds, block), out_sha...]
    psum x1 -> x0, blocking collectives: 39.8 us -> none  [per_device(): lax.psum(jnp.stack([gain_one_grad, gain_two_grad]), ('fsdp', 'ctx'))]
    reduce_scatter x4 -> x2, waiting for transfers between devices: 65 us -> 30.4 us  [scatter_rows(): lax.psum_scatter(values.astype(jnp.bfloat16), 'fsdp', scatter_dimension=0...]
    pallas_call x4 -> x2, Pallas kernels: 61.8 us -> 28.8 us  [exchange(): pl.pallas_call(functools.partial(exchange_kernel, count), out_shape=jax.S...]
    all_gather x4 -> x3, waiting for transfers between devices: 50.9 us -> 21 us  [gather_rows(): return lax.all_gather(values, 'fsdp', axis=0, tiled=True)]
    dot_general x7 -> x3, matrix products: 19 us -> 10.5 us  [product_rows(): lax.dot_general(left, right, (((0,), (0,)), ((), ())), preferred_element_...]
    dot_general x7 -> x6, matrix products: 25.8 us -> 18.7 us  [product_back(): lax.dot_general(left, right, (((1,), (1,)), ((), ())), preferred_element_...]
  transfers between devices with their start and end apart: 9 -> 5, of which waited for: 7 -> 3; matrix products, arithmetic and copies ran while one was open for 5% -> 13% of each run, Pallas kernels for 0% -> 54%
where the time goes in v4:
time: 522 us; the launch traced here: 516 us
  Pallas kernels  315 us (60%)
  waiting for transfers between devices  52.6 us (10%)
  matrix products  51.5 us (10%)
  other arithmetic  33.2 us (6%)
  blocking collectives  33.1 us (6%)
  local copies, waits for them, and re-layouts  16.4 us (3%)
  between operations  14.4 us (3%)
    pallas_call x1, Pallas kernels, backward(): pl.pallas_call(functools.partial(backward_kernel, rounds, block), out_sha...  280 us
    reduce_scatter x2, waiting for transfers between devices, scatter_rows(): lax.psum_scatter(values.astype(jnp.bfloat16), 'fsdp', scatter_dimension=0...  30.4 us
    pallas_call x2, Pallas kernels, exchange(): pl.pallas_call(functools.partial(exchange_kernel, count), out_shape=jax.S...  28.8 us
    all_gather x1, blocking collectives, per_device(): key_places = lax.all_gather(query_places, 'ctx', axis=1, tiled=True)  26.9 us
    dot_general x4, matrix products, product(): return jnp.dot(left, right, preferred_element_type=jnp.float32)  22.3 us
    all_gather x3, waiting for transfers between devices, gather_rows(): return lax.all_gather(values, 'fsdp', axis=0, tiled=True)  21 us
    dot_general x6, matrix products, product_back(): lax.dot_general(left, right, (((1,), (1,)), ((), ())), preferred_element_...  18.7 us
    convert_element_type x3, other arithmetic, per_device(): parts.append(summed[start:start + grad.shape[0]].astype(jnp.float32))  16.8 us
  transfers between devices with their start and end apart: 5, of which 3 were waited for; matrix products, arithmetic and copies ran while one was open for 13% of the time, Pallas kernels for 54%

profile of v4, /device:TPU:0, one launch (start us, length us, event | category | flops | bytes accessed | tf_op | source)
XLA Modules:
  0.0 516.3 jit_solution(7054721525280069132)
XLA Ops:
  8.0 6.2 %all-gather = s32[4,1,128]{2,1,0:T(1,128)S(1)} all-gather(s32[1,1,128]{2,1,0:T(1,128)} %bitcast.78), channel_id=1, replica_groups=mesh['fsdp'=4,'ctx'=8] {'fsdp'}, dimensions={0}, use_global_device_ids=true | all-gather | bytes 2560 | tf_op jit(solution)/shard_map/all_gather | solution.py:1053
  16.1 26.9 %all_gather.16 = s32[4,1024]{1,0:T(4,128)S(1)} all-gather(s32[4,128]{1,0:T(4,128)S(1)} %bitcast.76), channel_id=1, replica_groups=mesh['fsdp'=4,'ctx'=8] {'ctx'}, dimensions={1}, use_global_device_ids=true | all-gather | bytes 18432 | tf_op jit(solution)/shard_map/all_gather | solution.py:1087
  44.3 1.9 fusion
  49.6 2.1 fusion.13
  54.6 12.4 %exchange_1.1 = bf16[8,128,384]{2,1,0:T(8,128)(2,1)} custom-call(bf16[8,128,384]{2,1,0:T(8,128)(2,1)} %bitcast.66), custom_call_target="tpu_custom_call" | custom-call | tf_op jit(solution)/shard_map/exchange_1/pallas_call | solution.py:272
  68.1 5.6 %attention_forward.1 = bf16[1024,192]{1,0:T(8,128)(2,1)S(1)} custom-call(s32[1024]{0:T(1024)S(1)} %bitcast.63, bf16[1024,384]{1,0:T(8,128)(2,1)S(1)} %bitcast.61), custom_call_target="tpu_custom_call" | custom-call | tf_op jit(solution)/shard_map/attention_forward/pallas_call | solution.py:1134
  74.5 16.4 %exchange_2.1 = bf16[8,128,192]{2,1,0:T(8,128)(2,1)} custom-call(bf16[8,128,192]{2,1,0:T(8,128)(2,1)} %bitcast.62), custom_call_target="tpu_custom_call" | custom-call | tf_op jit(solution)/shard_map/exchange_2/pallas_call | solution.py:272
  92.3 2.1 convolution_convert_fusion.4
  94.5 30.4 %reduce-scatter.3.cloned.1.call-done = bf16[128,1536]{1,0:T(8,128)(2,1)} async-done(((bf16[512,1536]{1,0:T(8,128)(2,1)}), bf16[128,1536]{1,0:T(8,128)(2,1)}) %reduce-scatter.3.cloned.1.call-update) | async-done | bytes 393232 | tf_op jit(solution)/shard_map/reduce_scatter | solution.py:1057
  124.9 2.0 convert_add_fusion
  127.0 1.9 multiply_convert_fusion.3
  130.8 1.5 concatenate.34.cosine_ref
  132.3 1.7 concatenate.35.sine_ref
  136.0 1.5 fusion.6.half_swap_ref
  137.5 1.6 pad_maximum_fusion.weight_ref
  140.1 8.6 %all-gather.7.cloned.1.call-done = bf16[512,1536]{1,0:T(8,128)(2,1)} async-done(((bf16[128,1536]{1,0:T(8,128)(2,1)}), bf16[512,1536]{1,0:T(8,128)(2,1)}) %all-gather.7.cloned.1.call-update) | async-done | bytes 1572880 | tf_op jit(solution)/shard_map/all_gather | solution.py:1053
  148.7 5.6 %fusion.16 = f32[512,1024]{1,0:T(8,128)} fusion(bf16[512,1536]{1,0:T(8,128)(2,1)} %all-gather.7.cloned.1.call-done, bf16[1024,1536]{1,0:T(8,128)(2,1)} %param.22), kind=kOutput, calls=%fused_computation.71 | convolution fusion | flops 1610612736 | bytes 6815744 | tf_op jit(solution)/shard_map/dot_general | solution.py:25
  154.3 3.1 fusion.15
  157.5 12.3 %all-gather.9.cloned.1.call-done = bf16[512,1536]{1,0:T(8,128)(2,1)} async-done(((bf16[128,1536]{1,0:T(8,128)(2,1)}), bf16[512,1536]{1,0:T(8,128)(2,1)}) %all-gather.9.cloned.1.call-update) | async-done | bytes 1572880 | tf_op jit(solution)/shard_map/all_gather | solution.py:1053
  169.8 6.5 %multiply_convert_fusion = (bf16[512,1024]{1,0:T(8,128)(2,1)}, bf16[512,1024]{1,0:T(8,128)(2,1)}, bf16[512,1024]{1,0:T(8,128)(2,1)S(1)}) fusion(f32[512,1024]{1,0:T(8,128)} %fusion.15, f32[512,1024]{1,0:T(8,128)} %fusion.16, bf16[512,1536]{1,0:T(8,128)(2,1)} %all-gather.9.cloned.1.call-done, bf16[1024,1536]{1,0:T(8,128)(2,1)S(1)} %copy-done.16), kind=kOutput, calls=%fused_computation.16 | convolution fusion | flops 1618477056 | bytes 12058624 | tf_op jit(solution)/shard_map/dot_general | solution.py:25
  177.3 3.0 convolution_convert_fusion.3
  180.3 4.1 fusion.17
  184.5 3.5 convolution_convert_fusion.down_ref
  188.0 3.5 convolution_convert_fusion.2.gate_ref
  191.5 3.5 convolution_convert_fusion.1.up_ref
  195.0 13.1 %fusion.3.part_ref = bf16[512,1536]{1,0:T(8,128)(2,1)} fusion(f32[512,1536]{1,0:T(8,128)S(1)} %fusion.17, bf16[512,1024]{1,0:T(8,128)(2,1)S(1)} %copy-done.22, bf16[1024,1536]{1,0:T(8,128)(2,1)S(1)} %copy-done.18), kind=kOutput, calls=%fused_computation.12 | convolution fusion | flops 1612185600 | bytes 8912896 | tf_op jit(solution)/shard_map/dot_general | solution.py:21
  208.1 280.4 %backward.1 = (bf16[4320,1536]{1,0:T(8,128)(2,1)}, f32[2,1536]{1,0:T(2,128)}, f32[128,1536]{1,0:T(8,128)}) custom-call(s32[32]{0:T(128)} %pad_add_fusion.order_ref, bf16[1024,1536]{1,0:T(8,128)(2,1)} %convolution_convert_fusion.2.gate_ref, bf16[1024,1536]{1,0:T(8,128)(2,1)} %convolution_convert_fusion.1.up_ref, ...), custom_call_target="tpu_custom_call" | custom-call | tf_op jit(solution)/shard_map/backward/pallas_call | solution.py:999
  488.4 1.4 slice_reduce_fusion.1
  489.9 2.9 slice_convert_fusion.5
  492.8 4.5 slice_convert_fusion.3
  497.3 9.4 %slice_convert_fusion = (f32[1024,1536]{1,0:T(8,128)}, f32[1024,1536]{1,0:T(8,128)}, f32[1024,1536]{1,0:T(8,128)}) fusion(bf16[4320,1536]{1,0:T(8,128)(2,1)} %get-tuple-element.16), kind=kLoop, calls=%fused_computation.9 | loop fusion | flops 4718592 | bytes 28311552 | tf_op jit(solution)/shard_map/convert_element_type | solution.py:1221
  506.7 2.0 add_convert_fusion
  (104 shorter events, 20.1 us)
Async XLA Ops:
  7.2 37.1 %all-gather.5.cloned.1.call-start = ((), (), s32[]{:S(2)}) async-start(), calls=%async_computation.2 | async-start | bytes 1966080 | tf_op jit(solution)/shard_map/all_gather | solution.py:1053
  7.9 117.0 %reduce-scatter.3.cloned.1.call-start = ((), (), s32[]{:S(2)}) async-start(), calls=%async_computation.3 | async-start | bytes 1966080 | tf_op jit(solution)/shard_map/reduce_scatter | solution.py:1057
  44.2 2.0 copy-start.5
  44.3 2.4 copy-start.11
  46.7 2.9 copy-start.2
  46.7 1.5 copy-start.8
  51.7 0.9 copy-start.13
  54.6 37.7 %copy-start.6 = (bf16[384,1536]{1,0:T(8,128)(2,1)S(1)}, bf16[384,1536]{1,0:T(8,128)(2,1)}, u32[]{:S(2)}) copy-start(bf16[384,1536]{1,0:T(8,128)(2,1)} %output_weight_ref.1) | copy-start | bytes 3538948
  67.0 1.1 copy-start
  73.7 0.8 copy-start.1
  92.2 2.3 copy-start.15
  92.2 32.7 %copy-start.3 = (bf16[128,1536]{1,0:T(8,128)(2,1)S(1)}, bf16[128,1536]{1,0:T(8,128)(2,1)}, u32[]{:S(2)}) copy-start(bf16[128,1536]{1,0:T(8,128)(2,1)} %input_ref.1) | copy-start | bytes 1179652
  94.4 36.3 %copy-start.14 = (bf16[1536]{0:T(1024)(128)(2,1)S(1)}, bf16[1536]{0:T(1024)(128)(2,1)}, u32[]{:S(2)}) copy-start(bf16[1536]{0:T(1024)(128)(2,1)} %param.15) | copy-start | bytes 9220
  94.4 54.2 %all-gather.7.cloned.1.call-start = ((), (), s32[]{:S(2)}) async-start(), calls=%async_computation.4 | async-start | bytes 1966080 | tf_op jit(solution)/shard_map/all_gather | solution.py:1053
  128.9 40.9 %all-gather.9.cloned.1.call-start = ((), (), s32[]{:S(2)}) async-start(), calls=%async_computation.6 | async-start | bytes 1966080 | tf_op jit(solution)/shard_map/all_gather | solution.py:1053
  129.5 377.2 %reduce-scatter.5.cloned.1.call-start = ((), (), s32[]{:S(2)}) async-start(), calls=%async_computation.5 | async-start | bytes 1966080 | tf_op jit(solution)/shard_map/reduce_scatter | solution.py:1057
  132.3 5.2 %copy-start.9 = (bf16[384,1536]{1,0:T(8,128)(2,1)S(1)}, bf16[384,1536]{1,0:T(8,128)(2,1)}, u32[]{:S(2)}) copy-start(bf16[384,1536]{1,0:T(8,128)(2,1)} %param.16) | copy-start | bytes 3538948
  132.3 5.2 %copy-start.12 = (bf16[192,1536]{1,0:T(8,128)(2,1)S(1)}, bf16[192,1536]{1,0:T(8,128)(2,1)}, u32[]{:S(2)}) copy-start(bf16[192,1536]{1,0:T(8,128)(2,1)} %param.18) | copy-start | bytes 1769476
  148.7 5.7 %copy-start.17 = (bf16[1024,1536]{1,0:T(8,128)(2,1)S(1)}, bf16[1024,1536]{1,0:T(8,128)(2,1)}, u32[]{:S(2)}) copy-start(bf16[1024,1536]{1,0:T(8,128)(2,1)} %param.21) | copy-start | bytes 9437188
  148.7 5.7 %copy-start.19 = (bf16[512,1536]{1,0:T(8,128)(2,1)S(1)}, bf16[512,1536]{1,0:T(8,128)(2,1)}, u32[]{:S(2)}) copy-start(bf16[512,1536]{1,0:T(8,128)(2,1)} %all-gather.7.cloned.1.call-done) | copy-start | bytes 4718596
  154.3 15.5 %copy-start.16 = (bf16[1024,1536]{1,0:T(8,128)(2,1)S(1)}, bf16[1024,1536]{1,0:T(8,128)(2,1)}, u32[]{:S(2)}) copy-start(bf16[1024,1536]{1,0:T(8,128)(2,1)} %param.23) | copy-start | bytes 9437188
  176.3 1.0 copy-start.24
  180.3 4.2 copy-start.21
  180.3 4.2 copy-start.25
  184.4 3.5 copy-start.20
  184.5 3.5 copy-start.23
  188.0 3.5 copy-start.22
  191.5 3.5 copy-start.18
  497.3 9.4 %copy-start.4 = (bf16[128,1536]{1,0:T(8,128)(2,1)S(1)}, bf16[128,1536]{1,0:T(8,128)(2,1)}, u32[]{:S(2)}) copy-start(bf16[128,1536]{1,0:T(8,128)(2,1)} %input_ref.1) | copy-start | bytes 1179652
  497.3 9.4 %copy-start.7 = (bf16[128,1536]{1,0:T(8,128)(2,1)S(1)}, bf16[128,1536]{1,0:T(8,128)(2,1)}, u32[]{:S(2)}) copy-start(bf16[128,1536]{1,0:T(8,128)(2,1)} %reduce-scatter.3.cloned.1.call-done) | copy-start | bytes 1179652
  506.7 2.0 copy-start.10
Sparse Core Ops, SparseCore 0:
  9.5 22.3 all-gather.4
  94.6 30.3 reduce-scatter.2
  129.0 19.6 all-gather.6
  150.1 19.6 all-gather.8
  180.4 27.9 reduce-scatter.4

commit v5 on v4

--- a/solution.py
+++ b/solution.py
@@ -186,102 +186,12 @@
     return lax.fori_loop(0, block_total, grad_step, initial)
 
 
-def sort_places(place_ref, source_ref, targets, block):
-    block_total = source_ref.shape[0] // block
-    for slot in range(block_total):
-        place = place_ref[slot * block]
-        rows = source_ref[pl.ds(slot * block, block), :]
-        start = 0
-        for target in targets:
-            width = target.shape[-1]
-            target[pl.ds(pl.multiple_of(place, block), block), :] = rows[:, start : start + width]
-            start += width
-
-
-def attention_forward_kernel(block, place_ref, packed_ref, out_ref, q0, q1, k, v, result):
-    sort_places(place_ref, packed_ref, (q0, q1, k, v), block)
-    length = packed_ref.shape[0]
-    tile = min(256, length)
-    for first in range(0, length, tile):
-        parts = []
-        for q in (q0, q1):
-            soft = softmax_parts(q[first : first + tile, :], k[: first + tile, :], first)
-            parts.append(product(soft.astype(jnp.bfloat16), v[: first + tile, :]))
-        result[first : first + tile, :] = jnp.concatenate(parts, axis=-1)
-    for slot in range(length // block):
-        place = pl.multiple_of(place_ref[slot * block], block)
-        out_ref[pl.ds(slot * block, block), :] = result[pl.ds(place, block), :].astype(
-            jnp.bfloat16
-        )
-
-
 def vmem():
     return pl.BlockSpec(memory_space=pltpu.VMEM)
 
 
-def attention_call(length, block):
-    pair = 2 * HEAD_DIM
-    half = [pltpu.VMEM((length, HEAD_DIM), jnp.bfloat16)]
-    params = pltpu.CompilerParams(vmem_limit_bytes=48 * 2**20)
-    places = pl.BlockSpec(memory_space=pltpu.SMEM)
-    forward = pl.pallas_call(
-        functools.partial(attention_forward_kernel, block),
-        out_shape=jax.ShapeDtypeStruct((length, pair), jnp.bfloat16),
-        in_specs=[places, vmem()],
-        out_specs=vmem(),
-        scratch_shapes=half * 4 + [pltpu.VMEM((length, pair), jnp.float32)],
-        compiler_params=params,
-        name="attention_forward",
-    )
-    return forward
-
-
 def peer(ctx_index):
     return dict(device_id={"ctx": ctx_index}, device_id_type=pl.DeviceIdType.MESH)
-
-
-def exchange_kernel(count, in_ref, out_ref, send_sem, recv_sem, own_sem):
-    me = lax.axis_index("ctx")
-    barrier = pltpu.get_barrier_semaphore()
-    for step in range(1, count):
-        pl.semaphore_signal(barrier, inc=1, **peer(lax.rem(me + step, count)))
-    own = pltpu.make_async_copy(in_ref.at[me], out_ref.at[me], own_sem)
-    own.start()
-    pl.semaphore_wait(barrier, count - 1)
-    copies = []
-    for step in range(1, count):
-        other = lax.rem(me + step, count)
-        copies.append(
-            pltpu.make_async_remote_copy(
-                src_ref=in_ref.at[other],
-                dst_ref=out_ref.at[me],
-                send_sem=send_sem.at[step],
-                recv_sem=recv_sem.at[step],
-                **peer(other),
-            )
-        )
-    for copy in copies:
-        copy.start()
-    own.wait()
-    for copy in copies:
-        copy.wait()
-
-
-def exchange(values, key):
-    count = values.shape[0]
-    return pl.pallas_call(
-        functools.partial(exchange_kernel, count),
-        out_shape=jax.ShapeDtypeStruct(values.shape, values.dtype),
-        in_specs=[pl.BlockSpec(memory_space=pl.ANY)],
-        out_specs=pl.BlockSpec(memory_space=pl.ANY),
-        scratch_shapes=[
-            pltpu.SemaphoreType.DMA((count,)),
-            pltpu.SemaphoreType.DMA((count,)),
-            pltpu.SemaphoreType.DMA,
-        ],
-        compiler_params=pltpu.CompilerParams(collective_id=key, has_side_effects=True),
-        name=f"exchange_{key}",
-    )(values)
 
 
 SPINE_ROWS = 48
@@ -379,11 +289,12 @@
 
 
 class Gather:
-    def __init__(self, place, full, send_sem, recv_sem):
+    def __init__(self, place, full, send_sem, recv_sem, count=TILE):
         self.place, self.full, self.send_sem, self.recv_sem = place, full, send_sem, recv_sem
+        self.count = count
 
     def copy(self, block, target, key):
-        span = rows_at(block * TILE, TILE)
+        span = pl.ds(pl.multiple_of(block * self.count, self.count), self.count)
         return pltpu.make_async_remote_copy(
             src_ref=self.full.at[span],
             dst_ref=self.full.at[span],
@@ -400,8 +311,10 @@
         self.copy(self.place.across, self.place.across, 1).wait_recv()
         self.copy(self.place.across, self.place.partner, 2).start()
 
+    def first(self):
+        self.copy(self.place.partner, self.place.partner, 0).wait_recv()
+
     def arrive(self):
-        self.copy(self.place.partner, self.place.partner, 0).wait_recv()
         self.copy(self.place.corner, self.place.partner, 2).wait_recv()
         self.copy(self.place.row, self.place.across, 1).wait_send()
         self.copy(self.place.row, self.place.partner, 0).wait_send()
@@ -409,33 +322,41 @@
 
 
 class Swap:
-    def __init__(self, place, source, target, send_sem, recv_sem):
+    def __init__(self, place, source, target, send_sem, recv_sem, count, share=1):
         self.place, self.source, self.target = place, source, target
-        self.send_sem, self.recv_sem = send_sem, recv_sem
-
-    def copy(self, step):
-        other = lax.rem(self.place.ctx + step, 8)
+        self.send_sem, self.recv_sem, self.count, self.share = send_sem, recv_sem, count, share
+
+    def span(self, index):
+        return pl.ds(pl.multiple_of(index * self.count, self.count), self.count)
+
+    def copy(self, other, sender):
         return pltpu.make_async_remote_copy(
-            src_ref=self.source.at[self.span(other)],
-            dst_ref=self.target.at[self.span(self.place.ctx)],
-            send_sem=self.send_sem.at[step],
-            recv_sem=self.recv_sem.at[step],
+            src_ref=self.source.at[self.span(lax.div(other, self.share))],
+            dst_ref=self.target.at[self.span(sender)],
+            send_sem=self.send_sem.at[other],
+            recv_sem=self.recv_sem.at[sender],
             **peer(other),
         )
 
-    def span(self, index):
-        blocks = self.source.shape[0] // 8
-        return pl.ds(index * blocks, blocks)
-
-    def start(self):
-        for step in range(1, 8):
-            self.copy(step).start()
-        own = self.span(self.place.ctx)
-        self.target[own] = self.source[own]
+    def start(self, other):
+        me = self.place.ctx
+
+        @pl.when(other != me)
+        def _():
+            self.copy(other, me).start()
+
+        @pl.when(other == me)
+        def _():
+            self.target[self.span(me)] = self.source[self.span(lax.div(me, self.share))]
+
+    def start_all(self):
+        for step in range(1, 9):
+            self.start(lax.rem(self.place.ctx + step, 8))
 
     def arrive(self):
         for step in range(1, 8):
-            self.copy(step).wait()
+            other = lax.rem(self.place.ctx + step, 8)
+            self.copy(other, other).wait()
 
 
 class Spread:
@@ -738,8 +659,8 @@
     fold_two = Fold(place, part, near.at[0], send.at[0], far.at[0], fold_send.at[0], fold_recv.at[0])
     fold_one = Fold(place, part, near.at[1], send.at[1], far.at[1], fold_send.at[1], fold_recv.at[1])
     gather = Gather(place, branch, gather_send, gather_recv)
-    swap_heads = Swap(place, heads_out, heads_in, swap_send.at[0], swap_recv.at[0])
-    swap_packed = Swap(place, packed_out, packed_in, swap_send.at[1], swap_recv.at[1])
+    swap_heads = Swap(place, heads_out, heads_in, swap_send.at[0], swap_recv.at[0], halves)
+    swap_packed = Swap(place, packed_out, packed_in, swap_send.at[1], swap_recv.at[1], halves)
     spread_near = Spread(gain_near, place.row, 4, near_fsdp, near_send, near_recv)
     spread_far = Spread(gain_far, me, 8, peer, far_send, far_recv)
     fold_two.start()
@@ -796,6 +717,7 @@
 
     def stage_heads():
         fetch(output_weight_ref)
+        gather.first()
         gather.arrive()
 
         @pl.loop(0, 4)
@@ -807,7 +729,7 @@
                     :, head * PAIR : (head + 1) * PAIR
                 ].reshape(halves, block, PAIR)
 
-        swap_heads.start()
+        swap_heads.start_all()
 
     def stage_sort():
         fetch(packed_ref)
@@ -815,11 +737,18 @@
 
     def stage_output_grad():
         fetch(attended_ref)
-        for first in range(0, own.shape[1], 512):
-            columns = slice(first, first + 512)
-            own[base + 2 * WIDE :base + 3 * WIDE, columns] = product_rows(
-                attended[...], branch[:, columns]
-            ).astype(jnp.bfloat16)
+        for head in range(2):
+            rows = [
+                attended[(2 * index + head) * halves : (2 * index + head + 1) * halves]
+                for index in range(4)
+            ]
+            rows = jnp.concatenate(rows, axis=0).reshape(4 * TILE, PAIR)
+            first_row = base + 2 * WIDE + head * PAIR
+            for first in range(0, own.shape[1], 512):
+                columns = slice(first, first + 512)
+                own[first_row : first_row + PAIR, columns] = product_rows(
+                    rows, branch[:, columns]
+                ).astype(jnp.bfloat16)
 
     def stage_sort_grads():
         swap_heads.arrive()
@@ -852,7 +781,7 @@
             packed_out[slot] = jnp.concatenate(
                 [result[spot], dk[spot], dv[spot]], axis=-1
             ).astype(jnp.bfloat16)
-        swap_packed.start()
+        swap_packed.start_all()
 
     def stage_turn():
         fetch(cosine_ref, sine_ref, half_swap_ref, weight_ref)
@@ -867,7 +796,7 @@
                 grads = grads.reshape(TILE, WIDE)
                 swapped = product(grads, half_swap[...])
                 low = (
-                    grads.astype(jnp.float32) * cosine[span, :] + swapped * sine[span, :]
+                    grads.astype(jnp.float32) * cosine[span, :] - swapped * sine[span, :]
                 ).astype(jnp.bfloat16)
                 turned[head, span, :] = low
                 term = product(low, weight[head])
@@ -983,8 +912,7 @@
     width = hidden.shape[1]
     rows = 3 * grads[0].shape[0] + 3 * WIDE
     rounds = -(-rows // ROUND_ROWS)
-    length = packed.shape[0]
-    packed = packed.reshape(-1, block, WIDE)
+    length = packed.shape[0] * block
     dma = pltpu.SemaphoreType.DMA
     low, full = jnp.bfloat16, jnp.float32
     any_spec = pl.BlockSpec(memory_space=pl.ANY)
@@ -1049,6 +977,349 @@
     )(*operands)
 
 
+def forward_kernel(
+    block,
+    place_ref,
+    table_ref,
+    gain_ref,
+    input_ref,
+    cotangent_ref,
+    query_weight_ref,
+    key_weight_ref,
+    value_weight_ref,
+    output_weight_ref,
+    gate_weight_ref,
+    up_weight_ref,
+    down_weight_ref,
+    place_out,
+    part_out,
+    hidden_out,
+    attended_out,
+    packed_out,
+    normed_one_out,
+    cosine_out,
+    sine_out,
+    cotangent_out,
+    normed_two_out,
+    mixed_out,
+    grad_gate_out,
+    grad_up_out,
+    places,
+    tables,
+    inputs,
+    cotangents,
+    normed_one,
+    normed_two,
+    cosine,
+    sine,
+    weight,
+    output_weight,
+    gate_weight,
+    up_weight,
+    down_weight,
+    packed_from,
+    packed,
+    q0,
+    q1,
+    k,
+    v,
+    result,
+    heads_from,
+    heads,
+    part,
+    near,
+    send,
+    far,
+    hidden,
+    mixed,
+    grad_gate,
+    grad_up,
+    fetch_sem,
+    store_sem,
+    gather_send,
+    gather_recv,
+    swap_send,
+    swap_recv,
+    fold_send,
+    fold_recv,
+):
+    place = Place()
+    length, width = q0.shape[0], inputs.shape[1]
+    halves = TILE // block
+    half = HEAD_DIM // 2
+    pair_rows = 2 * TILE
+    fetches, stores = {}, []
+
+    def fetch_all(key, *copies):
+        base = sum(len(group) for group in fetches.values())
+        fetches[key] = [
+            pltpu.make_async_copy(part_of, target, fetch_sem.at[base + index])
+            for index, (part_of, target) in enumerate(copies)
+        ]
+        for copy in fetches[key]:
+            copy.start()
+
+    def fetch(*keys):
+        for key in keys:
+            for copy in fetches[key]:
+                copy.wait()
+
+    def store(source, target):
+        copy = pltpu.make_async_copy(source, target, store_sem.at[len(stores)])
+        copy.start()
+        stores.append(copy)
+
+    own_rows = rows_at(place.row * TILE, TILE)
+    fetch_all("inputs", (input_ref, inputs.at[own_rows]))
+    fetch_all("cotangent", (cotangent_ref, cotangents.at[own_rows]))
+    copies = []
+    for head in range(2):
+        query_base, key_base = head * PAIR, head * HEAD_DIM
+        target = weight.at[head]
+        heads_of = [(query_weight_ref, query_base), (query_weight_ref, query_base + HEAD_DIM)]
+        heads_of += [(key_weight_ref, key_base), (value_weight_ref, key_base)]
+        for index, (source, first) in enumerate(heads_of):
+            copies.append(
+                (source.at[pl.ds(first, HEAD_DIM)], target.at[pl.ds(index * HEAD_DIM, HEAD_DIM)])
+            )
+            for side in range(2):
+                copies.append(
+                    (
+                        source.at[pl.ds(first + (1 - side) * half, half)],
+                        target.at[pl.ds(WIDE + index * HEAD_DIM + side * half, half)],
+                    )
+                )
+    fetch_all("weight", *copies)
+    fetch_all("output", (output_weight_ref, output_weight))
+    fetch_all("gate", (gate_weight_ref, gate_weight))
+    fetch_all("up", (up_weight_ref, up_weight))
+    fetch_all("down", (down_weight_ref, down_weight))
+    places[pl.ds(pl.multiple_of(place.row * 8, 8), 8), :] = place_ref[...]
+    tables[own_rows, :] = table_ref[...]
+    gather_places = Gather(place, places, gather_send.at[0], gather_recv.at[0], 8)
+    gather_tables = Gather(place, tables, gather_send.at[1], gather_recv.at[1])
+    gather_inputs = Gather(place, inputs, gather_send.at[2], gather_recv.at[2])
+    gather_cotangents = Gather(place, cotangents, gather_send.at[3], gather_recv.at[3])
+    gather_two = Gather(place, normed_two, gather_send.at[4], gather_recv.at[4])
+    swap_places = Swap(place, places, place_out, swap_send.at[0], swap_recv.at[0], 8, 2)
+    swap_packed = Swap(place, packed_from, packed, swap_send.at[1], swap_recv.at[1], halves)
+    swap_heads = Swap(place, heads_from, heads, swap_send.at[2], swap_recv.at[2], halves)
+    fold = Fold(place, part, near, send, far, fold_send, fold_recv)
+    place.greet()
+    fetch("inputs")
+    gather_tables.start()
+    gather_inputs.start()
+    gather_places.start()
+    fetch("cotangent")
+    gather_cotangents.start()
+
+    def project(chip):
+        base = chip * pair_rows
+
+        @pl.loop(0, pair_rows // 16)
+        def _(piece):
+            span = rows_at(base + piece * 16, 16)
+            rows = inputs[span, :].astype(jnp.float32)
+            normed_one[span, :] = (rows * rms_scale(rows) * gain_ref[0:1, :]).astype(jnp.bfloat16)
+
+        span = rows_at(base, pair_rows)
+        low_cosine, low_sine = tables[span, :half], tables[span, half:HEAD_DIM]
+        ones = jnp.ones((pair_rows, HEAD_DIM), jnp.float32)
+        cosine[span, :] = jnp.concatenate([low_cosine] * 6 + [ones], axis=-1)
+        sine[span, :] = jnp.concatenate([-low_sine, low_sine] * 3 + [ones * 0.0], axis=-1)
+
+        for head in range(2):
+            products = product_back(normed_one[span, :], weight[head])
+            low = (
+                products[:, :WIDE] * cosine[span, :] + products[:, WIDE:] * sine[span, :]
+            ).astype(jnp.bfloat16)
+            for index in range(2):
+                packed_from[pl.ds(((2 * chip + index) * 2 + head) * halves, halves)] = low[
+                    index * TILE : (index + 1) * TILE
+                ].reshape(halves, block, WIDE)
+        for index in range(4):
+            swap_packed.start(4 * chip + index)
+
+    gather_tables.first()
+    gather_inputs.first()
+    gather_places.first()
+    fetch("weight")
+    project(place.chip)
+    gather_tables.relay()
+    gather_inputs.relay()
+    gather_places.relay()
+    gather_tables.arrive()
+    gather_inputs.arrive()
+    gather_places.arrive()
+    project(1 - place.chip)
+    swap_places.start_all()
+    store(normed_one, normed_one_out)
+    store(cosine, cosine_out)
+    store(sine, sine_out)
+    swap_places.arrive()
+    swap_packed.arrive()
+    store(packed, packed_out)
+
+    def place_row(first, count):
+        blocks = [place_out[8 * index : 8 * index + 1, :] for index in range(first, first + count)]
+        return jnp.concatenate(blocks, axis=-1)
+
+    tile = min(256, length)
+    order = place_row(0, length // TILE)
+    flat = packed[...].reshape(length, WIDE)
+    for first in range(0, length, tile):
+        rows = lax.broadcasted_iota(jnp.int32, (tile, length), 0) + first
+        chosen = jnp.where(rows == order, 1.0, 0.0).astype(jnp.bfloat16)
+        moved = product(chosen, flat).astype(jnp.bfloat16)
+        for index, target in enumerate((q0, q1, k, v)):
+            target[first : first + tile, :] = moved[:, index * HEAD_DIM : (index + 1) * HEAD_DIM]
+    for first in range(0, length, tile):
+        parts = []
+        for q in (q0, q1):
+            soft = softmax_parts(q[first : first + tile, :], k[: first + tile, :], first)
+            parts.append(product(soft.astype(jnp.bfloat16), v[: first + tile, :]))
+        result[first : first + tile, :] = jnp.concatenate(parts, axis=-1).astype(jnp.bfloat16)
+    for first in range(0, length, tile):
+        rows = lax.broadcasted_iota(jnp.int32, (length, tile), 0)
+        chosen = jnp.where(rows == place_row(first // TILE, tile // TILE), 1.0, 0.0)
+        moved = product_rows(chosen.astype(jnp.bfloat16), result[...]).astype(jnp.bfloat16)
+        heads_from[first // block : (first + tile) // block] = moved.reshape(-1, block, PAIR)
+    swap_heads.start_all()
+    gather_cotangents.first()
+    gather_cotangents.relay()
+    fetch("output")
+    swap_heads.arrive()
+    store(heads, attended_out)
+
+    @pl.loop(0, 4)
+    def _(sequence):
+        total = None
+        for head in range(2):
+            rows = heads[pl.ds((2 * sequence + head) * halves, halves)].reshape(TILE, PAIR)
+            term = product(rows, output_weight[head * PAIR : (head + 1) * PAIR, :])
+            total = term if total is None else total + term
+        part[rows_at(sequence * TILE, TILE), :] = total.astype(jnp.bfloat16)
+
+    fold.start()
+    gather_cotangents.arrive()
+    store(cotangents, cotangent_out)
+    fold.relay()
+    fold.arrive()
+
+    @pl.loop(0, TILE // 16)
+    def _(piece):
+        span = rows_at(piece * 16, 16)
+        own = rows_at(place.row * TILE + piece * 16, 16)
+        rows = inputs[own, :].astype(jnp.float32) + fold.rows(piece * 16, 16)
+        hidden[span, :] = rows
+        normed_two[own, :] = (rows * rms_scale(rows) * gain_ref[1:2, :]).astype(jnp.bfloat16)
+
+    gather_two.start()
+    store(hidden, hidden_out)
+    fetch("gate", "up", "down")
+
+    def feed(chip):
+        span = rows_at(chip * pair_rows, pair_rows)
+
+        @pl.loop(0, mixed.shape[1] // 256)
+        def _(index):
+            units = rows_at(index * 256, 256)
+            columns = pl.ds(pl.multiple_of(index * 256, 256), 256)
+            gate = product_back(normed_two[span, :], gate_weight[units, :])
+            upward = product_back(normed_two[span, :], up_weight[units, :])
+            grad_mixed = product_back(cotangents[span, :], down_weight[units, :])
+            sigmoid = jax.nn.sigmoid(gate)
+            activated = gate * sigmoid
+            mixed[span, columns] = (activated * upward).astype(jnp.bfloat16)
+            grad_gate[span, columns] = (
+                grad_mixed * upward * sigmoid * (1.0 + gate * (1.0 - sigmoid))
+            ).astype(jnp.bfloat16)
+            grad_up[span, columns] = (grad_mixed * activated).astype(jnp.bfloat16)
+
+        @pl.loop(0, width // 512)
+        def _(index):
+            columns = pl.ds(pl.multiple_of(index * 512, 512), 512)
+            part[span, columns] = (
+                product(grad_gate[span, :], gate_weight[:, columns])
+                + product(grad_up[span, :], up_weight[:, columns])
+            ).astype(jnp.bfloat16)
+
+    gather_two.first()
+    feed(place.chip)
+    gather_two.relay()
+    gather_two.arrive()
+    store(normed_two, normed_two_out)
+    feed(1 - place.chip)
+    store(part, part_out)
+    store(mixed, mixed_out)
+    store(grad_gate, grad_gate_out)
+    store(grad_up, grad_up_out)
+    for copy in stores:
+        copy.wait()
+
+
+def forward(places, table, gains, inputs, cotangent, query_weight, key_weight, value_weight,
+            output_weight, gate_weight, up_weight, down_weight, length, block, key):
+    width = inputs.shape[1]
+    hidden_units = gate_weight.shape[0]
+    rows = 4 * TILE
+    blocks = length // block
+    low, full = jnp.bfloat16, jnp.float32
+    dma = pltpu.SemaphoreType.DMA
+    any_spec = pl.BlockSpec(memory_space=pl.ANY)
+
+    def out(shape, dtype):
+        return jax.ShapeDtypeStruct(shape, dtype)
+
+    wide = (rows, width)
+    return pl.pallas_call(
+        functools.partial(forward_kernel, block),
+        out_shape=(
+            out((64, 128), jnp.int32),
+            out(wide, low), out((TILE, width), full),
+            out((blocks, block, PAIR), low), out((blocks, block, WIDE), low),
+            out(wide, low), out((rows, WIDE), full), out((rows, WIDE), full),
+            out(wide, low), out(wide, low),
+            out((rows, hidden_units), low), out((rows, hidden_units), low),
+            out((rows, hidden_units), low),
+        ),
+        in_specs=[vmem()] * 3 + [any_spec] * 9,
+        out_specs=(vmem(),) + (any_spec,) * 12,
+        scratch_shapes=[
+            pltpu.VMEM((32, 128), jnp.int32),
+            pltpu.VMEM((rows, 128), full),
+            pltpu.VMEM(wide, low), pltpu.VMEM(wide, low),
+            pltpu.VMEM(wide, low), pltpu.VMEM(wide, low),
+            pltpu.VMEM((rows, WIDE), full), pltpu.VMEM((rows, WIDE), full),
+            pltpu.VMEM((2, 2 * WIDE, width), low),
+            pltpu.VMEM(output_weight.shape, low),
+            pltpu.VMEM((hidden_units, width), low), pltpu.VMEM((hidden_units, width), low),
+            pltpu.VMEM((hidden_units, width), low),
+            pltpu.VMEM((blocks, block, WIDE), low), pltpu.VMEM((blocks, block, WIDE), low),
+        ]
+        + [pltpu.VMEM((length, HEAD_DIM), low)] * 4
+        + [
+            pltpu.VMEM((length, PAIR), low),
+            pltpu.VMEM((blocks, block, PAIR), low), pltpu.VMEM((blocks, block, PAIR), low),
+            pltpu.VMEM(wide, low),
+            pltpu.VMEM((2, TILE, width), low),
+            pltpu.VMEM((TILE, width), low), pltpu.VMEM((TILE, width), low),
+            pltpu.VMEM((TILE, width), full),
+            pltpu.VMEM((rows, hidden_units), low), pltpu.VMEM((rows, hidden_units), low),
+            pltpu.VMEM((rows, hidden_units), low),
+            dma((30,)), dma((12,)),
+            dma((5, 3)), dma((5, 3)),
+            dma((3, 8)), dma((3, 8)),
+            dma((3,)), dma((3,)),
+        ],
+        compiler_params=pltpu.CompilerParams(
+            collective_id=key, has_side_effects=True, vmem_limit_bytes=63 * 2**20
+        ),
+        name="forward",
+    )(places, table, gains, inputs, cotangent, query_weight, key_weight, value_weight,
+      output_weight, gate_weight, up_weight, down_weight)
+
+
 def gather_rows(values):
     return lax.all_gather(values, "fsdp", axis=0, tiled=True)
 
@@ -1059,7 +1330,7 @@
     ).astype(jnp.float32)
 
 
-def per_device(
+def per_device_gathered(
     inputs,
     positions,
     cotangent,
@@ -1103,60 +1374,29 @@
     ).astype(jnp.bfloat16)
     value_low = product_back(normed_one, value_weight).astype(jnp.bfloat16)
     ctx_size = lax.axis_size("ctx")
-    by_head = ctx_size == seq_count * kv_heads
-
-    def to_heads(parts):
-        grouped = [
-            part.reshape(seq_count, row_count, kv_heads, -1).swapaxes(1, 2) for part in parts
-        ]
-        return jnp.concatenate(grouped, axis=-1).reshape(ctx_size, row_count, -1)
-
-    def from_heads(values, widths):
-        grouped = values.reshape(seq_count, kv_heads, row_count, -1).swapaxes(1, 2)
-        parts, start = [], 0
-        for width in widths:
-            parts.append(grouped[..., start : start + width].reshape(total_rows, kv_heads * width))
-            start += width
-        return parts
-
-    pair = groups * HEAD_DIM
-    flat_query = query_low.reshape(total_rows, query_heads * HEAD_DIM)
-    if by_head:
-        own_sequence = lax.axis_index("ctx") // kv_heads
-        head_places = lax.dynamic_index_in_dim(key_places, own_sequence, 0, keepdims=False)
-        length = head_places.shape[0]
-        block = row_count // 2
-        forward_call = attention_call(length, block)
-        packed = exchange(
-            to_heads([flat_query, key_low.reshape(total_rows, kv_width), value_low]), 1
-        ).reshape(length, -1)
-        attended_low = from_heads(
-            exchange(forward_call(head_places, packed).reshape(ctx_size, row_count, pair), 2),
-            (pair,),
-        )[0]
-    else:
-        def spread(values):
-            rows = lax.all_gather(values, "ctx", axis=0, tiled=True)
-            rows = rows.reshape(ctx_size, seq_count, row_count, kv_width).swapaxes(0, 1)
-            return rows.reshape(seq_count, ctx_size * row_count, kv_width)
-
-        def collect(values):
-            rows = values.astype(jnp.bfloat16).swapaxes(1, 2)
-            rows = rows.reshape(seq_count, ctx_size, row_count, kv_width).swapaxes(0, 1)
-            return lax.psum_scatter(
-                rows.reshape(-1, kv_width), "ctx", scatter_dimension=0, tiled=True
-            )
-
-        all_keys = spread(key_low.reshape(total_rows, kv_width))
-        all_values = spread(value_low)
-        total_keys = all_keys.shape[1]
-        key_grid = all_keys.reshape(seq_count, total_keys, kv_heads, HEAD_DIM).swapaxes(1, 2)
-        value_grid = all_values.reshape(seq_count, total_keys, kv_heads, HEAD_DIM).swapaxes(1, 2)
-        query_grouped = query_low.reshape(seq_count, row_count, kv_heads, groups, HEAD_DIM)
-        attended, log_total = attend_forward(
-            query_grouped, query_places, key_grid, value_grid, key_places
-        )
-        attended_low = attended.reshape(total_rows, query_heads * HEAD_DIM).astype(jnp.bfloat16)
+
+    def spread(values):
+        rows = lax.all_gather(values, "ctx", axis=0, tiled=True)
+        rows = rows.reshape(ctx_size, seq_count, row_count, kv_width).swapaxes(0, 1)
+        return rows.reshape(seq_count, ctx_size * row_count, kv_width)
+
+    def collect(values):
+        rows = values.astype(jnp.bfloat16).swapaxes(1, 2)
+        rows = rows.reshape(seq_count, ctx_size, row_count, kv_width).swapaxes(0, 1)
+        return lax.psum_scatter(
+            rows.reshape(-1, kv_width), "ctx", scatter_dimension=0, tiled=True
+        )
+
+    all_keys = spread(key_low.reshape(total_rows, kv_width))
+    all_values = spread(value_low)
+    total_keys = all_keys.shape[1]
+    key_grid = all_keys.reshape(seq_count, total_keys, kv_heads, HEAD_DIM).swapaxes(1, 2)
+    value_grid = all_values.reshape(seq_count, total_keys, kv_heads, HEAD_DIM).swapaxes(1, 2)
+    query_grouped = query_low.reshape(seq_count, row_count, kv_heads, groups, HEAD_DIM)
+    attended, log_total = attend_forward(
+        query_grouped, query_places, key_grid, value_grid, key_places
+    )
+    attended_low = attended.reshape(total_rows, query_heads * HEAD_DIM).astype(jnp.bfloat16)
     hidden_state = inputs.astype(jnp.float32) + scatter_rows(product(attended_low, output_weight))
     scale_two = rms_scale(hidden_state)
     unit_two = hidden_state * scale_two
@@ -1176,53 +1416,6 @@
     grad_unit_part = (
         product(grad_gate_low, gate_weight) + product(grad_up_low, up_weight)
     ).astype(jnp.bfloat16)
-    if by_head:
-        starts = head_places.reshape(-1, block)[:, 0] // block
-        slots = jnp.arange(length // block, dtype=jnp.int32)
-        found = jnp.where(starts[None, :] == slots[:, None], slots[None, :], 0)
-        order = jnp.concatenate([jnp.sum(found, axis=1), starts]).astype(jnp.int32)
-        half = HEAD_DIM // 2
-        flat_cosine, flat_sine = cosine[:, 0, :], sine[:, 0, :]
-        ones = jnp.ones((total_rows, HEAD_DIM), jnp.float32)
-        wide_cosine = jnp.concatenate([flat_cosine] * (2 * groups + 2) + [ones], axis=1)
-        wide_sine = jnp.concatenate(
-            [flat_sine, -flat_sine] * (groups + 1) + [jnp.zeros_like(ones)], axis=1
-        )
-        lanes = jnp.arange(WIDE, dtype=jnp.int32)
-        partner_lane = lanes + jnp.where(lanes % HEAD_DIM < half, half, -half)
-        half_swap = jnp.logical_and(
-            lanes[:, None] == partner_lane[None, :], lanes[None, :] < PAIR + HEAD_DIM
-        ).astype(jnp.bfloat16)
-        width = inputs.shape[1]
-        weight = jnp.concatenate(
-            [
-                query_weight.reshape(kv_heads, pair, width),
-                key_weight.reshape(kv_heads, HEAD_DIM, width),
-                value_weight.reshape(kv_heads, HEAD_DIM, width),
-            ],
-            axis=1,
-        )
-        layer_output = (hidden_state + scatter_rows(product(mixed_hidden, down_weight))).astype(
-            jnp.bfloat16
-        )
-        ff_grads = (
-            product_rows(grad_gate_low, normed_two).astype(jnp.bfloat16),
-            product_rows(grad_up_low, normed_two).astype(jnp.bfloat16),
-            grad_down.astype(jnp.bfloat16),
-        )
-        summed, gain_sums, input_grad = backward(
-            order, ff_grads, grad_unit_part, hidden_state, cotangent, inputs,
-            jnp.stack([gain_one, gain_two]), output_weight, attended_low, packed, normed_one,
-            wide_cosine, wide_sine, half_swap, weight, block, 5,
-        )
-        parts, start = [], 0
-        for grad in (gate_weight, up_weight, down_weight, query_weight, key_weight, value_weight,
-                     output_weight):
-            parts.append(summed[start : start + grad.shape[0]].astype(jnp.float32))
-            start += grad.shape[0]
-        return (
-            layer_output, input_grad, gain_sums[0], *parts[3:], gain_sums[1], *parts[:3],
-        )
     grad_normed_two = scatter_rows(grad_unit_part)
     gain_two_grad = jnp.sum(grad_normed_two * unit_two, axis=0)
     grad_hidden = grad_out + norm_back(scale_two, unit_two, grad_normed_two * gain_two)
@@ -1282,6 +1475,76 @@
     )
 
 
+def per_device_by_head(
+    inputs,
+    positions,
+    cotangent,
+    attention_gain,
+    query_weight,
+    key_weight,
+    value_weight,
+    output_weight,
+    feedforward_gain,
+    gate_weight,
+    up_weight,
+    down_weight,
+):
+    gains = jnp.stack([attention_gain, feedforward_gain]).astype(jnp.float32)
+    block = TILE // 2
+    length = TILE * 8
+    cosine, sine = rotary_tables(positions)
+    table = jnp.concatenate([cosine[:, 0, :], sine[:, 0, :]], axis=1)
+    table = jnp.pad(table, ((0, 0), (0, 128 - table.shape[1])))
+    (
+        places, part, hidden, attended, packed, normed_one, wide_cosine, wide_sine,
+        cotangents, normed_two, mixed, grad_gate, grad_up,
+    ) = forward(
+        jnp.broadcast_to(positions[None, :], (8, TILE)), table, gains, inputs, cotangent,
+        query_weight, key_weight, value_weight, output_weight, gate_weight, up_weight,
+        down_weight, length, block, 1,
+    )
+    starts = places.reshape(8, 8, TILE)[:, 0, ::block].reshape(-1) // block
+    slots = jnp.arange(length // block, dtype=jnp.int32)
+    found = jnp.where(starts[None, :] == slots[:, None], slots[None, :], 0)
+    order = jnp.concatenate([jnp.sum(found, axis=1), starts]).astype(jnp.int32)
+    half = HEAD_DIM // 2
+    lanes = jnp.arange(WIDE, dtype=jnp.int32)
+    partner_lane = lanes + jnp.where(lanes % HEAD_DIM < half, half, -half)
+    half_swap = jnp.logical_and(
+        lanes[:, None] == partner_lane[None, :], lanes[None, :] < PAIR + HEAD_DIM
+    ).astype(jnp.bfloat16)
+    width = inputs.shape[1]
+    weight = jnp.concatenate(
+        [
+            query_weight.reshape(2, PAIR, width),
+            key_weight.reshape(2, HEAD_DIM, width),
+            value_weight.reshape(2, HEAD_DIM, width),
+        ],
+        axis=1,
+    )
+    layer_output = (hidden + scatter_rows(product(mixed, down_weight))).astype(jnp.bfloat16)
+    ff_grads = (
+        product_rows(grad_gate, normed_two).astype(jnp.bfloat16),
+        product_rows(grad_up, normed_two).astype(jnp.bfloat16),
+        product_rows(mixed, cotangents).astype(jnp.bfloat16),
+    )
+    summed, gain_sums, input_grad = backward(
+        order, ff_grads, part, hidden, cotangent, inputs, gains, output_weight, attended,
+        packed, normed_one, wide_cosine, wide_sine, half_swap, weight, block, 5,
+    )
+    parts, start = [], 0
+    for grad in (gate_weight, up_weight, down_weight, query_weight, key_weight, value_weight,
+                 output_weight):
+        parts.append(summed[start : start + grad.shape[0]].astype(jnp.float32))
+        start += grad.shape[0]
+    return (layer_output, input_grad, gain_sums[0], *parts[3:], gain_sums[1], *parts[:3])
+
+
+def per_device(*arrays):
+    fits = lax.axis_size("fsdp") == 4 and lax.axis_size("ctx") == 8
+    return (per_device_by_head if fits else per_device_gathered)(*arrays)
+
+
 def solution(mesh):
     in_specs = (
         P(("fsdp", "ctx"), None),

time: 522 us -> 445 us (0.85)
  Pallas kernels: 315 us -> 384 us
  waiting for transfers between devices: 52.6 us -> 0.02 us
  matrix products: 51.5 us -> 15.8 us
  blocking collectives: 33.1 us -> 0 us
  local copies, waits for them, and re-layouts: 16.4 us -> 5.9 us
  other arithmetic: 33.2 us -> 24.1 us
    pallas_call x3 -> x1, Pallas kernels: 34.4 us -> 96.8 us  [forward(): pl.pallas_call(functools.partial(forward_kernel, block), out_shape=(out((...]
    all_gather x2 -> x0, blocking collectives: 33.1 us -> none  [the longest x1 26.9 us: per_device(): key_places = lax.all_gather(query_places, 'ctx', axis=1, tiled=True)]
    reduce_scatter x2 -> x1, waiting for transfers between devices: 30.4 us -> 0.01 us  [scatter_rows(): lax.psum_scatter(values.astype(jnp.bfloat16), 'fsdp', scatter_dimension=0...]
    all_gather x3 -> x0, waiting for transfers between devices: 21 us -> none  [gather_rows(): return lax.all_gather(values, 'fsdp', axis=0, tiled=True)]
    dot_general x6 -> x0, matrix products: 18.7 us -> none  [product_back(): lax.dot_general(left, right, (((1,), (1,)), ((), ())), preferred_element_...]
    dot_general x4 -> x1, matrix products: 22.3 us -> 5.29 us  [product(): return jnp.dot(left, right, preferred_element_type=jnp.float32)]
    pallas_call x1, Pallas kernels: 280 us -> 287 us  [backward(): pl.pallas_call(functools.partial(backward_kernel, rounds, block), out_sha...]
    convert_element_type x9 -> x6, other arithmetic: 23.3 us -> 20.1 us  [the longest x3 16.8 us: per_device_by_head(): parts.append(summed[start:start + grad.shape[0]].astype(jnp.float32))]
  transfers between devices with their start and end apart: 5 -> 1, of which waited for: 3 -> 0; matrix products, arithmetic and copies ran while one was open for 13% -> 7% of each run, Pallas kernels for 54% -> 65%
where the time goes in v5:
time: 445 us; the launch traced here: 444 us
  Pallas kernels  384 us (86%)
  other arithmetic  24.1 us (5%)
  matrix products  15.8 us (4%)
  between operations  14.2 us (3%)
  local copies, waits for them, and re-layouts  5.9 us (1%)
    pallas_call x1, Pallas kernels, backward(): pl.pallas_call(functools.partial(backward_kernel, rounds, block), out_sha...  287 us
    pallas_call x1, Pallas kernels, forward(): pl.pallas_call(functools.partial(forward_kernel, block), out_shape=(out((...  96.8 us
    convert_element_type x3, other arithmetic, per_device_by_head(): parts.append(summed[start:start + grad.shape[0]].astype(jnp.float32))  16.8 us
    dot_general x3, matrix products, product_rows(): lax.dot_general(left, right, (((0,), (0,)), ((), ())), preferred_element_...  10.5 us
  transfers between devices with their start and end apart: 1, of which 0 were waited for; matrix products, arithmetic and copies ran while one was open for 7% of the time, Pallas kernels for 65%

profile of v5, /device:TPU:0, one launch (start us, length us, event | category | flops | bytes accessed | tf_op | source)
XLA Modules:
  0.0 444.2 jit_solution(15541235455099431167)
XLA Ops:
  7.2 0.0 reduce-scatter.2.cloned.1.call-start
  7.2 0.7 convert_element_type.50
  7.9 0.7 stack.9
  8.6 0.7 stack.10
  9.3 0.6 maximum_convert_fusion.gain_ref
  9.9 0.3 multiply_cosine_fusion
  10.2 0.7 select_maximum_fusion.table_ref
  10.9 1.2 broadcast_in_dim.18.place_ref
  12.2 96.8 %forward.1 = (s32[64,128]{1,0:T(8,128)}, bf16[512,1536]{1,0:T(8,128)(2,1)}, f32[128,1536]{1,0:T(8,128)}, bf16[16,64,192]{2,1,0:T(8,128)(2,1)}, bf16[16,64,384]{2...) custom-call(s32[8,128]{1,0:T(8,128)} %broadcast_in_dim.18.place_ref,, ...), custom_call_target="tpu_custom_call" | custom-call | tf_op jit(solution)/shard_map/forward/pallas_call | solution.py:1275
  109.0 0.0 copy-start.6
  109.0 0.0 copy-start.9
  109.0 5.3 %convolution_convert_fusion.3 = bf16[512,1536]{1,0:T(8,128)(2,1)} fusion(bf16[512,1024]{1,0:T(8,128)(2,1)} %get-tuple-element.28, bf16[1024,1536]{1,0:T(8,128)(2,1)} %down_weight_ref.1), kind=kOutput, calls=%fused_computation.6 | convolution fusion | flops 1611399168 | bytes 5767168 | tf_op jit(solution)/shard_map/dot_general | solution.py:21
  114.3 0.0 reduce-scatter.2.cloned.1.call-update
  114.4 0.8 slice.30
  115.2 0.1 reshape_squeeze.3
  115.3 0.1 select_reduce_fusion
  115.4 0.0 copy-done.9
  115.4 0.0 copy-start.5
  115.5 3.5 convolution_convert_fusion.down_ref
  119.0 0.0 copy-start.3
  119.0 3.5 convolution_convert_fusion.2.gate_ref
  122.5 1.6 pad_maximum_fusion.weight_ref
  124.1 0.6 pad_add_fusion.order_ref
  124.7 0.8 fusion.1.half_swap_ref
  125.5 3.5 convolution_convert_fusion.1.up_ref
  129.0 287.4 %backward.1 = (bf16[4320,1536]{1,0:T(8,128)(2,1)}, f32[2,1536]{1,0:T(2,128)}, f32[128,1536]{1,0:T(8,128)}) custom-call(s32[32]{0:T(128)} %pad_add_fusion.order_ref, bf16[1024,1536]{1,0:T(8,128)(2,1)} %convolution_convert_fusion.2.gate_ref, bf16[1024,1536]{1,0:T(8,128)(2,1)} %convolution_convert_fusion.1.up_ref, ...), custom_call_target="tpu_custom_call" | custom-call | tf_op jit(solution)/shard_map/backward/pallas_call | solution.py:927
  416.4 1.4 slice_reduce_fusion
  417.8 2.9 slice_convert_fusion.5
  420.8 4.5 %slice_convert_fusion.3 = (f32[384,1536]{1,0:T(8,128)}, f32[384,1536]{1,0:T(8,128)}) fusion(bf16[4320,1536]{1,0:T(8,128)(2,1)} %get-tuple-element.42), kind=kLoop, calls=%fused_computation.8 | loop fusion | flops 1179648 | bytes 7077888 | tf_op jit(solution)/shard_map/convert_element_type | solution.py:1538
  425.2 9.5 %slice_convert_fusion = (f32[1024,1536]{1,0:T(8,128)}, f32[1024,1536]{1,0:T(8,128)}, f32[1024,1536]{1,0:T(8,128)}) fusion(bf16[4320,1536]{1,0:T(8,128)(2,1)} %get-tuple-element.42), kind=kLoop, calls=%fused_computation.3 | loop fusion | flops 4718592 | bytes 28311552 | tf_op jit(solution)/shard_map/convert_element_type | solution.py:1538
  434.7 1.8 add_convert_fusion
  436.5 0.9 copy.30
  (20 shorter events, 0.1 us)
Async XLA Ops:
  7.2 427.5 %reduce-scatter.2.cloned.1.call-start = ((), (), s32[]{:S(2)}) async-start(), calls=%async_computation.1 | async-start | bytes 1966080 | tf_op jit(solution)/shard_map/reduce_scatter | solution.py:1328
  109.0 6.4 %copy-start.6 = (bf16[512,1536]{1,0:T(8,128)(2,1)S(1)}, bf16[512,1536]{1,0:T(8,128)(2,1)}, u32[]{:S(2)}) copy-start(bf16[512,1536]{1,0:T(8,128)(2,1)} %get-tuple-element.33) | copy-start | bytes 4718596
  109.0 6.4 %copy-start.9 = (bf16[512,1024]{1,0:T(8,128)(2,1)S(1)}, bf16[512,1024]{1,0:T(8,128)(2,1)}, u32[]{:S(2)}) copy-start(bf16[512,1024]{1,0:T(8,128)(2,1)} %get-tuple-element.28) | copy-start | bytes 3145732
  115.4 3.5 copy-start.5
  115.5 3.5 copy-start.8
  119.0 3.5 copy-start
  119.0 3.5 copy-start.2
  119.0 3.5 copy-start.3
  122.5 3.0 copy-start.7
  425.2 9.5 %copy-start.1 = (f32[128,1536]{1,0:T(8,128)S(1)}, f32[128,1536]{1,0:T(8,128)}, u32[]{:S(2)}) copy-start(f32[128,1536]{1,0:T(8,128)} %get-tuple-element.27.hidden_ref) | copy-start | bytes 2359300
  425.2 11.3 %copy-start.4 = (f32[128,1536]{1,0:T(8,128)S(1)}, f32[128,1536]{1,0:T(8,128)}, u32[]{:S(2)}) copy-start(f32[128,1536]{1,0:T(8,128)} %get-tuple-element.66) | copy-start | bytes 2359300
Sparse Core Ops, SparseCore 0:
  114.5 36.6 reduce-scatter.1

commit v6 on v5

--- a/solution.py
+++ b/solution.py
@@ -533,31 +533,40 @@
     rounds,
     block,
     order_ref,
-    gate_ref,
-    up_ref,
-    down_ref,
+    gain_one_ref,
+    gain_two_ref,
+    grad_gate_ref,
+    grad_up_ref,
+    mixed_ref,
+    normed_two_ref,
+    cotangent_ref,
     part_ref,
     hidden_ref,
-    cotangent_ref,
     input_ref,
-    gain_ref,
+    query_weight_ref,
+    key_weight_ref,
+    value_weight_ref,
     output_weight_ref,
+    down_weight_ref,
     attended_ref,
     packed_ref,
     normed_ref,
     cosine_ref,
     sine_ref,
-    half_swap_ref,
-    weight_ref,
     out_ref,
     gain_out_ref,
     input_grad_ref,
+    layer_output_ref,
     own,
     spine_in,
     line_in,
+    grad_gate,
+    grad_up,
+    mixed,
+    normed_two,
+    cotangents,
     part,
     hidden,
-    cotangent,
     inputs,
     output_weight,
     attended,
@@ -615,7 +624,8 @@
     me = place.ctx
     depth, side = lax.div(me, 2), lax.rem(me, 2)
     other_side = me + 1 - 2 * side
-    hidden_units = gate_ref.shape[0]
+    hidden_units = mixed.shape[1]
+    width = own.shape[1]
     base = 3 * hidden_units
     spare = rounds * ROUND_ROWS - base - 3 * WIDE
     length = q0.shape[0]
@@ -625,38 +635,66 @@
     scale = 1.0 / math.sqrt(HEAD_DIM)
 
     fetches = {}
-    for key, (source, target) in enumerate(
-        (
-            (part_ref, part),
-            (gate_ref, own.at[pl.ds(0, hidden_units)]),
-            (up_ref, own.at[pl.ds(hidden_units, hidden_units)]),
-            (hidden_ref, hidden),
-            (cotangent_ref, cotangent),
-            (output_weight_ref, output_weight),
-            (packed_ref, packed),
-            (attended_ref, attended),
-            (down_ref, own.at[pl.ds(2 * hidden_units, hidden_units)]),
-            (normed_ref, normed),
-            (cosine_ref, cosine),
-            (sine_ref, sine),
-            (half_swap_ref, half_swap),
-            (weight_ref, weight),
-            (input_ref, inputs),
-        )
-    ):
-        fetches[id(source)] = pltpu.make_async_copy(source, target, fetch_sem.at[key])
+
+    def fetch_all(source, *copies):
+        first = sum(len(group) for group in fetches.values())
+        fetches[id(source)] = [
+            pltpu.make_async_copy(*copy, fetch_sem.at[first + index])
+            for index, copy in enumerate(copies or ())
+        ]
+        for copy in fetches[id(source)]:
+            copy.start()
 
     def fetch(*sources):
         for source in sources:
-            fetches[id(source)].wait()
-
-    for copy in fetches.values():
-        copy.start()
-    if spare:
-        own[base + 3 * WIDE :, :] = jnp.zeros((spare, own.shape[1]), own.dtype)
+            for copy in fetches[id(source)]:
+                copy.wait()
+
+    for source, target in (
+        (part_ref, part),
+        (grad_gate_ref, grad_gate),
+        (normed_two_ref, normed_two),
+        (grad_up_ref, grad_up),
+        (mixed_ref, mixed),
+        (cotangent_ref, cotangents),
+        (hidden_ref, hidden),
+        (packed_ref, packed),
+        (down_weight_ref, own.at[pl.ds(base, hidden_units)]),
+        (output_weight_ref, output_weight),
+        (attended_ref, attended),
+        (normed_ref, normed),
+        (cosine_ref, cosine),
+        (sine_ref, sine),
+        (input_ref, inputs),
+    ):
+        fetch_all(source, (source, target))
+    for source, first, count in (
+        (query_weight_ref, 0, PAIR),
+        (key_weight_ref, PAIR, HEAD_DIM),
+        (value_weight_ref, PAIR + HEAD_DIM, HEAD_DIM),
+    ):
+        fetch_all(
+            source,
+            *(
+                (source.at[pl.ds(head * count, count)], weight.at[head, pl.ds(first, count)])
+                for head in range(2)
+            ),
+        )
+    gain_one = gain_one_ref[...].astype(jnp.float32).reshape(1, -1)
+    gain_two = gain_two_ref[...].astype(jnp.float32).reshape(1, -1)
+    lanes = (WIDE, WIDE)
+    row_lane = lax.broadcasted_iota(jnp.int32, lanes, 0)
+    column_lane = lax.broadcasted_iota(jnp.int32, lanes, 1)
+    half = HEAD_DIM // 2
+    inner = lax.rem(column_lane, HEAD_DIM)
+    partner_lane = column_lane + jnp.where(inner < half, half, -half)
+    half_swap[...] = jnp.where(row_lane == partner_lane, 1.0, 0.0).astype(jnp.bfloat16)
     place.greet()
     fetch(part_ref)
     fold_two = Fold(place, part, near.at[0], send.at[0], far.at[0], fold_send.at[0], fold_recv.at[0])
+    fold_output = Fold(
+        place, part, near.at[0], send.at[0], far.at[0], fold_send.at[0], fold_recv.at[0]
+    )
     fold_one = Fold(place, part, near.at[1], send.at[1], far.at[1], fold_send.at[1], fold_recv.at[1])
     gather = Gather(place, branch, gather_send, gather_recv)
     swap_heads = Swap(place, heads_out, heads_in, swap_send.at[0], swap_recv.at[0], halves)
@@ -664,7 +702,23 @@
     spread_near = Spread(gain_near, place.row, 4, near_fsdp, near_send, near_recv)
     spread_far = Spread(gain_far, me, 8, peer, far_send, far_recv)
     fold_two.start()
-    fetch(gate_ref, up_ref, down_ref)
+
+    def stage_feed(first):
+        sides = ((grad_gate, normed_two), (grad_up, normed_two), (mixed, cotangents))
+        left, right = sides[first // hidden_units]
+        if first == 0:
+            fetch(grad_gate_ref, normed_two_ref)
+        elif first == hidden_units:
+            fetch(grad_up_ref)
+
+        @pl.loop(0, 2)
+        def _(index):
+            start = first % hidden_units + index * 256
+            columns = pl.ds(pl.multiple_of(start, 256), 256)
+            rows = pl.ds(pl.multiple_of(first + index * 256, 256), 256)
+            own[rows, :] = product_rows(left[:, columns], right[...]).astype(jnp.bfloat16)
+
+    stage_feed(0)
 
     spine_sems = (spine_up, spine_got, spine_down, spine_back)
     line_sems = (line_up, line_got, line_down, line_back)
@@ -709,9 +763,10 @@
             grad = fold_two.rows(piece * 16, 16)
             unit, back = norm_back_rows(hidden[span, :], None)
             gain_part[1] += (grad * unit).reshape(2, 8, -1).sum(axis=0)
-            total = cotangent[span, :].astype(jnp.float32) + back(grad * gain_ref[1:2, :])
+            here = rows_at(place.row * TILE + piece * 16, 16)
+            total = cotangents[here, :].astype(jnp.float32) + back(grad * gain_two)
             grad_hidden[span, :] = total
-            branch[rows_at(place.row * TILE + piece * 16, 16), :] = total.astype(jnp.bfloat16)
+            branch[here, :] = total.astype(jnp.bfloat16)
 
         gather.start()
 
@@ -784,7 +839,7 @@
         swap_packed.start_all()
 
     def stage_turn():
-        fetch(cosine_ref, sine_ref, half_swap_ref, weight_ref)
+        fetch(cosine_ref, sine_ref, query_weight_ref, key_weight_ref, value_weight_ref)
         swap_packed.arrive()
 
         @pl.loop(0, 4)
@@ -828,7 +883,7 @@
             grad = fold_one.rows(piece * 16, 16)
             unit, back = norm_back_rows(inputs[span, :].astype(jnp.float32), None)
             gain_part[0] += (grad * unit).reshape(2, 8, -1).sum(axis=0)
-            input_grad_ref[span, :] = grad_hidden[span, :] + back(grad * gain_ref[0:1, :])
+            input_grad_ref[span, :] = grad_hidden[span, :] + back(grad * gain_one)
 
         gain_near[place.row] = jnp.sum(gain_part[...], axis=1)
         spread_near.start()
@@ -837,14 +892,49 @@
         gain_far[me] = spread_near.total()
         spread_far.start()
 
+    def stage_output():
+        fetch(down_weight_ref)
+
+        @pl.loop(0, 4)
+        def _(sequence):
+            span = rows_at(sequence * TILE, TILE)
+            part[span, :] = product(
+                mixed[span, :], own[base : base + hidden_units, :]
+            ).astype(jnp.bfloat16)
+
+    def stage_output_sum():
+        fold_output.arrive()
+
+        @pl.loop(0, TILE // 16)
+        def _(piece):
+            span = rows_at(piece * 16, 16)
+            total = hidden[span, :] + fold_output.rows(piece * 16, 16)
+            layer_output_ref[span, :] = total.astype(jnp.bfloat16)
+
+    def stage_clear():
+        if spare:
+            own[base + 3 * WIDE :, :] = jnp.zeros((spare, width), own.dtype)
+
+    units = 2 * 256
     stages = [
         (0, fold_two.relay),
+        (0, functools.partial(stage_feed, units)),
         (0, stage_sort),
+        (1, functools.partial(stage_feed, 2 * units)),
+        (1, functools.partial(stage_feed, 3 * units)),
+        (2, lambda: fetch(mixed_ref)),
         (2, stage_norm_two),
         (3, gather.relay),
+        (3, functools.partial(stage_feed, 4 * units)),
+        (3, stage_output),
         (4, stage_heads),
+        (4, fold_output.start),
+        (5, fold_output.relay),
+        (5, functools.partial(stage_feed, 5 * units)),
         (5, stage_output_grad),
+        (5, stage_clear),
         (6, stage_sort_grads),
+        (8, stage_output_sum),
     ]
     stages += [(6 + index, functools.partial(stage_attention, index)) for index in range(tiles)]
     now = 6 + tiles - 1
@@ -907,18 +997,21 @@
     gain_out_ref[...] = spread_far.total()
 
 
-def backward(order, grads, part, hidden, cotangent, inputs, gains, output_weight, attended,
-             packed, normed, cosine, sine, half_swap, weight, block, key):
+def backward(order, gain_one, gain_two, grad_gate, grad_up, mixed, normed_two, cotangents, part,
+             hidden, inputs, query_weight, key_weight, value_weight, output_weight, down_weight,
+             attended, packed, normed, cosine, sine, key):
     width = hidden.shape[1]
-    rows = 3 * grads[0].shape[0] + 3 * WIDE
+    rows = 3 * mixed.shape[1] + 3 * WIDE
     rounds = -(-rows // ROUND_ROWS)
+    block = packed.shape[1]
     length = packed.shape[0] * block
     dma = pltpu.SemaphoreType.DMA
     low, full = jnp.bfloat16, jnp.float32
     any_spec = pl.BlockSpec(memory_space=pl.ANY)
     operands = (
-        order, *grads, part, hidden, cotangent, inputs, gains, output_weight, attended,
-        packed, normed, cosine, sine, half_swap, weight,
+        order, gain_one, gain_two, grad_gate, grad_up, mixed, normed_two, cotangents, part,
+        hidden, inputs, query_weight, key_weight, value_weight, output_weight, down_weight,
+        attended, packed, normed, cosine, sine,
     )
 
     def like(array):
@@ -930,19 +1023,19 @@
             jax.ShapeDtypeStruct((rounds * ROUND_ROWS, width), low),
             jax.ShapeDtypeStruct((2, width), full),
             jax.ShapeDtypeStruct((TILE, width), full),
+            jax.ShapeDtypeStruct((TILE, width), low),
         ),
-        in_specs=[pl.BlockSpec(memory_space=pltpu.SMEM)]
-        + [any_spec] * 7
-        + [vmem()]
-        + [any_spec] * 8,
-        out_specs=(any_spec, vmem(), vmem()),
+        in_specs=[pl.BlockSpec(memory_space=pltpu.SMEM)] + [vmem()] * 2 + [any_spec] * 18,
+        out_specs=(any_spec, vmem(), vmem(), vmem()),
         scratch_shapes=[
             pltpu.VMEM((rounds * ROUND_ROWS, width), low),
             pltpu.VMEM((3, RING * SPINE_ROWS, width), low),
             pltpu.VMEM((3, RING * LINE_ROWS, width), low),
-            like(part), like(hidden), like(cotangent), like(inputs), like(output_weight),
+            like(grad_gate), like(grad_up), like(mixed), like(normed_two), like(cotangents),
+            like(part), like(hidden), like(inputs), like(output_weight),
             like(attended), like(packed), like(normed), like(cosine), like(sine),
-            like(half_swap), like(weight),
+            pltpu.VMEM((WIDE, WIDE), low),
+            pltpu.VMEM((2, WIDE, width), low),
             pltpu.VMEM((2, 2, TILE, width), low),
             pltpu.VMEM((2, TILE, width), low),
             pltpu.VMEM((2, TILE, width), low),
@@ -961,7 +1054,7 @@
             pltpu.VMEM((2, 4 * TILE, WIDE), low),
             pltpu.VMEM((4, 2, width), full),
             pltpu.VMEM((8, 2, width), full),
-            dma((15,)),
+            dma((21,)),
             dma((RING,)), dma((3, RING)), dma((3, RING)), dma((RING,)),
             dma((RING,)), dma((RING,)),
             dma((RING,)), dma((3, RING)), dma((3, RING)), dma((RING,)),
@@ -981,7 +1074,8 @@
     block,
     place_ref,
     table_ref,
-    gain_ref,
+    gain_one_ref,
+    gain_two_ref,
     input_ref,
     cotangent_ref,
     query_weight_ref,
@@ -1094,7 +1188,11 @@
     fetch_all("gate", (gate_weight_ref, gate_weight))
     fetch_all("up", (up_weight_ref, up_weight))
     fetch_all("down", (down_weight_ref, down_weight))
-    places[pl.ds(pl.multiple_of(place.row * 8, 8), 8), :] = place_ref[...]
+    places[pl.ds(pl.multiple_of(place.row * 8, 8), 8), :] = jnp.broadcast_to(
+        place_ref[...], (8, place_ref.shape[1])
+    )
+    gain_one = gain_one_ref[...].astype(jnp.float32).reshape(1, -1)
+    gain_two = gain_two_ref[...].astype(jnp.float32).reshape(1, -1)
     tables[own_rows, :] = table_ref[...]
     gather_places = Gather(place, places, gather_send.at[0], gather_recv.at[0], 8)
     gather_tables = Gather(place, tables, gather_send.at[1], gather_recv.at[1])
@@ -1120,7 +1218,7 @@
         def _(piece):
             span = rows_at(base + piece * 16, 16)
             rows = inputs[span, :].astype(jnp.float32)
-            normed_one[span, :] = (rows * rms_scale(rows) * gain_ref[0:1, :]).astype(jnp.bfloat16)
+            normed_one[span, :] = (rows * rms_scale(rows) * gain_one).astype(jnp.bfloat16)
 
         span = rows_at(base, pair_rows)
         low_cosine, low_sine = tables[span, :half], tables[span, half:HEAD_DIM]
@@ -1212,7 +1310,7 @@
         own = rows_at(place.row * TILE + piece * 16, 16)
         rows = inputs[own, :].astype(jnp.float32) + fold.rows(piece * 16, 16)
         hidden[span, :] = rows
-        normed_two[own, :] = (rows * rms_scale(rows) * gain_ref[1:2, :]).astype(jnp.bfloat16)
+        normed_two[own, :] = (rows * rms_scale(rows) * gain_two).astype(jnp.bfloat16)
 
     gather_two.start()
     store(hidden, hidden_out)
@@ -1258,7 +1356,7 @@
         copy.wait()
 
 
-def forward(places, table, gains, inputs, cotangent, query_weight, key_weight, value_weight,
+def forward(places, table, gain_one, gain_two, inputs, cotangent, query_weight, key_weight, value_weight,
             output_weight, gate_weight, up_weight, down_weight, length, block, key):
     width = inputs.shape[1]
     hidden_units = gate_weight.shape[0]
@@ -1283,7 +1381,7 @@
             out((rows, hidden_units), low), out((rows, hidden_units), low),
             out((rows, hidden_units), low),
         ),
-        in_specs=[vmem()] * 3 + [any_spec] * 9,
+        in_specs=[vmem()] * 4 + [any_spec] * 9,
         out_specs=(vmem(),) + (any_spec,) * 12,
         scratch_shapes=[
             pltpu.VMEM((32, 128), jnp.int32),
@@ -1316,8 +1414,70 @@
             collective_id=key, has_side_effects=True, vmem_limit_bytes=63 * 2**20
         ),
         name="forward",
-    )(places, table, gains, inputs, cotangent, query_weight, key_weight, value_weight,
+    )(places, table, gain_one, gain_two, inputs, cotangent, query_weight, key_weight, value_weight,
       output_weight, gate_weight, up_weight, down_weight)
+
+
+def widen_kernel(plan, source, *refs):
+    targets, (low, full, load_sem, store_sem) = refs[:-4], refs[-4:]
+    slots = low.shape[0]
+    loads, stores = [], []
+    for index, (first, which, target_row, chunk) in enumerate(plan):
+        slot = index % slots
+        span = pl.ds(0, chunk)
+        loads.append(
+            pltpu.make_async_copy(
+                source.at[pl.ds(first, chunk)], low.at[slot, span], load_sem.at[slot]
+            )
+        )
+        stores.append(
+            pltpu.make_async_copy(
+                full.at[slot, span],
+                targets[which].at[pl.ds(target_row, chunk)],
+                store_sem.at[slot],
+            )
+        )
+    for load in loads[:slots]:
+        load.start()
+    for index, (load, store) in enumerate(zip(loads, stores)):
+        slot = index % slots
+        load.wait()
+        if index >= slots:
+            stores[index - slots].wait()
+
+        @pl.loop(0, plan[index][3] // 16)
+        def _(piece):
+            span = rows_at(piece * 16, 16)
+            full[slot, span, :] = low[slot, span, :].astype(jnp.float32)
+
+        store.start()
+        if index + slots < len(plan):
+            loads[index + slots].start()
+    for store in stores[-slots:]:
+        store.wait()
+
+
+def widen(values, counts):
+    slots, width, first, plan = 6, values.shape[1], 0, []
+    for which, count in enumerate(counts):
+        chunk = math.gcd(count, 256) if count % 192 else 192
+        plan += [(first + row, which, row, chunk) for row in range(0, count, chunk)]
+        first += count
+    any_spec = pl.BlockSpec(memory_space=pl.ANY)
+    return pl.pallas_call(
+        functools.partial(widen_kernel, plan),
+        out_shape=tuple(jax.ShapeDtypeStruct((count, width), jnp.float32) for count in counts),
+        in_specs=[any_spec],
+        out_specs=(any_spec,) * len(counts),
+        scratch_shapes=[
+            pltpu.VMEM((slots, 256, width), values.dtype),
+            pltpu.VMEM((slots, 256, width), jnp.float32),
+            pltpu.SemaphoreType.DMA((slots,)),
+            pltpu.SemaphoreType.DMA((slots,)),
+        ],
+        compiler_params=pltpu.CompilerParams(vmem_limit_bytes=63 * 2**20),
+        name="widen",
+    )(values)
 
 
 def gather_rows(values):
@@ -1489,7 +1649,7 @@
     up_weight,
     down_weight,
 ):
-    gains = jnp.stack([attention_gain, feedforward_gain]).astype(jnp.float32)
+    gain_one, gain_two = attention_gain, feedforward_gain
     block = TILE // 2
     length = TILE * 8
     cosine, sine = rotary_tables(positions)
@@ -1499,44 +1659,22 @@
         places, part, hidden, attended, packed, normed_one, wide_cosine, wide_sine,
         cotangents, normed_two, mixed, grad_gate, grad_up,
     ) = forward(
-        jnp.broadcast_to(positions[None, :], (8, TILE)), table, gains, inputs, cotangent,
-        query_weight, key_weight, value_weight, output_weight, gate_weight, up_weight,
-        down_weight, length, block, 1,
+        positions[None, :], table, gain_one, gain_two, inputs, cotangent, query_weight,
+        key_weight, value_weight, output_weight, gate_weight, up_weight, down_weight, length,
+        block, 1,
     )
     starts = places.reshape(8, 8, TILE)[:, 0, ::block].reshape(-1) // block
     slots = jnp.arange(length // block, dtype=jnp.int32)
     found = jnp.where(starts[None, :] == slots[:, None], slots[None, :], 0)
     order = jnp.concatenate([jnp.sum(found, axis=1), starts]).astype(jnp.int32)
-    half = HEAD_DIM // 2
-    lanes = jnp.arange(WIDE, dtype=jnp.int32)
-    partner_lane = lanes + jnp.where(lanes % HEAD_DIM < half, half, -half)
-    half_swap = jnp.logical_and(
-        lanes[:, None] == partner_lane[None, :], lanes[None, :] < PAIR + HEAD_DIM
-    ).astype(jnp.bfloat16)
-    width = inputs.shape[1]
-    weight = jnp.concatenate(
-        [
-            query_weight.reshape(2, PAIR, width),
-            key_weight.reshape(2, HEAD_DIM, width),
-            value_weight.reshape(2, HEAD_DIM, width),
-        ],
-        axis=1,
-    )
-    layer_output = (hidden + scatter_rows(product(mixed, down_weight))).astype(jnp.bfloat16)
-    ff_grads = (
-        product_rows(grad_gate, normed_two).astype(jnp.bfloat16),
-        product_rows(grad_up, normed_two).astype(jnp.bfloat16),
-        product_rows(mixed, cotangents).astype(jnp.bfloat16),
-    )
-    summed, gain_sums, input_grad = backward(
-        order, ff_grads, part, hidden, cotangent, inputs, gains, output_weight, attended,
-        packed, normed_one, wide_cosine, wide_sine, half_swap, weight, block, 5,
-    )
-    parts, start = [], 0
-    for grad in (gate_weight, up_weight, down_weight, query_weight, key_weight, value_weight,
-                 output_weight):
-        parts.append(summed[start : start + grad.shape[0]].astype(jnp.float32))
-        start += grad.shape[0]
+    summed, gain_sums, input_grad, layer_output = backward(
+        order, gain_one, gain_two, grad_gate, grad_up, mixed, normed_two, cotangents, part,
+        hidden, inputs, query_weight, key_weight, value_weight, output_weight, down_weight,
+        attended, packed, normed_one, wide_cosine, wide_sine, 5,
+    )
+    owners = (gate_weight, up_weight, down_weight, query_weight, key_weight, value_weight,
+              output_weight)
+    parts = widen(summed, [owner.shape[0] for owner in owners])
     return (layer_output, input_grad, gain_sums[0], *parts[3:], gain_sums[1], *parts[:3])
 
 

time: 445 us -> 406 us (0.912)
  other arithmetic: 24.1 us -> 2.42 us
  matrix products: 15.8 us -> 0 us
  Pallas kernels: 384 us -> 398 us
  between operations: 14.2 us -> 0.7 us
    convert_element_type x6 -> x0, other arithmetic: 20.1 us -> none  [the longest x3 16.8 us: per_device_by_head(): parts.append(summed[start:start + grad.shape[0]].astype(jnp.float32))]
    dot_general x4 -> x0, matrix products: 15.8 us -> none  [the longest x3 10.5 us: product_rows(): lax.dot_general(left, right, (((0,), (0,)), ((), ())), preferred_element_...]
    pallas_call x0 -> x1, Pallas kernels: none -> 12.8 us  [widen(): pl.pallas_call(functools.partial(widen_kernel, plan), out_shape=tuple((ja...]
  transfers between devices with their start and end apart: 1 -> 0, of which waited for: 0 -> 0; matrix products, arithmetic and copies ran while one was open for 7% -> 0% of each run, Pallas kernels for 65% -> 0%
where the time goes in v6:
time: 406 us
  Pallas kernels  398 us (98%)
  local copies, waits for them, and re-layouts  4.21 us (1%)
    pallas_call x1, Pallas kernels, backward(): pl.pallas_call(functools.partial(backward_kernel, rounds, block), out_sha...  289 us
    pallas_call x1, Pallas kernels, forward(): pl.pallas_call(functools.partial(forward_kernel, block), out_shape=(out((...  96.8 us
    pallas_call x1, Pallas kernels, widen(): pl.pallas_call(functools.partial(widen_kernel, plan), out_shape=tuple((ja...  12.8 us

profile of v6, /device:TPU:0, one launch (start us, length us, event | category | flops | bytes accessed | tf_op | source)
XLA Modules:
  0.0 405.6 jit_solution(6301337060549559439)
XLA Ops:
  0.6 0.7 convert_element_type.5
  1.3 0.3 multiply_cosine_fusion
  1.6 0.7 select_maximum_fusion.table_ref
  2.4 96.8 %forward.1 = (s32[64,128]{1,0:T(8,128)}, bf16[512,1536]{1,0:T(8,128)(2,1)}, f32[128,1536]{1,0:T(8,128)}, bf16[16,64,192]{2,1,0:T(8,128)(2,1)}, bf16[16,64,384]{2...) custom-call(s32[1,128]{1,0:T(1,128)} %bitcast.6, ...), custom_call_target="tpu_custom_call" | custom-call | tf_op jit(solution)/shard_map/forward/pallas_call | solution.py:1373
  99.1 0.8 slice.9
  100.0 0.1 reshape_squeeze.3
  100.1 0.1 select_reduce_fusion
  100.2 0.6 pad_add_fusion.order_ref
  100.8 288.7 %backward.1 = (bf16[4320,1536]{1,0:T(8,128)(2,1)}, f32[2,1536]{1,0:T(2,128)}, f32[128,1536]{1,0:T(8,128)}, bf16[128,1536]{1,0:T(8,128)(2,1)}) custom-call(s32[32]{0:T(128)} %pad_add_fusion.order_ref, bf16[1536]{0:T(1024)(128)(2,1)} %gain_one_ref.3, bf16[1536]{0:T(1024)(128)(2,1)} %gain_two_ref.3, bf16[512,1024]{1,0:T(8,128)(2,1)} %get-tuple-element.36.grad_gate_ref, ...), custom_call_target="tpu_custom_call" | custom-call | tf_op jit(solution)/shard_map/backward/pallas_call | solution.py:1020
  389.5 0.0 copy-start.1
  389.5 0.0 copy-start
  389.5 12.8 %widen.1 = (f32[1024,1536]{1,0:T(8,128)}, f32[1024,1536]{1,0:T(8,128)}, f32[1024,1536]{1,0:T(8,128)}, f32[384,1536]{1,0:T(8,128)}, f32[192,1536]{1,0:T(8,128)}, ...) custom-call(bf16[4320,1536]{1,0:T(8,128)(2,1)} %get-tuple-element.51.source), custom_call_target="tpu_custom_call" | custom-call | tf_op jit(solution)/shard_map/widen/pallas_call | solution.py:1467
  402.3 0.0 copy-done.1
  402.3 0.6 slice_reduce_fusion
  403.0 1.8 copy.31
  404.7 0.0 copy-done
  404.7 0.9 copy.32
  (2 shorter events, 0.0 us)
Async XLA Ops:
  389.5 12.8 %copy-start.1 = (f32[2,1536]{1,0:T(2,128)S(1)}, f32[2,1536]{1,0:T(2,128)}, u32[]{:S(2)}) copy-start(f32[2,1536]{1,0:T(2,128)} %get-tuple-element.50) | copy-start | bytes 36868
  389.5 15.2 %copy-start = (f32[128,1536]{1,0:T(8,128)S(1)}, f32[128,1536]{1,0:T(8,128)}, u32[]{:S(2)}) copy-start(f32[128,1536]{1,0:T(8,128)} %get-tuple-element.75) | copy-start | bytes 2359300

commit v7 on v6

--- a/solution.py
+++ b/solution.py
@@ -194,11 +194,14 @@
     return dict(device_id={"ctx": ctx_index}, device_id_type=pl.DeviceIdType.MESH)
 
 
-SPINE_ROWS = 48
-LINE_ROWS = 64
+SPINE_ROWS = 32
+LINE_ROWS = 32
 ROUND_ROWS = 2 * SPINE_ROWS + LINE_ROWS
-LEAD = 2
-RING = 12
+LEAD = 4
+HOP = 2
+FEED = (1, 3, 5, 8)
+CHAIN = (0, 4, 6, 8, 10, 12, 19, 22, 26, 28)
+RING = 20
 TILE = 128
 PAIR = (HEADS // KV_HEADS) * HEAD_DIM
 WIDE = PAIR + 2 * HEAD_DIM
@@ -512,10 +515,20 @@
     return spread * (1.0 / jnp.sum(spread, axis=-1, keepdims=True))
 
 
-def sort_blocks(slot_ref, source, targets):
-    block_total, block, _ = source.shape
+def pack_pairs(blocks):
+    half = blocks.shape[1] // 2
+    return jnp.concatenate([blocks[:, :half], blocks[:, half:]], axis=-1)
+
+
+def unpack_pairs(blocks):
+    return jnp.concatenate([blocks[..., :PAIR], blocks[..., PAIR:]], axis=-2)
+
+
+def sort_blocks(slot_ref, source, targets, opened=lambda rows: rows):
+    block_total = source.shape[0]
+    block = targets[0].shape[0] // block_total
     for index in range(block_total):
-        rows = source[slot_ref[index]]
+        rows = opened(source[slot_ref[index]])
         start = 0
         for target in targets:
             width = target.shape[-1]
@@ -710,6 +723,8 @@
             fetch(grad_gate_ref, normed_two_ref)
         elif first == hidden_units:
             fetch(grad_up_ref)
+        elif first == 2 * hidden_units:
+            fetch(mixed_ref)
 
         @pl.loop(0, 2)
         def _(index):
@@ -719,6 +734,7 @@
             own[rows, :] = product_rows(left[:, columns], right[...]).astype(jnp.bfloat16)
 
     stage_feed(0)
+    stage_feed(2 * 256)
 
     spine_sems = (spine_up, spine_got, spine_down, spine_back)
     line_sems = (line_up, line_got, line_down, line_back)
@@ -780,9 +796,9 @@
             rows = branch[rows_at(sequence * TILE, TILE), :]
             grads = product_back(rows, output_weight[...]).astype(jnp.bfloat16)
             for head in range(2):
-                heads_out[pl.ds((2 * sequence + head) * halves, halves)] = grads[
-                    :, head * PAIR : (head + 1) * PAIR
-                ].reshape(halves, block, PAIR)
+                heads_out[pl.ds((2 * sequence + head) * halves, halves)] = pack_pairs(
+                    grads[:, head * PAIR : (head + 1) * PAIR].reshape(halves, block, PAIR)
+                )
 
         swap_heads.start_all()
 
@@ -797,7 +813,7 @@
                 attended[(2 * index + head) * halves : (2 * index + head + 1) * halves]
                 for index in range(4)
             ]
-            rows = jnp.concatenate(rows, axis=0).reshape(4 * TILE, PAIR)
+            rows = unpack_pairs(jnp.concatenate(rows, axis=0)).reshape(4 * TILE, PAIR)
             first_row = base + 2 * WIDE + head * PAIR
             for first in range(0, own.shape[1], 512):
                 columns = slice(first, first + 512)
@@ -807,7 +823,7 @@
 
     def stage_sort_grads():
         swap_heads.arrive()
-        sort_blocks(order_ref, heads_in, (g0, g1))
+        sort_blocks(order_ref, heads_in, (g0, g1), unpack_pairs)
         dk[...] = jnp.zeros_like(dk)
         dv[...] = jnp.zeros_like(dv)
 
@@ -917,38 +933,37 @@
 
     units = 2 * 256
     stages = [
-        (0, fold_two.relay),
-        (0, functools.partial(stage_feed, units)),
-        (0, stage_sort),
-        (1, functools.partial(stage_feed, 2 * units)),
-        (1, functools.partial(stage_feed, 3 * units)),
-        (2, lambda: fetch(mixed_ref)),
-        (2, stage_norm_two),
-        (3, gather.relay),
-        (3, functools.partial(stage_feed, 4 * units)),
-        (3, stage_output),
-        (4, stage_heads),
-        (4, fold_output.start),
-        (5, fold_output.relay),
-        (5, functools.partial(stage_feed, 5 * units)),
-        (5, stage_output_grad),
-        (5, stage_clear),
-        (6, stage_sort_grads),
-        (8, stage_output_sum),
+        (FEED[index], functools.partial(stage_feed, (index + 2) * units)) for index in range(4)
     ]
-    stages += [(6 + index, functools.partial(stage_attention, index)) for index in range(tiles)]
-    now = 6 + tiles - 1
     stages += [
-        (now, stage_unsort),
-        (now + 2, stage_turn),
-        (now + 3, fold_one.relay),
-        (now + 3, functools.partial(stage_projection_grads, 0)),
-        (now + 4, functools.partial(stage_projection_grads, 1)),
-        (now + 5, stage_norm_one),
-        (now + 6, stage_gain),
+        (CHAIN[0], fold_two.relay),
+        (CHAIN[0], stage_sort),
+        (CHAIN[1], stage_norm_two),
+        (CHAIN[2], gather.relay),
+        (CHAIN[2], stage_output),
+        (CHAIN[3], stage_heads),
+        (CHAIN[3], fold_output.start),
+        (CHAIN[4], fold_output.relay),
+        (CHAIN[4], stage_output_grad),
+        (CHAIN[4], stage_clear),
+        (CHAIN[5], stage_sort_grads),
     ]
-    needed = base // ROUND_ROWS - LEAD
-    assert now + 4 < needed
+    stages += [
+        (CHAIN[5] + index, functools.partial(stage_attention, index)) for index in range(tiles)
+    ]
+    stages += [
+        (CHAIN[5] + tiles - 1, stage_unsort),
+        (CHAIN[5] + tiles, stage_output_sum),
+        (CHAIN[6], stage_turn),
+        (CHAIN[7], fold_one.relay),
+        (CHAIN[7], functools.partial(stage_projection_grads, 0)),
+        (CHAIN[7] + 1, functools.partial(stage_projection_grads, 1)),
+        (CHAIN[8], stage_norm_one),
+        (CHAIN[9], stage_gain),
+    ]
+    assert CHAIN[7] + 1 < base // ROUND_ROWS - LEAD
+    for index in range(4):
+        assert FEED[index] < (index + 2) * units // ROUND_ROWS - LEAD
 
     for index in range(LEAD):
         leaf_copy(index).start()
@@ -968,23 +983,23 @@
         def _():
             leaf_copy(now + LEAD).start()
 
-        rising = spine(now - 3 + off_center)
+        rising = spine(now - HOP * (3 - off_center))
         pl.when(valid(rising.index))(rising.rise)
 
         @pl.loop(0, 5)
         def _(age):
-            tree = line(now - age)
+            tree = line(now - HOP * age)
             pl.when(jnp.logical_and(valid(tree.index), tree.rise_age == age))(tree.rise)
 
-        falling = spine(now - 3 - off_center)
+        falling = spine(now - HOP * (3 + off_center))
         pl.when(valid(falling.index))(falling.fall)
 
         @pl.loop(4, 9)
         def _(age):
-            tree = line(now - age)
+            tree = line(now - HOP * age)
             pl.when(jnp.logical_and(valid(tree.index), tree.fall_age == age))(tree.fall)
 
-        leaf_fall = now - 4 - far_side
+        leaf_fall = now - HOP * (4 + far_side)
 
         @pl.when(valid(leaf_fall))
         def _():
@@ -1042,8 +1057,8 @@
             pltpu.VMEM((4 * TILE, width), low),
             pltpu.VMEM((TILE, width), full),
             pltpu.VMEM((2, 8, width), full),
-            pltpu.VMEM((length // block, block, PAIR), low),
-            pltpu.VMEM((length // block, block, PAIR), low),
+            pltpu.VMEM((length // block, block // 2, 2 * PAIR), low),
+            pltpu.VMEM((length // block, block // 2, 2 * PAIR), low),
         ]
         + [pltpu.VMEM((length, HEAD_DIM), low)] * 6
         + [pltpu.VMEM((length // block, block, PAIR), full)]
@@ -1281,7 +1296,9 @@
         rows = lax.broadcasted_iota(jnp.int32, (length, tile), 0)
         chosen = jnp.where(rows == place_row(first // TILE, tile // TILE), 1.0, 0.0)
         moved = product_rows(chosen.astype(jnp.bfloat16), result[...]).astype(jnp.bfloat16)
-        heads_from[first // block : (first + tile) // block] = moved.reshape(-1, block, PAIR)
+        heads_from[first // block : (first + tile) // block] = pack_pairs(
+            moved.reshape(-1, block, PAIR)
+        )
     swap_heads.start_all()
     gather_cotangents.first()
     gather_cotangents.relay()
@@ -1293,7 +1310,8 @@
     def _(sequence):
         total = None
         for head in range(2):
-            rows = heads[pl.ds((2 * sequence + head) * halves, halves)].reshape(TILE, PAIR)
+            rows = heads[pl.ds((2 * sequence + head) * halves, halves)]
+            rows = unpack_pairs(rows).reshape(TILE, PAIR)
             term = product(rows, output_weight[head * PAIR : (head + 1) * PAIR, :])
             total = term if total is None else total + term
         part[rows_at(sequence * TILE, TILE), :] = total.astype(jnp.bfloat16)
@@ -1375,7 +1393,7 @@
         out_shape=(
             out((64, 128), jnp.int32),
             out(wide, low), out((TILE, width), full),
-            out((blocks, block, PAIR), low), out((blocks, block, WIDE), low),
+            out((blocks, block // 2, 2 * PAIR), low), out((blocks, block, WIDE), low),
             out(wide, low), out((rows, WIDE), full), out((rows, WIDE), full),
             out(wide, low), out(wide, low),
             out((rows, hidden_units), low), out((rows, hidden_units), low),
@@ -1398,7 +1416,8 @@
         + [pltpu.VMEM((length, HEAD_DIM), low)] * 4
         + [
             pltpu.VMEM((length, PAIR), low),
-            pltpu.VMEM((blocks, block, PAIR), low), pltpu.VMEM((blocks, block, PAIR), low),
+            pltpu.VMEM((blocks, block // 2, 2 * PAIR), low),
+            pltpu.VMEM((blocks, block // 2, 2 * PAIR), low),
             pltpu.VMEM(wide, low),
             pltpu.VMEM((2, TILE, width), low),
             pltpu.VMEM((TILE, width), low), pltpu.VMEM((TILE, width), low),

time: 406 us -> 384 us (0.946)
  Pallas kernels: 398 us -> 377 us
    pallas_call x1, Pallas kernels: 289 us -> 270 us  [backward(): pl.pallas_call(functools.partial(backward_kernel, rounds, block), out_sha...]
where the time goes in v7:
time: 384 us
  Pallas kernels  377 us (98%)
  local copies, waits for them, and re-layouts  4.21 us (1%)
    pallas_call x1, Pallas kernels, backward(): pl.pallas_call(functools.partial(backward_kernel, rounds, block), out_sha...  270 us
    pallas_call x1, Pallas kernels, forward(): pl.pallas_call(functools.partial(forward_kernel, block), out_shape=(out((...  93.7 us
    pallas_call x1, Pallas kernels, widen(): pl.pallas_call(functools.partial(widen_kernel, plan), out_shape=tuple((ja...  12.8 us

profile of v7, /device:TPU:0, one launch (start us, length us, event | category | flops | bytes accessed | tf_op | source)
XLA Modules:
  0.0 384.1 jit_solution(15431132260712976904)
XLA Ops:
  0.6 0.7 convert_element_type.5
  1.3 0.3 multiply_cosine_fusion
  1.6 0.7 select_maximum_fusion.table_ref
  2.4 93.7 %forward.1 = (s32[64,128]{1,0:T(8,128)}, bf16[512,1536]{1,0:T(8,128)(2,1)}, f32[128,1536]{1,0:T(8,128)}, bf16[16,32,384]{2,1,0:T(8,128)(2,1)}, bf16[16,64,384]{2...) custom-call(s32[1,128]{1,0:T(1,128)} %bitcast.6, ...), custom_call_target="tpu_custom_call" | custom-call | tf_op jit(solution)/shard_map/forward/pallas_call | solution.py:1391
  96.0 0.8 slice.9
  96.9 0.1 reshape_squeeze.3
  97.0 0.1 select_reduce_fusion
  97.1 0.6 pad_add_fusion.order_ref
  97.7 270.3 %backward.1 = (bf16[4224,1536]{1,0:T(8,128)(2,1)}, f32[2,1536]{1,0:T(2,128)}, f32[128,1536]{1,0:T(8,128)}, bf16[128,1536]{1,0:T(8,128)(2,1)}) custom-call(s32[32]{0:T(128)} %pad_add_fusion.order_ref, bf16[1536]{0:T(1024)(128)(2,1)} %gain_one_ref.3, bf16[1536]{0:T(1024)(128)(2,1)} %gain_two_ref.3, bf16[512,1024]{1,0:T(8,128)(2,1)} %get-tuple-element.36.grad_gate_ref, ...), custom_call_target="tpu_custom_call" | custom-call | tf_op jit(solution)/shard_map/backward/pallas_call | solution.py:1035
  368.0 0.0 copy-start.1
  368.0 0.0 copy-start
  368.0 12.8 %widen.1 = (f32[1024,1536]{1,0:T(8,128)}, f32[1024,1536]{1,0:T(8,128)}, f32[1024,1536]{1,0:T(8,128)}, f32[384,1536]{1,0:T(8,128)}, f32[192,1536]{1,0:T(8,128)}, ...) custom-call(bf16[4224,1536]{1,0:T(8,128)(2,1)} %get-tuple-element.51.source), custom_call_target="tpu_custom_call" | custom-call | tf_op jit(solution)/shard_map/widen/pallas_call | solution.py:1486
  380.8 0.0 copy-done.1
  380.8 0.6 slice_reduce_fusion
  381.4 1.8 copy.31
  383.2 0.0 copy-done
  383.2 0.9 copy.32
  (2 shorter events, 0.0 us)
Async XLA Ops:
  368.0 12.8 %copy-start.1 = (f32[2,1536]{1,0:T(2,128)S(1)}, f32[2,1536]{1,0:T(2,128)}, u32[]{:S(2)}) copy-start(f32[2,1536]{1,0:T(2,128)} %get-tuple-element.50) | copy-start | bytes 36868
  368.0 15.2 %copy-start = (f32[128,1536]{1,0:T(8,128)S(1)}, f32[128,1536]{1,0:T(8,128)}, u32[]{:S(2)}) copy-start(f32[128,1536]{1,0:T(8,128)} %get-tuple-element.75) | copy-start | bytes 2359300

commit v8 on v7

--- a/solution.py
+++ b/solution.py
@@ -199,8 +199,8 @@
 ROUND_ROWS = 2 * SPINE_ROWS + LINE_ROWS
 LEAD = 4
 HOP = 2
-FEED = (1, 3, 5, 8)
-CHAIN = (0, 4, 6, 8, 10, 12, 19, 22, 26, 28)
+FEED = (0, 1, 3, 5, 8)
+CHAIN = (0, 4, 6, 8, 10, 13, 24, 26, 30, 32)
 RING = 20
 TILE = 128
 PAIR = (HEADS // KV_HEADS) * HEAD_DIM
@@ -390,7 +390,7 @@
 
 
 class Tree:
-    def __init__(self, place, own, out_ref, index, line, box, sems, leaf_back):
+    def __init__(self, place, own, out_ref, index, rounds, line, box, sems, leaf_back):
         me = place.ctx
         depth, side = lax.div(me, 2), lax.rem(me, 2)
         other_side = me + 1 - 2 * side
@@ -398,7 +398,7 @@
         self.up, self.got, self.down, self.back = sems
         self.leaf_back = leaf_back
         if line:
-            center = lax.rem(index, 4)
+            center = jnp.where(index >= rounds - 6, 1 + lax.rem(index, 2), lax.rem(index, 4))
             count = LINE_ROWS
             start = index * ROUND_ROWS + 2 * SPINE_ROWS
             root_side = lax.rem(index, 2)
@@ -734,16 +734,15 @@
             own[rows, :] = product_rows(left[:, columns], right[...]).astype(jnp.bfloat16)
 
     stage_feed(0)
-    stage_feed(2 * 256)
 
     spine_sems = (spine_up, spine_got, spine_down, spine_back)
     line_sems = (line_up, line_got, line_down, line_back)
 
     def spine(index):
-        return Tree(place, own, out_ref, index, False, spine_in, spine_sems, leaf_back)
+        return Tree(place, own, out_ref, index, rounds, False, spine_in, spine_sems, leaf_back)
 
     def line(index):
-        return Tree(place, own, out_ref, index, True, line_in, line_sems, None)
+        return Tree(place, own, out_ref, index, rounds, True, line_in, line_sems, None)
 
     def leaf_rows(index):
         return rows_at(index * ROUND_ROWS + (1 - side) * SPINE_ROWS, SPINE_ROWS)
@@ -933,7 +932,7 @@
 
     units = 2 * 256
     stages = [
-        (FEED[index], functools.partial(stage_feed, (index + 2) * units)) for index in range(4)
+        (FEED[index], functools.partial(stage_feed, (index + 1) * units)) for index in range(5)
     ]
     stages += [
         (CHAIN[0], fold_two.relay),
@@ -962,8 +961,8 @@
         (CHAIN[9], stage_gain),
     ]
     assert CHAIN[7] + 1 < base // ROUND_ROWS - LEAD
-    for index in range(4):
-        assert FEED[index] < (index + 2) * units // ROUND_ROWS - LEAD
+    for index in range(5):
+        assert FEED[index] < (index + 1) * units // ROUND_ROWS - LEAD
 
     for index in range(LEAD):
         leaf_copy(index).start()
@@ -979,10 +978,6 @@
         for tree in (spine(done), line(done)):
             pl.when(valid(done))(tree.finish)
 
-        @pl.when(now + LEAD < rounds)
-        def _():
-            leaf_copy(now + LEAD).start()
-
         rising = spine(now - HOP * (3 - off_center))
         pl.when(valid(rising.index))(rising.rise)
 
@@ -990,6 +985,10 @@
         def _(age):
             tree = line(now - HOP * age)
             pl.when(jnp.logical_and(valid(tree.index), tree.rise_age == age))(tree.rise)
+
+        @pl.when(now + LEAD < rounds)
+        def _():
+            leaf_copy(now + LEAD).start()
 
         falling = spine(now - HOP * (3 + off_center))
         pl.when(valid(falling.index))(falling.fall)
@@ -1306,8 +1305,7 @@
     swap_heads.arrive()
     store(heads, attended_out)
 
-    @pl.loop(0, 4)
-    def _(sequence):
+    def project_out(sequence):
         total = None
         for head in range(2):
             rows = heads[pl.ds((2 * sequence + head) * halves, halves)]
@@ -1316,7 +1314,10 @@
             total = term if total is None else total + term
         part[rows_at(sequence * TILE, TILE), :] = total.astype(jnp.bfloat16)
 
-    fold.start()
+    for chip in (1 - place.chip, place.chip):
+        project_out(2 * chip + 1 - place.core)
+        fold.partner_copy(chip).start()
+        project_out(2 * chip + place.core)
     gather_cotangents.arrive()
     store(cotangents, cotangent_out)
     fold.relay()
@@ -1360,16 +1361,22 @@
                 + product(grad_up[span, :], up_weight[:, columns])
             ).astype(jnp.bfloat16)
 
+    def store_feed(chip):
+        span = rows_at(chip * pair_rows, pair_rows)
+        for source, target in (
+            (part, part_out), (mixed, mixed_out), (grad_gate, grad_gate_out),
+            (grad_up, grad_up_out),
+        ):
+            store(source.at[span], target.at[span])
+
     gather_two.first()
     feed(place.chip)
+    store_feed(place.chip)
     gather_two.relay()
     gather_two.arrive()
     store(normed_two, normed_two_out)
     feed(1 - place.chip)
-    store(part, part_out)
-    store(mixed, mixed_out)
-    store(grad_gate, grad_gate_out)
-    store(grad_up, grad_up_out)
+    store_feed(1 - place.chip)
     for copy in stores:
         copy.wait()
 
@@ -1424,7 +1431,7 @@
             pltpu.VMEM((TILE, width), full),
             pltpu.VMEM((rows, hidden_units), low), pltpu.VMEM((rows, hidden_units), low),
             pltpu.VMEM((rows, hidden_units), low),
-            dma((30,)), dma((12,)),
+            dma((30,)), dma((16,)),
             dma((5, 3)), dma((5, 3)),
             dma((3, 8)), dma((3, 8)),
             dma((3,)), dma((3,)),
@@ -1437,8 +1444,19 @@
       output_weight, gate_weight, up_weight, down_weight)
 
 
-def widen_kernel(plan, source, *refs):
+def widen_kernel(plan, kept, source, *refs):
+    sources, refs = refs[:kept], refs[kept:]
+    holds, refs, hold_sem = refs[-1 - kept : -1], refs[: -1 - kept], refs[-1]
     targets, (low, full, load_sem, store_sem) = refs[:-4], refs[-4:]
+    targets, copies = targets[: len(targets) - kept], targets[len(targets) - kept :]
+    takes = [
+        pltpu.make_async_copy(sources[index], holds[index], hold_sem.at[index])
+        for index in range(kept)
+    ]
+    gives = [
+        pltpu.make_async_copy(holds[index], copies[index], hold_sem.at[kept + index])
+        for index in range(kept)
+    ]
     slots = low.shape[0]
     loads, stores = [], []
     for index, (first, which, target_row, chunk) in enumerate(plan):
@@ -1456,7 +1474,7 @@
                 store_sem.at[slot],
             )
         )
-    for load in loads[:slots]:
+    for load in loads[:slots] + takes:
         load.start()
     for index, (load, store) in enumerate(zip(loads, stores)):
         slot = index % slots
@@ -1472,11 +1490,15 @@
         store.start()
         if index + slots < len(plan):
             loads[index + slots].start()
-    for store in stores[-slots:]:
+        if index == slots:
+            for take, give in zip(takes, gives):
+                take.wait()
+                give.start()
+    for store in stores[-slots:] + gives:
         store.wait()
 
 
-def widen(values, counts):
+def widen(values, counts, keep):
     slots, width, first, plan = 6, values.shape[1], 0, []
     for which, count in enumerate(counts):
         chunk = math.gcd(count, 256) if count % 192 else 192
@@ -1484,19 +1506,22 @@
         first += count
     any_spec = pl.BlockSpec(memory_space=pl.ANY)
     return pl.pallas_call(
-        functools.partial(widen_kernel, plan),
-        out_shape=tuple(jax.ShapeDtypeStruct((count, width), jnp.float32) for count in counts),
-        in_specs=[any_spec],
-        out_specs=(any_spec,) * len(counts),
+        functools.partial(widen_kernel, plan, len(keep)),
+        out_shape=tuple(jax.ShapeDtypeStruct((count, width), jnp.float32) for count in counts)
+        + tuple(jax.ShapeDtypeStruct(array.shape, array.dtype) for array in keep),
+        in_specs=[any_spec] * (1 + len(keep)),
+        out_specs=(any_spec,) * (len(counts) + len(keep)),
         scratch_shapes=[
             pltpu.VMEM((slots, 256, width), values.dtype),
             pltpu.VMEM((slots, 256, width), jnp.float32),
             pltpu.SemaphoreType.DMA((slots,)),
             pltpu.SemaphoreType.DMA((slots,)),
-        ],
+        ]
+        + [pltpu.VMEM(array.shape, array.dtype) for array in keep]
+        + [pltpu.SemaphoreType.DMA((2 * len(keep),))],
         compiler_params=pltpu.CompilerParams(vmem_limit_bytes=63 * 2**20),
         name="widen",
-    )(values)
+    )(values, *keep)
 
 
 def gather_rows(values):
@@ -1693,7 +1718,9 @@
     )
     owners = (gate_weight, up_weight, down_weight, query_weight, key_weight, value_weight,
               output_weight)
-    parts = widen(summed, [owner.shape[0] for owner in owners])
+    *parts, layer_output, input_grad = widen(
+        summed, [owner.shape[0] for owner in owners], (layer_output, input_grad)
+    )
     return (layer_output, input_grad, gain_sums[0], *parts[3:], gain_sums[1], *parts[:3])
 
 

time: 384 us -> 378 us (0.984)
  Pallas kernels: 377 us -> 373 us
    pallas_call x1, Pallas kernels: 270 us -> 266 us  [backward(): pl.pallas_call(functools.partial(backward_kernel, rounds, block), out_sha...]
where the time goes in v8:
time: 378 us; the launch traced here: 377 us
  Pallas kernels  373 us (99%)
    pallas_call x1, Pallas kernels, backward(): pl.pallas_call(functools.partial(backward_kernel, rounds, block), out_sha...  266 us
    pallas_call x1, Pallas kernels, forward(): pl.pallas_call(functools.partial(forward_kernel, block), out_shape=(out((...  93.4 us
    pallas_call x1, Pallas kernels, widen(): pl.pallas_call(functools.partial(widen_kernel, plan, len(keep)), out_shap...  13.3 us

profile of v8, /device:TPU:0, one launch (start us, length us, event | category | flops | bytes accessed | tf_op | source)
XLA Modules:
  0.0 377.3 jit_solution(1576709443024696512)
XLA Ops:
  0.6 0.7 convert_element_type.5
  1.3 0.3 multiply_cosine_fusion
  1.6 0.7 select_maximum_fusion.table_ref
  2.4 93.4 %forward.1 = (s32[64,128]{1,0:T(8,128)}, bf16[512,1536]{1,0:T(8,128)(2,1)}, f32[128,1536]{1,0:T(8,128)}, bf16[16,32,384]{2,1,0:T(8,128)(2,1)}, bf16[16,64,384]{2...) custom-call(s32[1,128]{1,0:T(1,128)} %bitcast.6, ...), custom_call_target="tpu_custom_call" | custom-call | tf_op jit(solution)/shard_map/forward/pallas_call | solution.py:1398
  95.7 0.8 slice.9
  96.6 0.1 reshape_squeeze.3
  96.7 0.1 select_reduce_fusion
  96.8 0.6 pad_add_fusion.order_ref
  97.4 266.0 %backward.1 = (bf16[4224,1536]{1,0:T(8,128)(2,1)}, f32[2,1536]{1,0:T(2,128)}, f32[128,1536]{1,0:T(8,128)}, bf16[128,1536]{1,0:T(8,128)(2,1)}) custom-call(s32[32]{0:T(128)} %pad_add_fusion.order_ref, bf16[1536]{0:T(1024)(128)(2,1)} %gain_one_ref.3, bf16[1536]{0:T(1024)(128)(2,1)} %gain_two_ref.3, bf16[512,1024]{1,0:T(8,128)(2,1)} %get-tuple-element.38.grad_gate_ref, ...), custom_call_target="tpu_custom_call" | custom-call | tf_op jit(solution)/shard_map/backward/pallas_call | solution.py:1034
  363.4 0.0 copy-start
  363.4 13.3 %widen.1 = (f32[1024,1536]{1,0:T(8,128)}, f32[1024,1536]{1,0:T(8,128)}, f32[1024,1536]{1,0:T(8,128)}, f32[384,1536]{1,0:T(8,128)}, f32[192,1536]{1,0:T(8,128)}, ...) custom-call(bf16[4224,1536]{1,0:T(8,128)(2,1)} %get-tuple-element.50.source, ...), custom_call_target="tpu_custom_call" | custom-call | tf_op jit(solution)/shard_map/widen/pallas_call | solution.py:1508
  376.7 0.0 copy-done
  376.7 0.6 slice_reduce_fusion
  (2 shorter events, 0.0 us)
Async XLA Ops:
  363.4 13.3 %copy-start = (f32[2,1536]{1,0:T(2,128)S(1)}, f32[2,1536]{1,0:T(2,128)}, u32[]{:S(2)}) copy-start(f32[2,1536]{1,0:T(2,128)} %get-tuple-element.55) | copy-start | bytes 36868

commit v9 on v8

--- a/solution.py
+++ b/solution.py
@@ -248,12 +248,13 @@
             **near_fsdp(self.place.partner),
         )
 
-    def across_copy(self):
+    def across_copy(self, piece):
+        span = pl.ds(piece * (TILE // 2), TILE // 2)
         return pltpu.make_async_remote_copy(
-            src_ref=self.send,
-            dst_ref=self.far,
-            send_sem=self.send_sem.at[2],
-            recv_sem=self.recv_sem.at[2],
+            src_ref=self.send.at[span],
+            dst_ref=self.far.at[span],
+            send_sem=self.send_sem.at[2 + piece],
+            recv_sem=self.recv_sem.at[2 + piece],
             **near_fsdp(self.place.across),
         )
 
@@ -265,24 +266,30 @@
         there = 1 - self.place.chip
         self.partner_copy(there).wait_recv()
         base = self.place.across * TILE
-
-        @pl.loop(0, TILE // 32)
-        def _(piece):
-            mine = self.part[rows_at(base + piece * 32, 32), :].astype(jnp.float32)
-            span = rows_at(piece * 32, 32)
-            self.send[span, :] = (
-                mine + self.near[there, span, :].astype(jnp.float32)
-            ).astype(jnp.bfloat16)
-
-        self.across_copy().start()
-
-    def arrive(self):
+        for half in range(2):
+
+            @pl.loop(2 * half, 2 * half + 2)
+            def _(piece):
+                mine = self.part[rows_at(base + piece * 32, 32), :].astype(jnp.float32)
+                span = rows_at(piece * 32, 32)
+                self.send[span, :] = (
+                    mine + self.near[there, span, :].astype(jnp.float32)
+                ).astype(jnp.bfloat16)
+
+            self.across_copy(half).start()
+
+    def arrive_near(self):
         self.partner_copy(self.place.chip).wait_recv()
-        copy = self.across_copy()
-        copy.wait_recv()
-        copy.wait_send()
         self.partner_copy(0).wait_send()
         self.partner_copy(1).wait_send()
+
+    def arrive_across(self, piece):
+        self.across_copy(piece).wait()
+
+    def arrive(self):
+        self.arrive_near()
+        self.arrive_across(0)
+        self.arrive_across(1)
 
     def rows(self, start, count):
         mine = self.part[rows_at(self.place.row * TILE + start, count), :].astype(jnp.float32)
@@ -292,36 +299,40 @@
 
 
 class Gather:
-    def __init__(self, place, full, send_sem, recv_sem, count=TILE):
+    def __init__(self, place, full, send_sem, recv_sem, count=TILE, pieces=1):
         self.place, self.full, self.send_sem, self.recv_sem = place, full, send_sem, recv_sem
-        self.count = count
-
-    def copy(self, block, target, key):
-        span = pl.ds(pl.multiple_of(block * self.count, self.count), self.count)
+        self.count, self.pieces = count, pieces
+
+    def copy(self, block, target, key, piece):
+        rows = self.count // self.pieces
+        span = pl.ds(pl.multiple_of(block * self.count + piece * rows, rows), rows)
         return pltpu.make_async_remote_copy(
             src_ref=self.full.at[span],
             dst_ref=self.full.at[span],
-            send_sem=self.send_sem.at[key],
-            recv_sem=self.recv_sem.at[key],
+            send_sem=self.send_sem.at[key * self.pieces + piece],
+            recv_sem=self.recv_sem.at[key * self.pieces + piece],
             **near_fsdp(target),
         )
 
-    def start(self):
-        self.copy(self.place.row, self.place.across, 1).start()
-        self.copy(self.place.row, self.place.partner, 0).start()
+    def start(self, piece=0):
+        self.copy(self.place.row, self.place.across, 1, piece).start()
+        self.copy(self.place.row, self.place.partner, 0, piece).start()
+
+    def first(self):
+        for piece in range(self.pieces):
+            self.copy(self.place.partner, self.place.partner, 0, piece).wait_recv()
 
     def relay(self):
-        self.copy(self.place.across, self.place.across, 1).wait_recv()
-        self.copy(self.place.across, self.place.partner, 2).start()
-
-    def first(self):
-        self.copy(self.place.partner, self.place.partner, 0).wait_recv()
+        for piece in range(self.pieces):
+            self.copy(self.place.across, self.place.across, 1, piece).wait_recv()
+            self.copy(self.place.across, self.place.partner, 2, piece).start()
 
     def arrive(self):
-        self.copy(self.place.corner, self.place.partner, 2).wait_recv()
-        self.copy(self.place.row, self.place.across, 1).wait_send()
-        self.copy(self.place.row, self.place.partner, 0).wait_send()
-        self.copy(self.place.across, self.place.partner, 2).wait_send()
+        for piece in range(self.pieces):
+            self.copy(self.place.corner, self.place.partner, 2, piece).wait_recv()
+            self.copy(self.place.row, self.place.across, 1, piece).wait_send()
+            self.copy(self.place.row, self.place.partner, 0, piece).wait_send()
+            self.copy(self.place.across, self.place.partner, 2, piece).wait_send()
 
 
 class Swap:
@@ -1072,7 +1083,7 @@
             dma((RING,)), dma((3, RING)), dma((3, RING)), dma((RING,)),
             dma((RING,)), dma((RING,)),
             dma((RING,)), dma((3, RING)), dma((3, RING)), dma((RING,)),
-            dma((2, 3)), dma((2, 3)),
+            dma((2, 4)), dma((2, 4)),
             dma((3,)), dma((3,)),
             dma((2, 8)), dma((2, 8)),
             dma((4,)), dma((4,)), dma((8,)), dma((8,)),
@@ -1210,9 +1221,9 @@
     tables[own_rows, :] = table_ref[...]
     gather_places = Gather(place, places, gather_send.at[0], gather_recv.at[0], 8)
     gather_tables = Gather(place, tables, gather_send.at[1], gather_recv.at[1])
-    gather_inputs = Gather(place, inputs, gather_send.at[2], gather_recv.at[2])
+    gather_inputs = Gather(place, inputs, gather_send.at[2], gather_recv.at[2], TILE, 2)
     gather_cotangents = Gather(place, cotangents, gather_send.at[3], gather_recv.at[3])
-    gather_two = Gather(place, normed_two, gather_send.at[4], gather_recv.at[4])
+    gather_two = Gather(place, normed_two, gather_send.at[4], gather_recv.at[4], TILE, 2)
     swap_places = Swap(place, places, place_out, swap_send.at[0], swap_recv.at[0], 8, 2)
     swap_packed = Swap(place, packed_from, packed, swap_send.at[1], swap_recv.at[1], halves)
     swap_heads = Swap(place, heads_from, heads, swap_send.at[2], swap_recv.at[2], halves)
@@ -1221,6 +1232,7 @@
     fetch("inputs")
     gather_tables.start()
     gather_inputs.start()
+    gather_inputs.start(1)
     gather_places.start()
     fetch("cotangent")
     gather_cotangents.start()
@@ -1321,17 +1333,19 @@
     gather_cotangents.arrive()
     store(cotangents, cotangent_out)
     fold.relay()
-    fold.arrive()
-
-    @pl.loop(0, TILE // 16)
-    def _(piece):
-        span = rows_at(piece * 16, 16)
-        own = rows_at(place.row * TILE + piece * 16, 16)
-        rows = inputs[own, :].astype(jnp.float32) + fold.rows(piece * 16, 16)
-        hidden[span, :] = rows
-        normed_two[own, :] = (rows * rms_scale(rows) * gain_two).astype(jnp.bfloat16)
-
-    gather_two.start()
+    fold.arrive_near()
+    for half_rows in range(2):
+        fold.arrive_across(half_rows)
+
+        @pl.loop(4 * half_rows, 4 * half_rows + 4)
+        def _(piece):
+            span = rows_at(piece * 16, 16)
+            own = rows_at(place.row * TILE + piece * 16, 16)
+            rows = inputs[own, :].astype(jnp.float32) + fold.rows(piece * 16, 16)
+            hidden[span, :] = rows
+            normed_two[own, :] = (rows * rms_scale(rows) * gain_two).astype(jnp.bfloat16)
+
+        gather_two.start(half_rows)
     store(hidden, hidden_out)
     fetch("gate", "up", "down")
 
@@ -1432,9 +1446,9 @@
             pltpu.VMEM((rows, hidden_units), low), pltpu.VMEM((rows, hidden_units), low),
             pltpu.VMEM((rows, hidden_units), low),
             dma((30,)), dma((16,)),
-            dma((5, 3)), dma((5, 3)),
+            dma((5, 6)), dma((5, 6)),
             dma((3, 8)), dma((3, 8)),
-            dma((3,)), dma((3,)),
+            dma((4,)), dma((4,)),
         ],
         compiler_params=pltpu.CompilerParams(
             collective_id=key, has_side_effects=True, vmem_limit_bytes=63 * 2**20

time: 378 us -> 376 us (level)
  no operation moved by 1% of the time
where the time goes in v9:
time: 376 us; the launch traced here: 375 us
  Pallas kernels  371 us (99%)
    pallas_call x1, Pallas kernels, backward(): pl.pallas_call(functools.partial(backward_kernel, rounds, block), out_sha...  267 us
    pallas_call x1, Pallas kernels, forward(): pl.pallas_call(functools.partial(forward_kernel, block), out_shape=(out((...  90.3 us
    pallas_call x1, Pallas kernels, widen(): pl.pallas_call(functools.partial(widen_kernel, plan, len(keep)), out_shap...  13.3 us

profile of v9, /device:TPU:0, one launch (start us, length us, event | category | flops | bytes accessed | tf_op | source)
XLA Modules:
  0.0 375.5 jit_solution(12161262516465055472)
XLA Ops:
  0.6 0.7 convert_element_type.5
  1.3 0.3 multiply_cosine_fusion
  1.6 0.7 select_maximum_fusion.table_ref
  2.4 90.3 %forward.1 = (s32[64,128]{1,0:T(8,128)}, bf16[512,1536]{1,0:T(8,128)(2,1)}, f32[128,1536]{1,0:T(8,128)}, bf16[16,32,384]{2,1,0:T(8,128)(2,1)}, bf16[16,64,384]{2...) custom-call(s32[1,128]{1,0:T(1,128)} %bitcast.6, ...), custom_call_target="tpu_custom_call" | custom-call | tf_op jit(solution)/shard_map/forward/pallas_call | solution.py:1412
  92.7 0.8 slice.9
  93.5 0.1 reshape_squeeze.3
  93.6 0.1 select_reduce_fusion
  93.7 0.6 pad_add_fusion.order_ref
  94.3 267.2 %backward.1 = (bf16[4224,1536]{1,0:T(8,128)(2,1)}, f32[2,1536]{1,0:T(2,128)}, f32[128,1536]{1,0:T(8,128)}, bf16[128,1536]{1,0:T(8,128)(2,1)}) custom-call(s32[32]{0:T(128)} %pad_add_fusion.order_ref, bf16[1536]{0:T(1024)(128)(2,1)} %gain_one_ref.3, bf16[1536]{0:T(1024)(128)(2,1)} %gain_two_ref.3, bf16[512,1024]{1,0:T(8,128)(2,1)} %get-tuple-element.38.grad_gate_ref, ...), custom_call_target="tpu_custom_call" | custom-call | tf_op jit(solution)/shard_map/backward/pallas_call | solution.py:1045
  361.5 0.0 copy-start
  361.5 13.3 %widen.1 = (f32[1024,1536]{1,0:T(8,128)}, f32[1024,1536]{1,0:T(8,128)}, f32[1024,1536]{1,0:T(8,128)}, f32[384,1536]{1,0:T(8,128)}, f32[192,1536]{1,0:T(8,128)}, ...) custom-call(bf16[4224,1536]{1,0:T(8,128)(2,1)} %get-tuple-element.50.source, ...), custom_call_target="tpu_custom_call" | custom-call | tf_op jit(solution)/shard_map/widen/pallas_call | solution.py:1522
  374.8 0.0 copy-done
  374.8 0.6 slice_reduce_fusion
  (2 shorter events, 0.0 us)
Async XLA Ops:
  361.5 13.3 %copy-start = (f32[2,1536]{1,0:T(2,128)S(1)}, f32[2,1536]{1,0:T(2,128)}, u32[]{:S(2)}) copy-start(f32[2,1536]{1,0:T(2,128)} %get-tuple-element.55) | copy-start | bytes 36868

commit v10 on v9

--- a/solution.py
+++ b/solution.py
@@ -1310,7 +1310,8 @@
         heads_from[first // block : (first + tile) // block] = pack_pairs(
             moved.reshape(-1, block, PAIR)
         )
-    swap_heads.start_all()
+        for index in range(first // TILE, (first + tile) // TILE):
+            swap_heads.start(index)
     gather_cotangents.first()
     gather_cotangents.relay()
     fetch("output")

time: 376 us -> 376 us (level)
  no operation moved by 1% of the time
where the time goes in v10:
time: 376 us
  Pallas kernels  371 us (99%)
    pallas_call x1, Pallas kernels, backward(): pl.pallas_call(functools.partial(backward_kernel, rounds, block), out_sha...  268 us
    pallas_call x1, Pallas kernels, forward(): pl.pallas_call(functools.partial(forward_kernel, block), out_shape=(out((...  90.5 us
    pallas_call x1, Pallas kernels, widen(): pl.pallas_call(functools.partial(widen_kernel, plan, len(keep)), out_shap...  13.3 us

profile of v10, /device:TPU:0, one launch (start us, length us, event | category | flops | bytes accessed | tf_op | source)
XLA Modules:
  0.0 376.2 jit_solution(1116263514411522504)
XLA Ops:
  0.6 0.7 convert_element_type.5
  1.3 0.3 multiply_cosine_fusion
  1.6 0.7 select_maximum_fusion.table_ref
  2.4 90.5 %forward.1 = (s32[64,128]{1,0:T(8,128)}, bf16[512,1536]{1,0:T(8,128)(2,1)}, f32[128,1536]{1,0:T(8,128)}, bf16[16,32,384]{2,1,0:T(8,128)(2,1)}, bf16[16,64,384]{2...) custom-call(s32[1,128]{1,0:T(1,128)} %bitcast.6, ...), custom_call_target="tpu_custom_call" | custom-call | tf_op jit(solution)/shard_map/forward/pallas_call | solution.py:1413
  92.8 0.8 slice.9
  93.7 0.1 reshape_squeeze.3
  93.8 0.1 select_reduce_fusion
  93.9 0.6 pad_add_fusion.order_ref
  94.5 267.7 %backward.1 = (bf16[4224,1536]{1,0:T(8,128)(2,1)}, f32[2,1536]{1,0:T(2,128)}, f32[128,1536]{1,0:T(8,128)}, bf16[128,1536]{1,0:T(8,128)(2,1)}) custom-call(s32[32]{0:T(128)} %pad_add_fusion.order_ref, bf16[1536]{0:T(1024)(128)(2,1)} %gain_one_ref.3, bf16[1536]{0:T(1024)(128)(2,1)} %gain_two_ref.3, bf16[512,1024]{1,0:T(8,128)(2,1)} %get-tuple-element.38.grad_gate_ref, ...), custom_call_target="tpu_custom_call" | custom-call | tf_op jit(solution)/shard_map/backward/pallas_call | solution.py:1045
  362.2 0.0 copy-start
  362.2 13.3 %widen.1 = (f32[1024,1536]{1,0:T(8,128)}, f32[1024,1536]{1,0:T(8,128)}, f32[1024,1536]{1,0:T(8,128)}, f32[384,1536]{1,0:T(8,128)}, f32[192,1536]{1,0:T(8,128)}, ...) custom-call(bf16[4224,1536]{1,0:T(8,128)(2,1)} %get-tuple-element.50.source, ...), custom_call_target="tpu_custom_call" | custom-call | tf_op jit(solution)/shard_map/widen/pallas_call | solution.py:1523
  375.5 0.0 copy-done
  375.5 0.6 slice_reduce_fusion
  (2 shorter events, 0.0 us)
Async XLA Ops:
  362.2 13.3 %copy-start = (f32[2,1536]{1,0:T(2,128)S(1)}, f32[2,1536]{1,0:T(2,128)}, u32[]{:S(2)}) copy-start(f32[2,1536]{1,0:T(2,128)} %get-tuple-element.55) | copy-start | bytes 36868
